TPU v7x, 32 devices: a whole 2x2x4 slice. The times are simulated.
32 devices in a mesh: wide: 8 (over z, x), narrow: 4 (over y, core).
Axes of the slice: x: 2, y: 2, z: 4, core: 2. Of those that a mesh axis runs over, the one named last changes fastest.
Arguments:
- tokens_in: bfloat16 [2048, 2048], P('wide'), may hold values from -7 to 7
- seg_ids: int32 [2048], P('wide'), may hold values from 0 to 7, as said below
- routes: int32 [2048, 6], P('wide'), may hold values from 0 to 15, all different within a row; in each aligned block of 256 rows (0 to 255, 256 to 511, ...) at most 144 rows name the same one
- gate_vals: float32 [2048, 6], P('wide'), may hold values from 0.1 to 0.6
- attn_gain: float32 [2048], replicated, may hold values from 0.5 to 1.5
- w_query: bfloat16 [2048, 3072], P('wide', 'narrow')
- w_latent: bfloat16 [2048, 576], P('wide')
- latent_gain: float32 [512], replicated, may hold values from 0.5 to 1.5
- w_expand: bfloat16 [512, 4096], P('wide', 'narrow'), may hold values from -0.25 to 0.25
- w_output: bfloat16 [2048, 2048], P('narrow', 'wide'), may hold values from -0.375 to 0.375
- ffn_gain: float32 [2048], replicated, may hold values from 0.5 to 1.5
- w_shared_in: bfloat16 [2048, 2, 2816], P('wide', None, 'narrow'), may hold values from -0.125 to 0.125
- w_shared_out: bfloat16 [2816, 2048], P('narrow', 'wide'), may hold values from -0.21875 to 0.21875
- w_expert_in: bfloat16 [16, 2048, 2, 1408], P('wide', None, None, 'narrow'), may hold values from -0.125 to 0.125
- w_expert_out: bfloat16 [16, 1408, 2048], P('wide', 'narrow'), may hold values from -0.3125 to 0.3125
- grad_output: bfloat16 [2048, 2048], P('wide'), may hold values from -6 to 6
Outputs:
- layer_out: bfloat16 [2048, 2048], P('wide', 'narrow')
- grad_tokens: float32 [2048, 2048], P('wide')
- grad_attn_gain: float32 [2048], P('wide')
- grad_w_query: float32 [2048, 3072], P('wide', 'narrow')
- grad_w_latent: float32 [2048, 576], P('wide')
- grad_latent_gain: float32 [512], P('wide')
- grad_w_expand: float32 [512, 4096], P('wide', 'narrow')
- grad_w_output: float32 [2048, 2048], P('narrow', 'wide')
- grad_ffn_gain: float32 [2048], P('wide')
- grad_shared_in: float32 [2048, 2, 2816], P('wide', None, 'narrow')
- grad_shared_out: float32 [2816, 2048], P('narrow', 'wide')
- grad_expert_in: float32 [16, 2048, 2, 1408], P('wide', None, None, 'narrow')
- grad_expert_out: float32 [16, 1408, 2048], P('wide', 'narrow')
Inputs may be any that keep to these rules, and one draw needn't show every extreme that they name: `seg_ids`: ids never decrease within one device's block of tokens; equal ids there mark one sequence, which lies inside that block; a block holds one to eight sequences, and some block holds a single sequence filling it. `routes`: each row names 6 different experts; within the 256 rows of one device no expert is named more than 144 times, and in some device's rows one expert is named exactly 144 times.
All inputs are finite; a program needn't handle non-finite values.
Results may differ from a plain program's by a relative error of at most 0.015.
Values may be sent and summed in bfloat16 or wider, within the bound.
A program may use at most 320 MiB of HBM per device.

v0:
```python
import jax
import jax.numpy as jnp
from jax import lax
from jax.sharding import PartitionSpec as P

DH = 128
DR = 64
KVR = 512
TOP = 6


EPS = 1e-06
THETA = 50000.0
NEG_BIG = -1e30
BLOCK_ROWS = 512


def positions(seg_ids):
    row_index = jnp.arange(seg_ids.shape[0], dtype=jnp.int32)
    starts = jnp.concatenate([jnp.ones((1,), dtype=bool), seg_ids[1:] != seg_ids[:-1]])
    begins = lax.cummax(jnp.where(starts, row_index, 0), axis=0)
    return (row_index - begins).astype(jnp.float32)


def rotary_tables(pos_float):
    half_dim = DR // 2
    inv_freq = THETA ** (-(jnp.arange(half_dim, dtype=jnp.float32) * 2.0 / DR))
    angles = pos_float[:, None] * inv_freq[None, :]
    return (jnp.cos(angles), jnp.sin(angles))


def rotate(values, cos_tab, sin_tab):
    half_dim = values.shape[-1] // 2
    lower_half = values[..., :half_dim]
    upper_half = values[..., half_dim:]
    return jnp.concatenate(
        [lower_half * cos_tab - upper_half * sin_tab, upper_half * cos_tab + lower_half * sin_tab],
        -1,
    )


def unrotate(values, cos_tab, sin_tab):
    half_dim = values.shape[-1] // 2
    lower_half = values[..., :half_dim]
    upper_half = values[..., half_dim:]
    return jnp.concatenate(
        [lower_half * cos_tab + upper_half * sin_tab, upper_half * cos_tab - lower_half * sin_tab],
        -1,
    )


def rms_forward(values, gain_vec):
    inv_rms = lax.rsqrt(jnp.mean(values * values, axis=-1, keepdims=True) + EPS)
    return (values * inv_rms * gain_vec, inv_rms)


def rms_backward(values, inv_rms, gain_vec, grad_out):
    scaled = grad_out * gain_vec
    grad_in = inv_rms * scaled - values * inv_rms**3 * jnp.mean(
        values * scaled, axis=-1, keepdims=True
    )
    grad_gain = jnp.sum(grad_out * values * inv_rms, axis=0)
    return (grad_in, grad_gain)


def swiglu(gate_up):
    gate_part = gate_up[..., 0, :]
    up_part = gate_up[..., 1, :]
    return gate_part * jax.nn.sigmoid(gate_part) * up_part


def swiglu_grad(gate_up, grad_act):
    gate_part = gate_up[..., 0, :]
    up_part = gate_up[..., 1, :]
    sigmoid_val = jax.nn.sigmoid(gate_part)
    grad_gate = grad_act * up_part * sigmoid_val * (1.0 + gate_part * (1.0 - sigmoid_val))
    grad_up = grad_act * gate_part * sigmoid_val
    return jnp.stack([grad_gate, grad_up], axis=-2)


def masked_scores(q_blk, k_heads, seg_rows, seg_cols, row_pos, col_pos):
    scale = (DH + DR) ** (-0.5)
    scores = jnp.einsum("hqc,hkc->hqk", q_blk, k_heads, preferred_element_type=jnp.float32) * scale
    allowed = (seg_rows[:, None] == seg_cols[None, :]) & (col_pos[None, :] <= row_pos[:, None])
    return jnp.where(allowed[None], scores, NEG_BIG)


def attention_forward(q_heads, k_heads, v_heads, seg_ids):
    head_count = q_heads.shape[0]
    row_total = q_heads.shape[1]
    block_rows = min(row_total, BLOCK_ROWS)
    block_count = row_total // block_rows
    col_pos = jnp.arange(row_total, dtype=jnp.int32)

    def one_block(start):
        row_pos = start + jnp.arange(block_rows, dtype=jnp.int32)
        scores = masked_scores(q_heads, k_heads, seg_ids, seg_ids, row_pos, col_pos)
        top_score = jnp.max(scores, axis=-1, keepdims=True)
        log_total = top_score + jnp.log(
            jnp.sum(jnp.exp(scores - top_score), axis=-1, keepdims=True)
        )
        prob_low = jnp.exp(scores - log_total).astype(jnp.bfloat16)
        attended = jnp.einsum("hqk,hkd->hqd", prob_low, v_heads, preferred_element_type=jnp.float32)
        return (attended.astype(jnp.bfloat16), log_total)

    starts = jnp.arange(block_count, dtype=jnp.int32) * block_rows
    attended, log_total = lax.map(one_block, starts)
    attended = attended.transpose(1, 0, 2, 3).reshape(head_count, row_total, -1)
    log_total = log_total.transpose(1, 0, 2, 3).reshape(head_count, row_total, 1)
    return (attended, log_total)


def attention_backward(q_heads, k_heads, v_heads, grad_att, log_total, seg_ids):
    scale = (DH + DR) ** (-0.5)
    head_count = q_heads.shape[0]
    row_total = q_heads.shape[1]
    block_rows = min(row_total, BLOCK_ROWS)
    block_count = row_total // block_rows
    col_pos = jnp.arange(row_total, dtype=jnp.int32)

    def one_block(carry, start):
        grad_k_acc, grad_v_acc = carry
        row_pos = start + jnp.arange(block_rows, dtype=jnp.int32)
        scores = masked_scores(q_heads, k_heads, seg_ids, seg_ids, row_pos, col_pos)
        prob_full = jnp.exp(scores - log_total)
        prob_low = prob_full.astype(jnp.bfloat16)
        grad_v_blk = jnp.einsum(
            "hqk,hqd->hkd", prob_low, grad_att, preferred_element_type=jnp.float32
        )
        grad_prob = jnp.einsum(
            "hqd,hkd->hqk", grad_att, v_heads, preferred_element_type=jnp.float32
        )
        row_dot = jnp.sum(prob_full * grad_prob, axis=-1, keepdims=True)
        grad_scores = (prob_full * (grad_prob - row_dot) * scale).astype(jnp.bfloat16)
        grad_q_blk = jnp.einsum(
            "hqk,hkc->hqc", grad_scores, k_heads, preferred_element_type=jnp.float32
        )
        grad_k_blk = jnp.einsum(
            "hqk,hqc->hkc", grad_scores, q_heads, preferred_element_type=jnp.float32
        )
        return ((grad_k_acc + grad_k_blk, grad_v_acc + grad_v_blk), grad_q_blk)

    starts = jnp.arange(block_count, dtype=jnp.int32) * block_rows
    init_acc = (jnp.zeros(k_heads.shape, jnp.float32), jnp.zeros(v_heads.shape, jnp.float32))
    (grad_k, grad_v), grad_q_blocks = lax.scan(one_block, init_acc, starts)
    grad_q = grad_q_blocks.transpose(1, 0, 2, 3).reshape(head_count, row_total, -1)
    return (grad_q, grad_k, grad_v)


def slot_layout(route_blk, gate_blk, num_experts, capacity):
    tok_count = route_blk.shape[0]
    top_count = route_blk.shape[1]
    flat_routes = route_blk.reshape(-1)
    onehot = (flat_routes[:, None] == jnp.arange(num_experts, dtype=jnp.int32)[None, :]).astype(
        jnp.int32
    )
    earlier = jnp.cumsum(onehot, axis=0) - onehot
    slot_rank = jnp.sum(earlier * onehot, axis=1)
    slot_ids = flat_routes * capacity + slot_rank
    token_ids = jnp.arange(tok_count * top_count, dtype=jnp.int32) // top_count
    slot_tokens = (
        jnp.full((num_experts * capacity,), tok_count, jnp.int32).at[slot_ids].set(token_ids)
    )
    slot_gates = (
        jnp.zeros((num_experts * capacity,), jnp.float32).at[slot_ids].set(gate_blk.reshape(-1))
    )
    return (slot_ids, slot_tokens, slot_gates)


def narrow_terms(terms):
    return lax.psum_scatter(terms, "narrow", scatter_dimension=3, tiled=True)


def per_device(
    tokens_in,
    seg_ids,
    routes,
    gate_vals,
    attn_gain,
    w_query,
    w_latent,
    latent_gain,
    w_expand,
    w_output,
    ffn_gain,
    w_shared_in,
    w_shared_out,
    w_expert_in,
    w_expert_out,
    grad_output,
):
    wide_count = lax.axis_size("wide")
    narrow_count = lax.axis_size("narrow")
    tok_rows = tokens_in.shape[0]
    width = tokens_in.shape[1]
    local_experts = w_expert_in.shape[0]
    num_experts = local_experts * wide_count
    capacity = 3 * tok_rows * TOP // (2 * num_experts)
    head_local = w_query.shape[1] // (DH + DR)
    shard_width = width // narrow_count
    wq_all, wkva_all, wkvb_all, wo_all, shin_all, shout_all = (
        lax.all_gather(w_query, "wide", axis=0, tiled=True),
        lax.all_gather(w_latent, "wide", axis=0, tiled=True),
        lax.all_gather(w_expand, "wide", axis=0, tiled=True),
        lax.all_gather(w_output, "wide", axis=1, tiled=True),
        lax.all_gather(w_shared_in, "wide", axis=0, tiled=True),
        lax.all_gather(w_shared_out, "wide", axis=1, tiled=True),
    )
    x_float = tokens_in.astype(jnp.float32)
    x_normed, inv_one = rms_forward(x_float, attn_gain)
    x_low = x_normed.astype(jnp.bfloat16)
    cos_tab, sin_tab = rotary_tables(positions(seg_ids))
    queries = (
        jnp.dot(x_low, wq_all, preferred_element_type=jnp.float32)
        .reshape(tok_rows, head_local, DH + DR)
        .transpose(1, 0, 2)
    )
    q_heads = jnp.concatenate(
        [queries[..., :DH], rotate(queries[..., DH:], cos_tab, sin_tab)], -1
    ).astype(jnp.bfloat16)
    latent_all = jnp.dot(x_low, wkva_all, preferred_element_type=jnp.float32)
    latent = latent_all[:, :KVR]
    latent_normed, inv_lat = rms_forward(latent, latent_gain)
    latent_low = latent_normed.astype(jnp.bfloat16)
    key_rope = rotate(latent_all[:, KVR:], cos_tab, sin_tab).astype(jnp.bfloat16)
    expanded = (
        jnp.dot(latent_low, wkvb_all, preferred_element_type=jnp.float32)
        .reshape(tok_rows, head_local, 2 * DH)
        .transpose(1, 0, 2)
    )
    key_nope = expanded[..., :DH].astype(jnp.bfloat16)
    v_heads = expanded[..., DH:].astype(jnp.bfloat16)
    k_heads = jnp.concatenate(
        [key_nope, jnp.broadcast_to(key_rope[None], (head_local, tok_rows, DR))], -1
    )
    attended, log_total = attention_forward(q_heads, k_heads, v_heads, seg_ids)
    merged = attended.transpose(1, 0, 2).reshape(tok_rows, head_local * DH)
    mixed_part = jnp.dot(merged, wo_all, preferred_element_type=jnp.float32)
    mixed_full = lax.psum(mixed_part, "narrow")
    resid_sum = x_float + mixed_full
    resid_normed, inv_two = rms_forward(resid_sum, ffn_gain)
    hidden_low = resid_normed.astype(jnp.bfloat16)
    shared_gu = jnp.einsum("td,dgf->tgf", hidden_low, shin_all, preferred_element_type=jnp.float32)
    shared_act = swiglu(shared_gu).astype(jnp.bfloat16)
    shared_part = jnp.dot(shared_act, shout_all, preferred_element_type=jnp.float32)
    slot_ids, slot_tokens, slot_gates = slot_layout(routes, gate_vals, num_experts, capacity)
    padded = jnp.concatenate([hidden_low, jnp.zeros((1, width), jnp.bfloat16)], 0)
    send_rows = padded[slot_tokens].reshape(wide_count, local_experts, capacity, width)
    received = lax.all_to_all(send_rows, "wide", split_axis=0, concat_axis=0, tiled=True)
    gate_up = jnp.einsum(
        "wecd,edgf->wecgf", received, w_expert_in, preferred_element_type=jnp.float32
    )
    activated = swiglu(gate_up).astype(jnp.bfloat16)
    partial_out = jnp.einsum(
        "wecf,efd->wecd", activated, w_expert_out, preferred_element_type=jnp.float32
    )
    partial_out = narrow_terms(partial_out)
    returned = lax.all_to_all(partial_out, "wide", split_axis=0, concat_axis=0, tiled=True)
    arrived = (returned, received, gate_up)
    returned, received_rows, expert_gu = arrived
    per_choice = returned.reshape(num_experts * capacity, -1)[slot_ids].reshape(tok_rows, TOP, -1)
    routed = jnp.sum(gate_vals[:, :, None] * per_choice, axis=1)
    summed = lax.psum_scatter(shared_part, "narrow", scatter_dimension=1, tiled=True)
    summed = summed + routed
    resid_shard = lax.dynamic_slice_in_dim(
        resid_sum, lax.axis_index("narrow") * shard_width, shard_width, 1
    )
    layer_out = (resid_shard + summed).astype(jnp.bfloat16)
    grad_out = grad_output.astype(jnp.float32)
    grad_shared_act = jnp.dot(grad_output, shout_all.T, preferred_element_type=jnp.float32)
    grad_shout = jnp.dot(shared_act.T, grad_output, preferred_element_type=jnp.float32)
    grad_shared_gu = swiglu_grad(shared_gu, grad_shared_act).astype(jnp.bfloat16)
    grad_shin = jnp.einsum(
        "td,tgf->dgf", hidden_low, grad_shared_gu, preferred_element_type=jnp.float32
    )
    grad_hidden_shared = jnp.einsum(
        "tgf,dgf->td", grad_shared_gu, shin_all, preferred_element_type=jnp.float32
    )
    grad_padded = jnp.concatenate([grad_out, jnp.zeros((1, width), jnp.float32)], 0)
    grad_send = (
        (slot_gates[:, None] * grad_padded[slot_tokens])
        .astype(jnp.bfloat16)
        .reshape(wide_count, local_experts, capacity, width)
    )
    grad_received = lax.all_to_all(grad_send, "wide", split_axis=0, concat_axis=0, tiled=True)
    activated = swiglu(expert_gu).astype(jnp.bfloat16)
    grad_act = jnp.einsum(
        "wecd,efd->wecf", grad_received, w_expert_out, preferred_element_type=jnp.float32
    )
    grad_exp_out = jnp.einsum(
        "wecf,wecd->efd", activated, grad_received, preferred_element_type=jnp.float32
    )
    grad_gu = swiglu_grad(expert_gu, grad_act).astype(jnp.bfloat16)
    grad_exp_in = jnp.einsum(
        "wecd,wecgf->edgf", received_rows, grad_gu, preferred_element_type=jnp.float32
    )
    grad_rows = jnp.einsum(
        "wecgf,edgf->wecd", grad_gu, w_expert_in, preferred_element_type=jnp.float32
    )
    grad_rows = narrow_terms(grad_rows)
    grad_back = lax.all_to_all(grad_rows, "wide", split_axis=0, concat_axis=0, tiled=True)
    grad_routed = jnp.sum(
        grad_back.reshape(num_experts * capacity, -1)[slot_ids].reshape(tok_rows, TOP, -1), axis=1
    )
    shared_shard = lax.psum_scatter(grad_hidden_shared, "narrow", scatter_dimension=1, tiled=True)
    grad_hidden = lax.all_gather(shared_shard + grad_routed, "narrow", axis=1, tiled=True)
    grad_resid, grad_ffn = rms_backward(resid_sum, inv_two, ffn_gain, grad_hidden)
    grad_resid = grad_resid + grad_out
    grad_low = grad_resid.astype(jnp.bfloat16)
    grad_merged = jnp.dot(grad_low, wo_all.T, preferred_element_type=jnp.float32)
    grad_wo = jnp.dot(merged.T, grad_low, preferred_element_type=jnp.float32)
    grad_att = grad_merged.reshape(tok_rows, head_local, DH).transpose(1, 0, 2).astype(jnp.bfloat16)
    grad_q, grad_k, grad_v = attention_backward(
        q_heads, k_heads, v_heads, grad_att, log_total, seg_ids
    )
    grad_q_pre = jnp.concatenate(
        [grad_q[..., :DH], unrotate(grad_q[..., DH:], cos_tab, sin_tab)], -1
    ).astype(jnp.bfloat16)
    grad_q_pre = grad_q_pre.transpose(1, 0, 2).reshape(tok_rows, head_local * (DH + DR))
    grad_rope_part = jnp.sum(grad_k[..., DH:], axis=0)
    grad_expanded = jnp.concatenate([grad_k[..., :DH], grad_v], -1).astype(jnp.bfloat16)
    grad_expanded = grad_expanded.transpose(1, 0, 2).reshape(tok_rows, head_local * 2 * DH)
    grad_wkvb = jnp.dot(latent_low.T, grad_expanded, preferred_element_type=jnp.float32)
    grad_latent_part = jnp.dot(grad_expanded, wkvb_all.T, preferred_element_type=jnp.float32)
    grad_x_part = jnp.dot(grad_q_pre, wq_all.T, preferred_element_type=jnp.float32)
    grad_wq = jnp.dot(x_low.T, grad_q_pre, preferred_element_type=jnp.float32)
    grad_latent_normed, grad_key_rope, grad_x_query = lax.psum(
        (grad_latent_part, grad_rope_part, grad_x_part), "narrow"
    )
    grad_latent, grad_lat_gain = rms_backward(latent, inv_lat, latent_gain, grad_latent_normed)
    grad_latent_all = jnp.concatenate(
        [grad_latent, unrotate(grad_key_rope, cos_tab, sin_tab)], -1
    ).astype(jnp.bfloat16)
    grad_wkva = jnp.dot(x_low.T, grad_latent_all, preferred_element_type=jnp.float32)
    grad_x_normed = grad_x_query + jnp.dot(
        grad_latent_all, wkva_all.T, preferred_element_type=jnp.float32
    )
    grad_x, grad_att_gain = rms_backward(x_float, inv_one, attn_gain, grad_x_normed)
    grad_tokens = grad_x + grad_resid
    reduced = (
        lax.psum_scatter(grad_wq, "wide", scatter_dimension=0, tiled=True),
        lax.psum_scatter(grad_wkva, "wide", scatter_dimension=0, tiled=True),
        lax.psum_scatter(grad_wkvb, "wide", scatter_dimension=0, tiled=True),
        lax.psum_scatter(grad_wo, "wide", scatter_dimension=1, tiled=True),
        lax.psum_scatter(grad_shin, "wide", scatter_dimension=0, tiled=True),
        lax.psum_scatter(grad_shout, "wide", scatter_dimension=1, tiled=True),
        lax.psum_scatter(grad_att_gain, "wide", scatter_dimension=0, tiled=True),
        lax.psum_scatter(grad_lat_gain, "wide", scatter_dimension=0, tiled=True),
        lax.psum_scatter(grad_ffn, "wide", scatter_dimension=0, tiled=True),
    )
    red_wq, red_wkva, red_wkvb, red_wo, red_shin, red_shout, red_att_gain, red_lat_gain, red_ffn = (
        reduced
    )
    return (
        layer_out,
        grad_tokens,
        red_att_gain,
        red_wq,
        red_wkva,
        red_lat_gain,
        red_wkvb,
        red_wo,
        red_ffn,
        red_shin,
        red_shout,
        grad_exp_in,
        grad_exp_out,
    )


def solution(mesh):
    placed = (
        P("wide", None),
        P("wide"),
        P("wide", None),
        P("wide", None),
        P(),
        P("wide", "narrow"),
        P("wide", None),
        P(),
        P("wide", "narrow"),
        P("narrow", "wide"),
        P(),
        P("wide", None, "narrow"),
        P("narrow", "wide"),
        P("wide", None, None, "narrow"),
        P("wide", "narrow", None),
        P("wide", None),
    )
    return jax.shard_map(
        per_device,
        mesh=mesh,
        in_specs=placed,
        out_specs=(
            P("wide", "narrow"),
            P("wide", None),
            P("wide"),
            P("wide", "narrow"),
            P("wide", None),
            P("wide"),
            P("wide", "narrow"),
            P("narrow", "wide"),
            P("wide"),
            P("wide", None, "narrow"),
            P("narrow", "wide"),
            P("wide", None, None, "narrow"),
            P("wide", "narrow", None),
        ),
        check_vma=False,
    )
```

profile of v0, /device:TPU:31, one launch (start us, length us, event | category | flops | bytes accessed | tf_op | source)
XLA Modules:
  0.0 2235.3 jit_solution(12019702773103367020)
XLA Ops:
  16.6 45.1 %all-gather.10.cloned.1.call-done = bf16[2048,576]{0,1:T(8,128)(2,1)} async-done(((bf16[256,576]{0,1:T(8,128)(2,1)}), bf16[2048,576]{0,1:T(8,128)(2,1)}) %all-gather.10.cloned.1.call-update) | async-done | bytes 2359312 | tf_op jit(solution)/shard_map/all_gather | solution.py:203
  65.4 35.7 %all-gather.12.cloned.1.call-done = bf16[512,1024]{1,0:T(8,128)(2,1)} async-done(((bf16[64,1024]{1,0:T(8,128)(2,1)}), bf16[512,1024]{1,0:T(8,128)(2,1)}) %all-gather.12.cloned.1.call-update) | async-done | bytes 1048592 | tf_op jit(solution)/shard_map/all_gather | solution.py:204
  108.9 54.7 %all-gather.8.cloned.1.call-done = bf16[2048,768]{1,0:T(8,128)(2,1)} async-done(((bf16[256,768]{1,0:T(8,128)(2,1)}), bf16[2048,768]{1,0:T(8,128)(2,1)}) %all-gather.8.cloned.1.call-update) | async-done | bytes 3145744 | tf_op jit(solution)/shard_map/all_gather | solution.py:202
  169.8 44.4 %all-gather.14.cloned.1.call-done = bf16[512,2048]{1,0:T(8,128)(2,1)} async-done(((bf16[512,256]{1,0:T(8,128)(2,1)}), bf16[512,2048]{1,0:T(8,128)(2,1)}) %all-gather.14.cloned.1.call-update) | async-done | bytes 2097168 | tf_op jit(solution)/shard_map/all_gather | solution.py:205
  224.2 6.2 scatter_custom_fusion
  230.4 39.1 %all-reduce.10.cloned.1.call-done = f32[256,2048]{1,0:T(8,128)} async-done(((f32[256,2048]{1,0:T(8,128)}), f32[256,2048]{1,0:T(8,128)}) %all-reduce.10.cloned.1.call-update) | async-done | bytes 2097168 | tf_op jit(solution)/shard_map/psum | solution.py:239
  275.5 19.7 gather_fusion
  295.2 14.5 all-to-all-start
  310.0 6.2 scatter_custom_fusion.1
  319.2 19.5 gather_fusion.2
  338.7 9.8 multiply_convert_fusion
  348.5 165.2 %all-to-all-done = bf16[8,2,144,2048]{3,2,1,0:T(8,128)(2,1)} async-done(((bf16[8,2,144,2048]{3,2,1,0:T(8,128)(2,1)}), bf16[8,2,144,2048]{3,2,1,0:T(8,128)(2,1)}, u32[]{:S(2)}, u32[]{:S(2)}) %all-to-all-start) | async-done | bytes 9437216 | tf_op jit(solution)/shard_map/all_to_all | solution.py:249
  513.7 5.7 all-to-all-start.2
  519.4 13.6 fusion.26
  533.0 190.2 %all-to-all-done.2 = bf16[8,2,144,2048]{3,2,1,0:T(8,128)(2,1)} async-done(((bf16[8,2,144,2048]{3,2,1,0:T(8,128)(2,1)}), bf16[8,2,144,2048]{3,2,1,0:T(8,128)(2,1)}, u32[]{:S(2)}, u32[]{:S(2)}) %all-to-all-start.2) | async-done | bytes 9437216 | tf_op jit(solution)/shard_map/all_to_all | solution.py:285
  723.1 10.9 fusion.41
  734.0 14.6 fusion.10
  748.7 12.9 copy.139
  763.1 136.2 %reduce-scatter.17.cloned.1.call-done = f32[8,2,144,512]{3,2,1,0:T(8,128)} async-done(((f32[8,2,144,2048]{3,2,1,0:T(8,128)}), f32[8,2,144,512]{3,2,1,0:T(8,128)}) %reduce-scatter.17.cloned.1.call-update) | async-done | bytes 4718608 | tf_op jit(solution)/shard_map/reduce_scatter | solution.py:171
  899.3 5.4 all-to-all-start.3
  904.9 170.4 %all-gather.16.cloned.1.call-done = bf16[2048,2,704]{0,2,1:T(8,128)(2,1)} async-done(((bf16[256,2,704]{0,2,1:T(8,128)(2,1)}), bf16[2048,2,704]{0,2,1:T(8,128)(2,1)}) %all-gather.16.cloned.1.call-update) | async-done | bytes 5767184 | tf_op jit(solution)/shard_map/all_gather | solution.py:206
  1075.3 5.8 fusion.49
  1081.1 53.9 %all-gather.18.cloned.1.call-done = bf16[704,2048]{1,0:T(8,128)(2,1)} async-done(((bf16[704,256]{1,0:T(8,128)(2,1)}), bf16[704,2048]{1,0:T(8,128)(2,1)}) %all-gather.18.cloned.1.call-update) | async-done | bytes 2883600 | tf_op jit(solution)/shard_map/all_gather | solution.py:207
  1134.9 4.6 fusion.68
  1143.6 8.0 gather_fusion.3
  1151.6 4.8 reshape.348
  1159.9 14.8 reduce-scatter.15.cloned.1.call-done
  1176.7 23.2 %all-gather.20.cloned.1.call-done = f32[256,2048]{1,0:T(8,128)} async-done(((f32[256,512]{1,0:T(8,128)}), f32[256,2048]{1,0:T(8,128)}) %all-gather.20.cloned.1.call-update) | async-done | bytes 2097168 | tf_op jit(solution)/shard_map/all_gather | solution.py:306
  1232.1 10.6 convolution_bitcast_fusion
  1247.9 4.6 fusion.133
  1253.5 7.2 fusion.47
  1269.2 23.2 %all-reduce.12.cloned.1.call-done = (f32[256,2048]{1,0:T(8,128)}, f32[256,64]{0,1:T(8,128)}, f32[256,512]{0,1:T(8,128)}) async-done(((f32[256,2048]{1,0:T(8,128)}, f32[256,64]{0,1:T(8,128)}, f32[256,512]{0,1:T(8,128)}), (f32[256,2048]{1,0:T(8,128)}, f32[256,64]{0,1:T(8,128)}, f32[256,512]{0,1:T(8,128)})) %all-reduce.12.cloned.1.call-update) | async-done | bytes 2686992 | tf_op jit(solution)/shard_map/psum | solution.py:327
  1300.8 6.4 fusion.119
  1307.2 125.3 %reduce-scatter.13.cloned.1.call-done = f32[8,2,144,512]{3,2,0,1:T(8,128)} async-done(((f32[8,2,144,2048]{3,2,0,1:T(8,128)}), f32[8,2,144,512]{3,2,0,1:T(8,128)}) %reduce-scatter.13.cloned.1.call-update) | async-done | bytes 4718608 | tf_op jit(solution)/shard_map/reduce_scatter | solution.py:171
  1432.5 5.2 copy.75
  1437.7 5.8 all-to-all-start.1
  1445.4 11.0 fusion.15
  1456.4 12.9 fusion.12
  1469.3 123.4 %all-to-all-done.1 = f32[8,2,144,512]{3,2,1,0:T(8,128)} async-done(((f32[8,2,144,512]{3,2,1,0:T(8,128)}), f32[8,2,144,512]{3,2,1,0:T(8,128)}, u32[]{:S(2)}, u32[]{:S(2)}) %all-to-all-start.1) | async-done | bytes 4718624 | tf_op jit(solution)/shard_map/all_to_all | solution.py:258
  1592.7 8.2 gather_fusion.1
  1600.9 4.7 reshape.345
  1612.3 5.0 fusion.39
  1617.2 27.3 %all-reduce.5 = (f32[2048]{0:T(1024)S(1)}, f32[512]{0:T(512)S(1)}, f32[2048]{0:T(1024)S(1)}) all-reduce(f32[2048]{0:T(1024)S(1)} %get-tuple-element.61, f32[512]{0:T(512)S(1)} %get-tuple-element.63, f32[2048]{0:T(1024)S(1)} %get-tuple-element.59), channel_id=6, replica_groups=mesh['wide'=8,'narrow'=4] {'wide'}, use_global_device_ids=true, to_apply=%region_28.29.clone | all-reduce | flops 4608 | bytes 36864
  1650.8 192.5 %reduce-scatter.27.cloned.1.call-done = f32[256,2,704]{0,2,1:T(8,128)} async-done(((f32[2048,2,704]{0,2,1:T(8,128)}), f32[256,2,704]{0,2,1:T(8,128)}) %reduce-scatter.27.cloned.1.call-update) | async-done | bytes 1441808 | tf_op jit(solution)/shard_map/reduce_scatter | solution.py:345
  1843.4 69.6 %reduce-scatter.23.cloned.1.call-done = f32[64,1024]{1,0:T(8,128)} async-done(((f32[512,1024]{1,0:T(8,128)}), f32[64,1024]{1,0:T(8,128)}) %reduce-scatter.23.cloned.1.call-update) | async-done | bytes 262160 | tf_op jit(solution)/shard_map/reduce_scatter | solution.py:343
  1913.0 94.4 %reduce-scatter.25.cloned.1.call-done = f32[512,256]{1,0:T(8,128)} async-done(((f32[512,2048]{1,0:T(8,128)}), f32[512,256]{1,0:T(8,128)}) %reduce-scatter.25.cloned.1.call-update) | async-done | bytes 524304 | tf_op jit(solution)/shard_map/reduce_scatter | solution.py:344
  2007.3 99.8 %reduce-scatter.21.cloned.1.call-done = f32[256,576]{0,1:T(8,128)} async-done(((f32[2048,576]{0,1:T(8,128)}), f32[256,576]{0,1:T(8,128)}) %reduce-scatter.21.cloned.1.call-update) | async-done | bytes 589840 | tf_op jit(solution)/shard_map/reduce_scatter | solution.py:342
  2107.2 121.4 %reduce-scatter.19.cloned.1.call-done = f32[256,768]{1,0:T(8,128)} async-done(((f32[2048,768]{1,0:T(8,128)}), f32[256,768]{1,0:T(8,128)}) %reduce-scatter.19.cloned.1.call-update) | async-done | bytes 786448 | tf_op jit(solution)/shard_map/reduce_scatter | solution.py:341
  (274 shorter events, 125.5 us)
Async XLA Ops:
  7.2 716.0 %copy-start = (bf16[2,352,2048]{2,1,0:T(8,128)(2,1)S(1)}, bf16[2,352,2048]{2,1,0:T(8,128)(2,1)}, u32[]{:S(2)}) copy-start(bf16[2,352,2048]{2,1,0:T(8,128)(2,1)} %param.30) | copy-start | bytes 8650756
  7.2 54.5 %copy-start.33 = (f32[2048]{0:T(1024)S(1)}, f32[2048]{0:T(1024)}, u32[]{:S(2)}) copy-start(f32[2048]{0:T(1024)} %param.20) | copy-start | bytes 24580
  7.2 54.5 %all-gather.10.cloned.1.call-start = ((), (), s32[]{:S(2)}) async-start(), calls=%async_computation.15 | async-start | bytes 2654208 | tf_op jit(solution)/shard_map/all_gather | solution.py:203
  7.9 93.1 %all-gather.12.cloned.1.call-start = ((), (), s32[]{:S(2)}) async-start(), calls=%async_computation.16 | async-start | bytes 1179648 | tf_op jit(solution)/shard_map/all_gather | solution.py:204
  8.7 154.9 %all-gather.8.cloned.1.call-start = ((), (), s32[]{:S(2)}) async-start(), calls=%async_computation.14 | async-start | bytes 3538944 | tf_op jit(solution)/shard_map/all_gather | solution.py:202
  9.4 204.8 %all-gather.14.cloned.1.call-start = ((), (), s32[]{:S(2)}) async-start(), calls=%async_computation.17 | async-start | bytes 2359296 | tf_op jit(solution)/shard_map/all_gather | solution.py:205
  10.0 259.5 %all-reduce.10.cloned.1.call-start = ((), (), s32[]{:S(2)}) async-start(), calls=%async_computation.18 | async-start | bytes 4194304 | tf_op jit(solution)/shard_map/psum | solution.py:239
  11.6 95.8 %copy-start.61 = (f32[256]{0:T(256)}, f32[256]{0:T(256)S(1)}, u32[]{:S(2)}) copy-start(f32[256]{0:T(256)S(1)} %fusion.105) | copy-start | bytes 3076
  12.9 48.8 %copy-start.29 = (s32[256,6]{1,0:T(8,128)}, s32[256,6]{1,0:T(8,128)S(1)}, u32[]{:S(2)}) copy-start(s32[256,6]{1,0:T(8,128)S(1)} %copy.71) | copy-start | bytes 18436
  15.2 148.4 %copy-start.44 = (f32[256]{0:T(256)}, f32[256]{0:T(256)S(1)}, u32[]{:S(2)}) copy-start(f32[256]{0:T(256)S(1)} %get-tuple-element.103) | copy-start | bytes 3076
  61.7 39.3 %copy-start.53 = (f32[512]{0:T(512)S(1)}, f32[512]{0:T(512)}, u32[]{:S(2)}) copy-start(f32[512]{0:T(512)} %param.23) | copy-start | bytes 6148
  64.6 102.6 %copy-start.8 = (f32[256,576]{0,1:T(8,128)}, f32[256,576]{0,1:T(8,128)S(1)}, u32[]{:S(2)}) copy-start(f32[256,576]{0,1:T(8,128)S(1)} %fusion.121) | copy-start | bytes 1769476
  65.4 40.3 %copy-start.56 = (f32[256]{0:T(256)}, f32[256]{0:T(256)S(1)}, u32[]{:S(2)}) copy-start(f32[256]{0:T(256)S(1)} %get-tuple-element.105) | copy-start | bytes 3076
  108.2 59.1 %copy-start.35 = (f32[256,32]{0,1:T(8,128)}, f32[256,32]{0,1:T(8,128)S(1)}, u32[]{:S(2)}) copy-start(f32[256,32]{0,1:T(8,128)S(1)} %get-tuple-element.98) | copy-start | bytes 98308
  108.2 59.1 %copy-start.37 = (f32[256,32]{0,1:T(8,128)}, f32[256,32]{0,1:T(8,128)S(1)}, u32[]{:S(2)}) copy-start(f32[256,32]{0,1:T(8,128)S(1)} %get-tuple-element.99) | copy-start | bytes 98308
  169.8 48.2 %copy-start.20 = (bf16[4,256,128]{1,2,0:T(8,128)(2,1)}, bf16[4,256,128]{1,2,0:T(8,128)(2,1)S(1)}, u32[]{:S(2)}) copy-start(bf16[4,256,128]{1,2,0:T(8,128)(2,1)S(1)} %convolution_convert_fusion.1) | copy-start | bytes 786436
  230.4 42.8 %copy-start.46 = (f32[2048]{0:T(1024)S(1)}, f32[2048]{0:T(1024)}, u32[]{:S(2)}) copy-start(f32[2048]{0:T(1024)} %param.26) | copy-start | bytes 24580
  295.2 14.6 copy-start.63
  295.2 218.5 %all-to-all-start = ((bf16[8,2,144,2048]{3,2,1,0:T(8,128)(2,1)}), bf16[8,2,144,2048]{3,2,1,0:T(8,128)(2,1)}, u32[]{:S(2)}, u32[]{:S(2)}) async-start(bf16[8,2,144,2048]{3,2,1,0:T(8,128)(2,1)} %bitcast.196), calls=%async_computation.1 | async-start | bytes 18874368 | tf_op jit(solution)/shard_map/all_to_all | solution.py:249
  309.9 28.8 %copy-start.27 = (f32[256,6]{1,0:T(8,128)}, f32[256,6]{1,0:T(8,128)S(1)}, u32[]{:S(2)}) copy-start(f32[256,6]{1,0:T(8,128)S(1)} %copy.69) | copy-start | bytes 18436
  513.7 209.4 %all-to-all-start.2 = ((bf16[8,2,144,2048]{3,2,1,0:T(8,128)(2,1)}), bf16[8,2,144,2048]{3,2,1,0:T(8,128)(2,1)}, u32[]{:S(2)}, u32[]{:S(2)}) async-start(bf16[8,2,144,2048]{3,2,1,0:T(8,128)(2,1)} %multiply_convert_fusion), calls=%async_computation.5 | async-start | bytes 18874368 | tf_op jit(solution)/shard_map/all_to_all | solution.py:285
  519.4 379.9 %reduce-scatter.17.cloned.1.call-start = ((), (), s32[]{:S(2)}) async-start(), calls=%async_computation.24 | async-start | bytes 23592960 | tf_op jit(solution)/shard_map/reduce_scatter | solution.py:171
  734.0 14.6 copy-start.68
  734.0 14.6 copy-start.70
  761.6 313.7 %all-gather.16.cloned.1.call-start = ((), (), s32[]{:S(2)}) async-start(), calls=%async_computation.19 | async-start | bytes 6488064 | tf_op jit(solution)/shard_map/all_gather | solution.py:206
  762.3 372.6 %all-gather.18.cloned.1.call-start = ((), (), s32[]{:S(2)}) async-start(), calls=%async_computation.20 | async-start | bytes 3244032 | tf_op jit(solution)/shard_map/all_gather | solution.py:207
  899.3 244.3 %all-to-all-start.3 = ((f32[8,2,144,512]{3,2,1,0:T(8,128)}), f32[8,2,144,512]{3,2,1,0:T(8,128)}, u32[]{:S(2)}, u32[]{:S(2)}) async-start(f32[8,2,144,512]{3,2,1,0:T(8,128)} %reduce-scatter.17.cloned.1.call-done), calls=%async_computation.7 | async-start | bytes 9437184 | tf_op jit(solution)/shard_map/all_to_all | solution.py:301
  904.7 270.0 %reduce-scatter.15.cloned.1.call-start = ((), (), s32[]{:S(2)}) async-start(), calls=%async_computation.23 | async-start | bytes 2621440 | tf_op jit(solution)/shard_map/reduce_scatter | solution.py:305
  1143.5 56.4 %all-gather.20.cloned.1.call-start = ((), (), s32[]{:S(2)}) async-start(), calls=%async_computation.25 | async-start | bytes 2621440 | tf_op jit(solution)/shard_map/all_gather | solution.py:306
  1156.4 43.5 %copy-start.47 = (f32[2048]{0:T(1024)S(1)}, f32[2048]{0:T(1024)}, u32[]{:S(2)}) copy-start(f32[2048]{0:T(1024)} %param.26) | copy-start | bytes 24580
  1156.4 43.5 %copy-start.60 = (f32[256]{0:T(256)S(1)}, f32[256]{0:T(256)}, u32[]{:S(2)}) copy-start(f32[256]{0:T(256)} %copy-done.59) | copy-start | bytes 3076
  1176.6 26.3 %copy-start.65 = (f32[256]{0:T(256)S(1)}, f32[256]{0:T(256)}, u32[]{:S(2)}) copy-start(f32[256]{0:T(256)} %get-tuple-element.106) | copy-start | bytes 3076
  1176.6 115.8 %all-reduce.12.cloned.1.call-start = ((), (), s32[]{:S(2)}) async-start(), calls=%async_computation.32 | async-start | bytes 5373952 | tf_op jit(solution)/shard_map/psum | solution.py:327
  1231.6 200.9 %reduce-scatter.13.cloned.1.call-start = ((), (), s32[]{:S(2)}) async-start(), calls=%async_computation.22 | async-start | bytes 23592960 | tf_op jit(solution)/shard_map/reduce_scatter | solution.py:171
  1242.7 367.2 %reduce-scatter.11.cloned.1.call-start = ((), (), s32[]{:S(2)}) async-start(), calls=%async_computation.21 | async-start | bytes 2621440 | tf_op jit(solution)/shard_map/reduce_scatter | solution.py:263
  1247.9 403.0 %reduce-scatter.29.cloned.1.call-start = ((), (), s32[]{:S(2)}) async-start(), calls=%async_computation.31 | async-start | bytes 6488064 | tf_op jit(solution)/shard_map/reduce_scatter | solution.py:346
  1252.5 590.9 %reduce-scatter.27.cloned.1.call-start = ((), (), s32[]{:S(2)}) async-start(), calls=%async_computation.30 | async-start | bytes 12976128 | tf_op jit(solution)/shard_map/reduce_scatter | solution.py:345
  1260.7 652.2 %reduce-scatter.23.cloned.1.call-start = ((), (), s32[]{:S(2)}) async-start(), calls=%async_computation.28 | async-start | bytes 2359296 | tf_op jit(solution)/shard_map/reduce_scatter | solution.py:343
  1264.7 742.7 %reduce-scatter.25.cloned.1.call-start = ((), (), s32[]{:S(2)}) async-start(), calls=%async_computation.29 | async-start | bytes 4718592 | tf_op jit(solution)/shard_map/reduce_scatter | solution.py:344
  1269.1 24.7 %copy-start.62 = (f32[256]{0:T(256)S(1)}, f32[256]{0:T(256)}, u32[]{:S(2)}) copy-start(f32[256]{0:T(256)} %copy-done.61) | copy-start | bytes 3076
  1269.1 25.7 %copy-start.66 = (f32[256]{0:T(256)S(1)}, f32[256]{0:T(256)}, u32[]{:S(2)}) copy-start(f32[256]{0:T(256)} %get-tuple-element.104) | copy-start | bytes 3076
  1269.1 27.6 %copy-start.34 = (f32[2048]{0:T(1024)S(1)}, f32[2048]{0:T(1024)}, u32[]{:S(2)}) copy-start(f32[2048]{0:T(1024)} %param.20) | copy-start | bytes 24580
  1269.1 27.6 %copy-start.45 = (f32[256]{0:T(256)S(1)}, f32[256]{0:T(256)}, u32[]{:S(2)}) copy-start(f32[256]{0:T(256)} %copy-done.44) | copy-start | bytes 3076
  1269.2 838.0 %reduce-scatter.21.cloned.1.call-start = ((), (), s32[]{:S(2)}) async-start(), calls=%async_computation.27 | async-start | bytes 5308416 | tf_op jit(solution)/shard_map/reduce_scatter | solution.py:342
  1299.8 928.8 %reduce-scatter.19.cloned.1.call-start = ((), (), s32[]{:S(2)}) async-start(), calls=%async_computation.26 | async-start | bytes 7077888 | tf_op jit(solution)/shard_map/reduce_scatter | solution.py:341
  1437.7 155.0 %all-to-all-start.1 = ((f32[8,2,144,512]{3,2,1,0:T(8,128)}), f32[8,2,144,512]{3,2,1,0:T(8,128)}, u32[]{:S(2)}, u32[]{:S(2)}) async-start(f32[8,2,144,512]{3,2,1,0:T(8,128)} %copy.75), calls=%async_computation.3 | async-start | bytes 9437184 | tf_op jit(solution)/shard_map/all_to_all | solution.py:258
  1445.4 11.0 copy-start.69
  1612.2 34.1 %copy-start.64 = (f32[256]{0:T(256)S(1)}, f32[256]{0:T(256)}, u32[]{:S(2)}) copy-start(f32[256]{0:T(256)} %get-tuple-element.102) | copy-start | bytes 3076
  (47 other events, 147.1 us)
Sparse Core Ops, SparseCore 0:
  10.1 51.6 all-gather.9
  63.9 37.1 all-gather.11
  103.3 60.2 all-gather.7
  165.5 48.7 all-gather.13
  218.1 51.4 all-reduce.9
  761.7 137.5 reduce-scatter.16
  901.3 173.9 all-gather.15
  1077.3 57.5 all-gather.17
  1143.7 30.9 reduce-scatter.14
  1176.8 23.1 all-gather.19
  1231.8 60.6 all-reduce.11
  1294.9 137.5 reduce-scatter.12
  1435.6 31.1 reduce-scatter.10
  1470.9 176.0 reduce-scatter.28
  1651.0 192.3 reduce-scatter.26
  1847.4 65.5 reduce-scatter.22
  1917.0 90.2 reduce-scatter.24
  2011.4 95.6 reduce-scatter.20
  2111.3 117.2 reduce-scatter.18
where the time goes:
time: 2240 us
  waiting for transfers between devices  1830 us (82%)
  matrix products  155 us (7%)
  local copies, waits for them, and re-layouts  123 us (5%)
  other arithmetic  53.9 us (2%)
  starting transfers between devices  32.7 us (1%)
  blocking collectives  27.3 us (1%)
    reduce_scatter x2, waiting for transfers between devices, narrow_terms(): return lax.psum_scatter(terms, 'narrow', scatter_dimension=3, tiled=True)  261 us
    reduce_scatter x1, waiting for transfers between devices, per_device(): lax.psum_scatter(grad_shin, 'wide', scatter_dimension=0, tiled=True)  193 us
    all_to_all x1, waiting for transfers between devices, per_device(): lax.all_to_all(grad_send, 'wide', split_axis=0, concat_axis=0, tiled=True)  190 us
    all_gather x1, waiting for transfers between devices, per_device(): lax.all_gather(w_shared_in, 'wide', axis=0, tiled=True)  170 us
    all_to_all x1, waiting for transfers between devices, per_device(): lax.all_to_all(send_rows, 'wide', split_axis=0, concat_axis=0, tiled=True)  165 us
    all_to_all x1, waiting for transfers between devices, per_device(): lax.all_to_all(partial_out, 'wide', split_axis=0, concat_axis=0, tiled=True)  123 us
    reduce_scatter x1, waiting for transfers between devices, per_device(): lax.psum_scatter(grad_wq, 'wide', scatter_dimension=0, tiled=True)  121 us
    reduce_scatter x1, waiting for transfers between devices, per_device(): lax.psum_scatter(grad_wkva, 'wide', scatter_dimension=0, tiled=True)  99.8 us
  transfers between devices with their start and end apart: 23, of which 20 were waited for; matrix products, arithmetic and copies ran while one was open for 10% of the time, Pallas kernels for 0%

commit v1 on v0

v1 whole, which is shorter than its diff:
```python
import functools

import jax
import jax.numpy as jnp
from jax import lax
from jax.experimental import pallas as pl
from jax.experimental.pallas import tpu as pltpu
from jax.sharding import PartitionSpec as P

DH = 128
DR = 64
KVR = 512


EPS = 1e-06
THETA = 50000.0
NEG_BIG = -1e30
BLOCK_ROWS = 512


def positions(seg_ids):
    row_index = jnp.arange(seg_ids.shape[0], dtype=jnp.int32)
    starts = jnp.concatenate([jnp.ones((1,), dtype=bool), seg_ids[1:] != seg_ids[:-1]])
    begins = lax.cummax(jnp.where(starts, row_index, 0), axis=0)
    return (row_index - begins).astype(jnp.float32)


def rotary_tables(pos_float):
    half_dim = DR // 2
    inv_freq = THETA ** (-(jnp.arange(half_dim, dtype=jnp.float32) * 2.0 / DR))
    angles = pos_float[:, None] * inv_freq[None, :]
    return (jnp.cos(angles), jnp.sin(angles))


def rotate(values, cos_tab, sin_tab):
    half_dim = values.shape[-1] // 2
    lower_half = values[..., :half_dim]
    upper_half = values[..., half_dim:]
    return jnp.concatenate(
        [lower_half * cos_tab - upper_half * sin_tab, upper_half * cos_tab + lower_half * sin_tab],
        -1,
    )


def unrotate(values, cos_tab, sin_tab):
    half_dim = values.shape[-1] // 2
    lower_half = values[..., :half_dim]
    upper_half = values[..., half_dim:]
    return jnp.concatenate(
        [lower_half * cos_tab + upper_half * sin_tab, upper_half * cos_tab - lower_half * sin_tab],
        -1,
    )


def rms_forward(values, gain_vec):
    inv_rms = lax.rsqrt(jnp.mean(values * values, axis=-1, keepdims=True) + EPS)
    return (values * inv_rms * gain_vec, inv_rms)


def rms_backward(values, inv_rms, gain_vec, grad_out):
    scaled = grad_out * gain_vec
    grad_in = inv_rms * scaled - values * inv_rms**3 * jnp.mean(
        values * scaled, axis=-1, keepdims=True
    )
    grad_gain = jnp.sum(grad_out * values * inv_rms, axis=0)
    return (grad_in, grad_gain)


def masked_scores(q_blk, k_heads, seg_rows, seg_cols, row_pos, col_pos):
    scale = (DH + DR) ** (-0.5)
    scores = jnp.einsum("hqc,hkc->hqk", q_blk, k_heads, preferred_element_type=jnp.float32) * scale
    allowed = (seg_rows[:, None] == seg_cols[None, :]) & (col_pos[None, :] <= row_pos[:, None])
    return jnp.where(allowed[None], scores, NEG_BIG)


def attention_forward(q_heads, k_heads, v_heads, seg_ids):
    head_count = q_heads.shape[0]
    row_total = q_heads.shape[1]
    block_rows = min(row_total, BLOCK_ROWS)
    block_count = row_total // block_rows
    col_pos = jnp.arange(row_total, dtype=jnp.int32)

    def one_block(start):
        row_pos = start + jnp.arange(block_rows, dtype=jnp.int32)
        scores = masked_scores(q_heads, k_heads, seg_ids, seg_ids, row_pos, col_pos)
        top_score = jnp.max(scores, axis=-1, keepdims=True)
        log_total = top_score + jnp.log(
            jnp.sum(jnp.exp(scores - top_score), axis=-1, keepdims=True)
        )
        prob_low = jnp.exp(scores - log_total).astype(jnp.bfloat16)
        attended = jnp.einsum("hqk,hkd->hqd", prob_low, v_heads, preferred_element_type=jnp.float32)
        return (attended.astype(jnp.bfloat16), log_total)

    starts = jnp.arange(block_count, dtype=jnp.int32) * block_rows
    attended, log_total = lax.map(one_block, starts)
    attended = attended.transpose(1, 0, 2, 3).reshape(head_count, row_total, -1)
    log_total = log_total.transpose(1, 0, 2, 3).reshape(head_count, row_total, 1)
    return (attended, log_total)


def attention_backward(q_heads, k_heads, v_heads, grad_att, log_total, seg_ids):
    scale = (DH + DR) ** (-0.5)
    head_count = q_heads.shape[0]
    row_total = q_heads.shape[1]
    block_rows = min(row_total, BLOCK_ROWS)
    block_count = row_total // block_rows
    col_pos = jnp.arange(row_total, dtype=jnp.int32)

    def one_block(carry, start):
        grad_k_acc, grad_v_acc = carry
        row_pos = start + jnp.arange(block_rows, dtype=jnp.int32)
        scores = masked_scores(q_heads, k_heads, seg_ids, seg_ids, row_pos, col_pos)
        prob_full = jnp.exp(scores - log_total)
        prob_low = prob_full.astype(jnp.bfloat16)
        grad_v_blk = jnp.einsum(
            "hqk,hqd->hkd", prob_low, grad_att, preferred_element_type=jnp.float32
        )
        grad_prob = jnp.einsum(
            "hqd,hkd->hqk", grad_att, v_heads, preferred_element_type=jnp.float32
        )
        row_dot = jnp.sum(prob_full * grad_prob, axis=-1, keepdims=True)
        grad_scores = (prob_full * (grad_prob - row_dot) * scale).astype(jnp.bfloat16)
        grad_q_blk = jnp.einsum(
            "hqk,hkc->hqc", grad_scores, k_heads, preferred_element_type=jnp.float32
        )
        grad_k_blk = jnp.einsum(
            "hqk,hqc->hkc", grad_scores, q_heads, preferred_element_type=jnp.float32
        )
        return ((grad_k_acc + grad_k_blk, grad_v_acc + grad_v_blk), grad_q_blk)

    starts = jnp.arange(block_count, dtype=jnp.int32) * block_rows
    init_acc = (jnp.zeros(k_heads.shape, jnp.float32), jnp.zeros(v_heads.shape, jnp.float32))
    (grad_k, grad_v), grad_q_blocks = lax.scan(one_block, init_acc, starts)
    grad_q = grad_q_blocks.transpose(1, 0, 2, 3).reshape(head_count, row_total, -1)
    return (grad_q, grad_k, grad_v)


MESH_IDS = pl.DeviceIdType.MESH


def axis_parts(mesh):
    devices = mesh.devices
    found = []
    for axis in range(devices.ndim):
        line = [devices[tuple(i if k == axis else 0 for k in range(devices.ndim))] for i in range(devices.shape[axis])]
        places = [(*dev.coords, dev.core_on_chip) for dev in line]
        parts = []
        for k, name in enumerate(("x", "y", "z", "core")):
            values = [p[k] for p in places]
            size = len(set(values))
            if size > 1:
                stride = next(i for i, v in enumerate(values) if v != values[0])
                parts.append((stride, name, size))
        found.append(tuple((name, size) for stride, name, size in sorted(parts, reverse=True)))
    return tuple(found)


def fits_kernels(mesh):
    (wide, narrow) = axis_parts(mesh)
    return (
        len(wide) == 2
        and wide[1][1] == 2
        and len(narrow) == 2
        and narrow[0][1] == 2
        and narrow[1] == ("core", 2)
    )


class Spot:
    def __init__(self, line):
        wide, narrow = lax.axis_index("wide"), lax.axis_index("narrow")
        self.line = line
        self.z, self.x = wide // 2, wide % 2
        self.y, self.c = narrow // 2, narrow % 2

    def flips(self, a, b, c):
        return a * (1 - c) + b * c, b * (1 - c) + a * c

    def at(self, z, a, b, c):
        fx, fy = self.flips(a, b, c)
        x = self.x + fx * (1 - 2 * self.x)
        y = self.y + fy * (1 - 2 * self.y)
        return z * 2 + x, y * 2 + c

    def device(self, z, a, b, c):
        wide, narrow = self.at(z, a, b, c)
        return {"wide": wide, "narrow": narrow}

    def inside(self, z):
        return (z >= 0) & (z < self.line)


def gather_offsets(kind, line):
    ks = [(0, 0)] if kind == "narrow" else [(0, 0)] + [(d, k) for k in range(1, line) for d in (1, -1)]
    out = []
    for d, k in ks:
        for a in (0, 1):
            if kind == "narrow" and a:
                continue
            for b in (0, 1):
                if kind == "wide" and b:
                    continue
                level = k + a + (2 if b else 0) + (a if b else 0)
                out.append((level, d, k, a, b))
    return sorted(out, key=lambda o: (o[0], o[3], o[4], o[2]))


def sends_of(kind, d, k, a, b):
    to = []
    if not a and not b and kind != "narrow":
        to += [("z", 1), ("z", -1)] if k == 0 else [("z", d)]
    if kind in ("all", "wide") and not a and not b:
        to.append(("a", 0))
    if kind in ("all", "narrow") and not b:
        to.append(("b", 0))
    if kind in ("all", "narrow"):
        to.append(("core", 0))
    return to


def count_sends(kind, line):
    return sum(len(sends_of(kind, *o[1:])) for o in gather_offsets(kind, line))


def gather_kernel(line, kinds, views, *refs):
    count = len(kinds)
    srcs, dsts = refs[:count], refs[count : 2 * count]
    sends, recvs, local = refs[2 * count : 3 * count], refs[3 * count : 4 * count], refs[4 * count]
    spot = Spot(line)
    z, c = spot.z, spot.c
    use_line = any(kind != "narrow" for kind in kinds)
    pairs = set()
    for kind in kinds:
        pairs |= {"all": {(1, 0, 0), (0, 1, 0), (0, 0, 1)}, "wide": {(1, 0, 0)}, "narrow": {(0, 1, 0), (0, 0, 1)}}[kind]
    greet_pairs = sorted(pairs)

    def color(kind):
        return c if kind == "all" else 0

    def target(kind, move, step):
        if kind == "all":
            where = {"z": (z + step, 0, 0, c), "a": (z, 1, 0, c), "b": (z, 0, 1, c), "core": (z, 0, 0, 1 - c)}[move]
            return spot.device(*where)
        wide, narrow = z * 2 + spot.x, spot.y * 2 + c
        if move == "z":
            return {"wide": wide + 2 * step, "narrow": narrow}
        if move == "a":
            return {"wide": z * 2 + 1 - spot.x, "narrow": narrow}
        if move == "b":
            return {"wide": wide, "narrow": (1 - spot.y) * 2 + c}
        return {"wide": wide, "narrow": spot.y * 2 + 1 - c}

    def origin(kind, zz, a, b, flip):
        if kind == "all":
            wide, narrow = spot.at(zz, a, b, c) if not flip else spot.at(zz, a, b, 1 - c)
            return wide * 4 + narrow
        if kind == "wide":
            return zz * 2 + spot.x + a * (1 - 2 * spot.x)
        return (spot.y + b * (1 - 2 * spot.y)) * 2 + c + flip * (1 - 2 * c)

    def move_of(i, block, first, move, step, number):
        view = views[i](dsts[i], block)
        return pltpu.make_async_remote_copy(
            src_ref=srcs[i] if first else view,
            dst_ref=view,
            send_sem=sends[i].at[number],
            recv_sem=recvs[i].at[block],
            device_id=target(kinds[i], move, step),
            device_id_type=MESH_IDS,
        )

    barrier = pltpu.get_barrier_semaphore()
    total = 0
    for a, b, flip in greet_pairs:
        dev = {"wide": z * 2 + spot.x + a * (1 - 2 * spot.x), "narrow": (spot.y + b * (1 - 2 * spot.y)) * 2 + c + flip * (1 - 2 * c)}
        pl.semaphore_signal(barrier, inc=1, device_id=dev, device_id_type=MESH_IDS)
        total += 1
    if use_line:
        for step in (-1, 1):
            @pl.when(spot.inside(z + step))
            def _():
                dev = {"wide": (z + step) * 2 + spot.x, "narrow": spot.y * 2 + c}
                pl.semaphore_signal(barrier, inc=1, device_id=dev, device_id_type=MESH_IDS)
        inner = spot.inside(z - 1) & spot.inside(z + 1)
        @pl.when(inner)
        def _():
            pl.semaphore_wait(barrier, total + 2)
        @pl.when(jnp.logical_not(inner))
        def _():
            pl.semaphore_wait(barrier, total + 1)
    else:
        pl.semaphore_wait(barrier, total)

    own_copies = []
    for i, kind in enumerate(kinds):
        own_copies.append(pltpu.make_async_copy(srcs[i], views[i](dsts[i], origin(kind, z, 0, 0, 0)), local.at[i]))
        own_copies[-1].start()

    pending = []
    plans = [(level, i, (d, k, a, b)) for i, kind in enumerate(kinds) for level, d, k, a, b in gather_offsets(kind, line)]
    numbers = [0] * count
    plans.sort(key=lambda p: p[0])
    for level, i, (d, k, a, b) in plans:
        kind = kinds[i]
        zz = z - d * k
        block = origin(kind, zz, a, b, 0)
        first = k == 0 and not a and not b
        outs = []
        for move, step in sends_of(kind, d, k, a, b):
            outs.append((move, step, numbers[i]))
            numbers[i] += 1

        def act(i=i, block=block, first=first, outs=outs, zz=zz):
            if not first:
                view = views[i](dsts[i], block)
                pltpu.make_async_remote_copy(
                    src_ref=view, dst_ref=view, send_sem=sends[i].at[0], recv_sem=recvs[i].at[block],
                    device_id=target(kinds[i], "core" if kinds[i] != "wide" else "a", 0), device_id_type=MESH_IDS,
                ).wait_recv()
            for move, step, number in outs:
                if move == "z":
                    @pl.when(spot.inside(z + step))
                    def _():
                        move_of(i, block, first, move, step, number).start()
                else:
                    move_of(i, block, first, move, step, number).start()

        def finish(i=i, block=block, first=first, outs=outs):
            for move, step, number in outs:
                if move == "z":
                    @pl.when(spot.inside(z + step))
                    def _():
                        move_of(i, block, first, move, step, number).wait_send()
                else:
                    move_of(i, block, first, move, step, number).wait_send()

        if k == 0:
            act()
        else:
            pl.when(spot.inside(zz))(act)
        pending.append((k, zz, finish))

    for i, kind in enumerate(kinds):
        if kind == "wide":
            continue
        for zz in range(line) if kind == "all" else (0,):
            for a in (0, 1) if kind == "all" else (0,):
                for b in (0, 1):
                    block = origin(kind, zz, a, b, 1)
                    view = views[i](dsts[i], block)
                    pltpu.make_async_remote_copy(
                        src_ref=view, dst_ref=view, send_sem=sends[i].at[0], recv_sem=recvs[i].at[block],
                        device_id=target(kind, "core", 0), device_id_type=MESH_IDS,
                    ).wait_recv()
    for k, zz, finish in pending:
        if k == 0:
            finish()
        else:
            pl.when(spot.inside(zz))(finish)
    for copy in own_copies:
        copy.wait()


def gather(line, items, collective_id):
    kinds = [kind for _, kind, _ in items]
    counts = {"all": line * 8, "wide": line * 2, "narrow": 4}

    def view_of(shape, axis):
        if axis == "grid":
            rows, cols = shape

            def tile(ref, block):
                at_row = pl.multiple_of((block % 4) * rows, rows)
                at_col = pl.multiple_of((block // 4) * cols, cols)
                return ref.at[pl.ds(at_row, rows), pl.ds(at_col, cols)]

            return tile
        size = shape[axis]

        def view(ref, block):
            at = pl.ds(pl.multiple_of(block * size, size), size)
            return ref.at[tuple(at if k == axis else slice(None) for k in range(len(shape)))]

        return view

    views = [view_of(arr.shape, axis) for arr, _, axis in items]
    def whole(arr, kind, axis):
        if axis == "grid":
            return (arr.shape[0] * 4, arr.shape[1] * line * 2)
        return tuple(s * counts[kind] if k == axis else s for k, s in enumerate(arr.shape))

    shapes = [jax.ShapeDtypeStruct(whole(*item), item[0].dtype) for item in items]
    moved = sum((counts[kind] - 1) * arr.size * arr.dtype.itemsize for arr, kind, _ in items)
    return pl.pallas_call(
        functools.partial(gather_kernel, line, kinds, views),
        out_shape=shapes,
        in_specs=[pl.BlockSpec(memory_space=pltpu.VMEM)] * len(items),
        out_specs=[pl.BlockSpec(memory_space=pl.ANY)] * len(items),
        scratch_shapes=[pltpu.SemaphoreType.DMA((count_sends(kind, line),)) for kind in kinds]
        + [pltpu.SemaphoreType.DMA((counts[kind],)) for kind in kinds]
        + [pltpu.SemaphoreType.DMA((len(items),))],
        compiler_params=pltpu.CompilerParams(collective_id=collective_id, has_side_effects=True),
        cost_estimate=pl.CostEstimate(flops=0, bytes_accessed=moved, transcendentals=0),
        name="gather_blocks",
    )(*[arr for arr, _, _ in items])


def reduce_kernel(line, kind, rows, part, out, held, summed, from_core, from_b, from_a, from_z,
                  load_sem, core_send, core_recv, b_send, b_recv, a_send, a_recv, z_send, z_recv):
    spot = Spot(line)
    z, c = spot.z, spot.c
    full = kind == "all"
    zs = range(line) if full else (0,)
    flags = (0, 1) if full else (0,)

    def where(zz, a, b, cc):
        if full:
            wide, narrow = spot.at(zz, a, b, cc)
            return wide * 4 + narrow
        return (spot.y + b * (1 - 2 * spot.y)) * 2 + cc

    def device(zz, a, b, cc):
        if full:
            return spot.device(zz, a, b, cc)
        return {"wide": lax.axis_index("wide"), "narrow": (spot.y + b * (1 - 2 * spot.y)) * 2 + cc}

    def block(ref, index):
        return ref.at[pl.ds(pl.multiple_of(index * rows, rows), rows), :]

    def slot(zz, a, b):
        return (zz * 2 + a) * 2 + b if full else b

    barrier = pltpu.get_barrier_semaphore()
    total = 0
    if full:
        pl.semaphore_signal(barrier, inc=1, device_id=device(z, 1, 0, c), device_id_type=MESH_IDS)
        total += 1
    pl.semaphore_signal(barrier, inc=1, device_id=device(z, 0, 1, c), device_id_type=MESH_IDS)
    pl.semaphore_signal(barrier, inc=1, device_id=device(z, 0, 0, 1 - c), device_id_type=MESH_IDS)
    total += 2
    if full:
        for step in (-1, 1):
            @pl.when(spot.inside(z + step))
            def _():
                pl.semaphore_signal(barrier, inc=1, device_id=device(z + step, 0, 0, c), device_id_type=MESH_IDS)
        inner = spot.inside(z - 1) & spot.inside(z + 1)
        @pl.when(inner)
        def _():
            pl.semaphore_wait(barrier, total + 2)
        @pl.when(jnp.logical_not(inner))
        def _():
            pl.semaphore_wait(barrier, total + 1)
    else:
        pl.semaphore_wait(barrier, total)

    if full:
        steps = [(d, k) for k in range(line - 1, 0, -1) for d in (1, -1)] + [(0, 0)]
    else:
        steps = [(0, 0)]
    order = [(b, a, d, k) for b in (1, 0) for a in reversed(flags) for d, k in steps]

    def to_core(zz, a, b):
        return pltpu.make_async_remote_copy(
            src_ref=block(part, where(zz, a, b, 1 - c)), dst_ref=from_core.at[slot(zz, a, b)],
            send_sem=core_send.at[slot(zz, a, b)], recv_sem=core_recv.at[slot(zz, a, b)],
            device_id=device(z, 0, 0, 1 - c), device_id_type=MESH_IDS,
        )

    def load(zz, a, b):
        return pltpu.make_async_copy(
            block(part, where(zz, a, b, c)), held.at[slot(zz, a, b)], load_sem.at[slot(zz, a, b)]
        )

    def to_b(zz, a):
        return pltpu.make_async_remote_copy(
            src_ref=summed.at[slot(zz, a, 1)], dst_ref=from_b.at[zz * 2 + a],
            send_sem=b_send.at[zz * 2 + a], recv_sem=b_recv.at[zz * 2 + a],
            device_id=device(z, 0, 1, c), device_id_type=MESH_IDS,
        )

    def to_a(zz):
        return pltpu.make_async_remote_copy(
            src_ref=summed.at[slot(zz, 1, 0)], dst_ref=from_a.at[zz],
            send_sem=a_send.at[zz], recv_sem=a_recv.at[zz],
            device_id=device(z, 1, 0, c), device_id_type=MESH_IDS,
        )

    def to_z(zz, d):
        way = (1 - d) // 2
        return pltpu.make_async_remote_copy(
            src_ref=summed.at[slot(zz, 0, 0)], dst_ref=from_z.at[way * line + zz],
            send_sem=z_send.at[zz], recv_sem=z_recv.at[way * line + zz],
            device_id=device(z + d, 0, 0, c), device_id_type=MESH_IDS,
        )

    def guarded(k, zz, act):
        if k == 0:
            act()
        else:
            pl.when(spot.inside(zz))(act)

    for b, a, d, k in order:
        zz = z + d * k if full else 0
        guarded(k, zz, lambda: (to_core(zz, a, b).start(), load(zz, a, b).start()) and None)

    for b, a, d, k in order:
        zz = z + d * k if full else 0

        def act():
            at = slot(zz, a, b)
            load(zz, a, b).wait()
            to_core(zz, a, b).wait_recv()
            value = held[at].astype(jnp.float32) + from_core[at].astype(jnp.float32)
            if b == 1:
                summed[at] = value.astype(summed.dtype)
                to_b(zz, a).start()
                return
            to_b(zz, a).wait_recv()
            value = value + from_b[zz * 2 + a].astype(jnp.float32)
            if a == 1:
                summed[at] = value.astype(summed.dtype)
                to_a(zz).start()
                return
            if full:
                to_a(zz).wait_recv()
                value = value + from_a[zz].astype(jnp.float32)
            if k:
                way = (1 - d) // 2
                summed[at] = value.astype(summed.dtype)
                @pl.when(spot.inside(z - d))
                def _():
                    to_z(zz, d).wait_recv()
                    summed[at] = (value + from_z[way * line + zz].astype(jnp.float32)).astype(summed.dtype)
                to_z(zz, d).start()
                return
            out[...] = value
            if full:
                for way_d in (1, -1):
                    @pl.when(spot.inside(z - way_d))
                    def _():
                        way = (1 - way_d) // 2
                        to_z(z, way_d).wait_recv()
                        out[...] += from_z[way * line + z].astype(jnp.float32)

        guarded(k, zz, act)

    for b, a, d, k in order:
        zz = z + d * k if full else 0

        def act():
            to_core(zz, a, b).wait_send()
            if b == 1:
                to_b(zz, a).wait_send()
            elif a == 1:
                to_a(zz).wait_send()
            elif k:
                to_z(zz, d).wait_send()

        guarded(k, zz, act)


def reduce_blocks(line, kind, part, collective_id):
    full = kind == "all"
    blocks = line * 8 if full else 4
    rows, width = part.shape[0] // blocks, part.shape[1]
    zs = line if full else 1
    slots = zs * 4 if full else 2
    dma = pltpu.SemaphoreType.DMA
    low = part.dtype
    return pl.pallas_call(
        functools.partial(reduce_kernel, line, kind, rows),
        out_shape=jax.ShapeDtypeStruct((rows, width), jnp.float32),
        in_specs=[pl.BlockSpec(memory_space=pl.ANY)],
        out_specs=pl.BlockSpec(memory_space=pltpu.VMEM),
        scratch_shapes=[
            pltpu.VMEM((slots, rows, width), low),
            pltpu.VMEM((slots, rows, width), low),
            pltpu.VMEM((slots, rows, width), low),
            pltpu.VMEM((zs * 2, rows, width), low),
            pltpu.VMEM((zs, rows, width), low),
            pltpu.VMEM((2 * zs, rows, width), low),
            dma((slots,)),
            dma((slots,)),
            dma((slots,)),
            dma((zs * 2,)),
            dma((zs * 2,)),
            dma((zs,)),
            dma((zs,)),
            dma((zs,)),
            dma((2 * zs,)),
        ],
        compiler_params=pltpu.CompilerParams(collective_id=collective_id, has_side_effects=True),
        cost_estimate=pl.CostEstimate(
            flops=part.size, bytes_accessed=2 * part.size * part.dtype.itemsize, transcendentals=0
        ),
        name="sum_blocks",
    )(part)

class Links:
    AXES = {"all": ("wide", "narrow"), "wide": "wide", "narrow": "narrow"}

    def __init__(self, mesh):
        self.line = axis_parts(mesh)[0][0][1] if fits_kernels(mesh) else None
        self.calls = 0

    def gather(self, *items):
        if self.line:
            self.calls += 1
            return gather(self.line, items, self.calls)
        return [self.plain(*item) for item in items]

    def plain(self, arr, kind, axis):
        if axis == "grid":
            return lax.all_gather(self.plain(arr, "narrow", 0), "wide", axis=1, tiled=True)
        return lax.all_gather(arr, self.AXES[kind], axis=axis, tiled=True)

    def reduce(self, kind, part):
        if self.line:
            self.calls += 1
            return reduce_blocks(self.line, kind, part, self.calls)
        summed = lax.psum_scatter(part, self.AXES[kind], scatter_dimension=0, tiled=True)
        return summed.astype(jnp.float32)


def rows_of(array, index, count):
    return lax.dynamic_slice_in_dim(array, index * count, count, 0)


def dot_nt(lhs, rhs):
    return lax.dot_general(lhs, rhs, (((1,), (1,)), ((), ())), preferred_element_type=jnp.float32)


def dot_tn(lhs, rhs):
    return lax.dot_general(lhs, rhs, (((0,), (0,)), ((), ())), preferred_element_type=jnp.float32)


def dot_nn(lhs, rhs):
    return jnp.dot(lhs, rhs, preferred_element_type=jnp.float32)


def per_device(
    links,
    tokens_in,
    seg_ids,
    routes,
    gate_vals,
    attn_gain,
    w_query,
    w_latent,
    latent_gain,
    w_expand,
    w_output,
    ffn_gain,
    w_shared_in,
    w_shared_out,
    w_expert_in,
    w_expert_out,
    grad_output,
):
    links.calls = 0
    both = ("wide", "narrow")
    low = jnp.bfloat16
    wide_count = lax.axis_size("wide")
    narrow_count = lax.axis_size("narrow")
    wide_at = lax.axis_index("wide")
    narrow_at = lax.axis_index("narrow")
    tok_rows, width = tokens_in.shape
    own_rows = tok_rows // narrow_count
    local_experts = w_expert_in.shape[0]
    hidden_local = w_expert_in.shape[3]
    num_experts = local_experts * wide_count
    head_local = w_query.shape[1] // (DH + DR)
    shared_local = w_shared_out.shape[0] // wide_count

    def mine(array):
        return rows_of(array, narrow_at, own_rows)

    latent_part = rows_of(w_latent.T, narrow_at, w_latent.shape[1] // narrow_count)
    wq_all, wkva_all, wkvb_all, wo_all = links.gather(
        (w_query, "wide", 0), (latent_part, "all", "grid"), (w_expand, "wide", 0), (w_output, "wide", 1)
    )
    grad_all = lax.all_gather(mine(grad_output), both, axis=0, tiled=True)
    shared_in = lax.all_to_all(
        w_shared_in.transpose(1, 2, 0), "wide", split_axis=1, concat_axis=2, tiled=True
    )
    shared_out = lax.all_to_all(w_shared_out, "wide", split_axis=0, concat_axis=1, tiled=True)
    chosen = routes[:, :, None] == jnp.arange(num_experts, dtype=jnp.int32)
    gate_table = jnp.sum(jnp.where(chosen, gate_vals[:, :, None], 0.0), axis=1)
    gates = lax.all_to_all(gate_table, "wide", split_axis=1, concat_axis=0, tiled=True).T

    x_float = tokens_in.astype(jnp.float32)
    x_normed, inv_one = rms_forward(x_float, attn_gain)
    x_low = x_normed.astype(low)
    x_cols = lax.all_to_all(x_low, "wide", split_axis=1, concat_axis=0, tiled=True)
    cos_tab, sin_tab = rotary_tables(positions(seg_ids))
    queries = dot_nn(x_low, wq_all).reshape(tok_rows, head_local, DH + DR).transpose(1, 0, 2)
    q_heads = jnp.concatenate(
        [queries[..., :DH], rotate(queries[..., DH:], cos_tab, sin_tab)], -1
    ).astype(low)
    latent_all = dot_nt(x_low, wkva_all)
    latent = latent_all[:, :KVR]
    latent_normed, inv_lat = rms_forward(latent, latent_gain)
    latent_low = latent_normed.astype(low)
    key_rope = rotate(latent_all[:, KVR:], cos_tab, sin_tab).astype(low)
    expanded = dot_nn(latent_low, wkvb_all).reshape(tok_rows, head_local, 2 * DH).transpose(1, 0, 2)
    key_nope = expanded[..., :DH].astype(low)
    v_heads = expanded[..., DH:].astype(low)
    k_heads = jnp.concatenate(
        [key_nope, jnp.broadcast_to(key_rope[None], (head_local, tok_rows, DR))], -1
    )
    attended, log_total = attention_forward(q_heads, k_heads, v_heads, seg_ids)
    merged = attended.transpose(1, 0, 2).reshape(tok_rows, head_local * DH)
    mixed_part = dot_nn(merged, wo_all).astype(low)
    mixed = links.reduce("narrow", mixed_part)

    x_rows = mine(x_float)
    inv_one_rows = mine(inv_one)
    resid = x_rows + mixed
    resid_normed, inv_two = rms_forward(resid, ffn_gain)
    (hidden,) = links.gather((resid_normed.astype(low), "all", 0))

    expert_rows = local_experts * hidden_local
    w_gate_up = w_expert_in.transpose(0, 2, 3, 1)
    expert_gu = dot_nt(w_gate_up.reshape(2 * expert_rows, width), hidden)
    expert_gu = expert_gu.reshape(local_experts, 2, hidden_local, -1)
    shared_gu = dot_nt(shared_in.reshape(2 * shared_local, width), hidden)
    shared_gu = shared_gu.reshape(2, shared_local, -1)
    down = jnp.concatenate([w_expert_out.reshape(expert_rows, width), shared_out], 0)
    grad_act = dot_nt(down, grad_all)
    grad_act_exp = grad_act[:expert_rows].reshape(local_experts, hidden_local, -1)
    grad_act_exp = grad_act_exp * gates[:, None, :]
    grad_act_sh = grad_act[expert_rows:]

    def both_ways(gate_part, up_part, grad_part):
        sig = jax.nn.sigmoid(gate_part)
        act = gate_part * sig * up_part
        grad_gate = grad_part * up_part * sig * (1.0 + gate_part * (1.0 - sig))
        grad_up = grad_part * gate_part * sig
        return act, grad_gate.astype(low), grad_up.astype(low)

    act_exp, dgate_exp, dup_exp = both_ways(expert_gu[:, 0], expert_gu[:, 1], grad_act_exp)
    act_sh, dgate_sh, dup_sh = both_ways(shared_gu[0], shared_gu[1], grad_act_sh)
    act_exp = (act_exp * gates[:, None, :]).astype(low).reshape(expert_rows, -1)
    act_all = jnp.concatenate([act_exp, act_sh.astype(low)], 0)
    grad_gu_exp = jnp.stack([dgate_exp, dup_exp], 1).reshape(2 * expert_rows, -1)
    grad_gu_sh = jnp.stack([dgate_sh, dup_sh], 0).reshape(2 * shared_local, -1)

    grad_hidden = dot_tn(grad_gu_exp, w_gate_up.reshape(2 * expert_rows, width)) + dot_tn(
        grad_gu_sh, shared_in.reshape(2 * shared_local, width)
    )
    grad_hidden = links.reduce("all", grad_hidden.astype(low))
    out_part = dot_tn(act_all, down)
    out_rows = lax.psum_scatter(out_part.astype(low), both, scatter_dimension=0, tiled=True)
    grad_down = dot_nn(act_all, grad_all)
    grad_exp_out = grad_down[:expert_rows].reshape(local_experts, hidden_local, width)
    red_shout = lax.all_to_all(
        grad_down[expert_rows:].astype(low), "wide", split_axis=1, concat_axis=0, tiled=True
    ).astype(jnp.float32)
    grad_exp_in = dot_nn(grad_gu_exp, hidden).reshape(local_experts, 2, hidden_local, width)
    grad_exp_in = grad_exp_in.transpose(0, 3, 1, 2)
    grad_shin = dot_nn(grad_gu_sh, hidden).reshape(2, shared_local, width).astype(low)
    red_shin = lax.all_to_all(grad_shin, "wide", split_axis=2, concat_axis=1, tiled=True)
    red_shin = red_shin.astype(jnp.float32).transpose(2, 0, 1)

    out_rows = (resid + out_rows.astype(jnp.float32)).astype(low)
    layer_out = lax.all_to_all(out_rows, "narrow", split_axis=1, concat_axis=0, tiled=True)

    grad_resid, grad_ffn = rms_backward(resid, inv_two, ffn_gain, grad_hidden)
    grad_resid = grad_resid + mine(grad_output).astype(jnp.float32)
    (grad_low,) = links.gather((grad_resid.astype(low), "narrow", 0))
    grad_merged = dot_nt(grad_low, wo_all)
    grad_wo = dot_tn(merged, grad_low).astype(low)
    red_wo = lax.psum_scatter(grad_wo, "wide", scatter_dimension=1, tiled=True)
    grad_att = grad_merged.reshape(tok_rows, head_local, DH).transpose(1, 0, 2).astype(low)
    grad_q, grad_k, grad_v = attention_backward(
        q_heads, k_heads, v_heads, grad_att, log_total, seg_ids
    )
    grad_q_pre = jnp.concatenate(
        [grad_q[..., :DH], unrotate(grad_q[..., DH:], cos_tab, sin_tab)], -1
    ).astype(low)
    grad_q_pre = grad_q_pre.transpose(1, 0, 2).reshape(tok_rows, head_local * (DH + DR))
    grad_rope_part = jnp.sum(grad_k[..., DH:], axis=0)
    grad_expanded = jnp.concatenate([grad_k[..., :DH], grad_v], -1).astype(low)
    grad_expanded = grad_expanded.transpose(1, 0, 2).reshape(tok_rows, head_local * 2 * DH)
    grad_latent_part = dot_nt(grad_expanded, wkvb_all)
    grad_x_part = dot_nt(grad_q_pre, wq_all)
    terms = jnp.concatenate([grad_x_part, grad_latent_part, grad_rope_part], 1)
    terms = links.reduce("narrow", terms.astype(low))
    grad_x_query, latent_terms = terms[:, :width], terms[:, width:]
    grad_wkvb = dot_tn(latent_low, grad_expanded).astype(low)
    red_wkvb = lax.psum_scatter(grad_wkvb, "wide", scatter_dimension=0, tiled=True)
    grad_latent, grad_lat_gain = rms_backward(
        mine(latent), mine(inv_lat), latent_gain, latent_terms[:, :KVR]
    )
    grad_rope = unrotate(latent_terms[:, KVR:], mine(cos_tab), mine(sin_tab))
    grad_latent_all = jnp.concatenate([grad_latent, grad_rope], -1).astype(low)
    grad_x_normed = grad_x_query + dot_nn(grad_latent_all, wkva_all)
    grad_x, grad_att_gain = rms_backward(x_rows, inv_one_rows, attn_gain, grad_x_normed)
    grad_tokens = (grad_x + grad_resid).astype(low)
    q_pre_all, latent_rows, grad_tokens = links.gather(
        (grad_q_pre, "wide", 0), (grad_latent_all, "all", 0), (grad_tokens, "narrow", 0)
    )
    grad_tokens = grad_tokens.astype(jnp.float32)
    red_wkva = dot_tn(x_cols, latent_rows)
    red_wq = dot_tn(x_cols, q_pre_all)
    gains = jnp.concatenate(
        [part.reshape(wide_count, -1) for part in (grad_att_gain, grad_ffn, grad_lat_gain)], 1
    )
    gains = lax.dynamic_index_in_dim(lax.psum(gains, both), wide_at, 0, keepdims=False)
    part = width // wide_count
    red_att_gain, red_ffn, red_lat_gain = gains[:part], gains[part : 2 * part], gains[2 * part :]
    return (
        layer_out,
        grad_tokens,
        red_att_gain,
        red_wq,
        red_wkva,
        red_lat_gain,
        red_wkvb.astype(jnp.float32),
        red_wo.astype(jnp.float32),
        red_ffn,
        red_shin,
        red_shout,
        grad_exp_in,
        grad_exp_out,
    )


def solution(mesh):
    placed = (
        P("wide", None),
        P("wide"),
        P("wide", None),
        P("wide", None),
        P(),
        P("wide", "narrow"),
        P("wide", None),
        P(),
        P("wide", "narrow"),
        P("narrow", "wide"),
        P(),
        P("wide", None, "narrow"),
        P("narrow", "wide"),
        P("wide", None, None, "narrow"),
        P("wide", "narrow", None),
        P("wide", None),
    )
    return jax.shard_map(
        functools.partial(per_device, Links(mesh)),
        mesh=mesh,
        in_specs=placed,
        out_specs=(
            P("wide", "narrow"),
            P("wide", None),
            P("wide"),
            P("wide", "narrow"),
            P("wide", None),
            P("wide"),
            P("wide", "narrow"),
            P("narrow", "wide"),
            P("wide"),
            P("wide", None, "narrow"),
            P("narrow", "wide"),
            P("wide", None, None, "narrow"),
            P("wide", "narrow", None),
        ),
        check_vma=False,
    )
```

time: 2240 us -> 694 us (0.31)
  waiting for transfers between devices: 1830 us -> 34.7 us
  Pallas kernels: 0 us -> 319 us
  local copies, waits for them, and re-layouts: 123 us -> 38.9 us
    reduce_scatter x9 -> x2, waiting for transfers between devices: 784 us -> 29.4 us  [the longest x1 29.4 us: per_device(): lax.psum_scatter(out_part.astype(low), both, scatter_dimension=0, tiled=T...]
    all_to_all x4 -> x7, waiting for transfers between devices: 479 us -> 5.28 us  [the longest x1 5.26 us: per_device(): lax.all_to_all(grad_shin, 'wide', split_axis=2, concat_axis=1, tiled=True)]
    all_gather x7 -> x1, waiting for transfers between devices: 427 us -> 0.01 us  [per_device(): grad_all = lax.all_gather(mine(grad_output), both, axis=0, tiled=True)]
    pallas_call x0 -> x7, Pallas kernels: none -> 319 us  [the longest x4 233 us: gather(): pl.pallas_call(functools.partial(gather_kernel, line, kinds, views), out_...]
    reduce_scatter x1, waiting for transfers between devices: 69.6 us -> 0.01 us  [per_device(): lax.psum_scatter(grad_wkvb, 'wide', scatter_dimension=0, tiled=True)]
    psum x2 -> x0, waiting for transfers between devices: 62.4 us -> none  [the longest x1 39.1 us: per_device(): mixed_full = lax.psum(mixed_part, 'narrow')]
    gather x4 -> x0, local copies, waits for them, and re-layouts: 55.4 us -> none  [the longest x1 19.7 us: per_device(): padded[slot_tokens].reshape(wide_count, local_experts, capacity, width)]
    psum x0 -> x1, blocking collectives: none -> 37 us  [per_device(): lax.psum(gains, both)]
  transfers between devices with their start and end apart: 23 -> 11, of which waited for: 20 -> 2; matrix products, arithmetic and copies ran while one was open for 10% -> 30% of each run, Pallas kernels for 0% -> 47%
where the time goes in v1:
time: 694 us; the launch traced here: 682 us
  Pallas kernels  319 us (46%)
  matrix products  151 us (22%)
  other arithmetic  45.5 us (7%)
  starting transfers between devices  41.5 us (6%)
  local copies, waits for them, and re-layouts  38.9 us (6%)
  blocking collectives  37 us (5%)
  waiting for transfers between devices  34.7 us (5%)
  between operations  15.1 us (2%)
    pallas_call x4, Pallas kernels, gather(): pl.pallas_call(functools.partial(gather_kernel, line, kinds, views), out_...  233 us
    pallas_call x3, Pallas kernels, reduce_blocks(): pl.pallas_call(functools.partial(reduce_kernel, line, kind, rows), out_sh...  85.4 us
    dot_general x7, matrix products, dot_tn(): lax.dot_general(lhs, rhs, (((0,), (0,)), ((), ())), preferred_element_typ...  54.4 us
    dot_general x7, matrix products, dot_nt(): lax.dot_general(lhs, rhs, (((1,), (1,)), ((), ())), preferred_element_typ...  44.1 us
    dot_general x7, matrix products, dot_nn(): return jnp.dot(lhs, rhs, preferred_element_type=jnp.float32)  43.5 us
    psum x1, blocking collectives, per_device(): lax.psum(gains, both)  37 us
    reduce_scatter x1, waiting for transfers between devices, per_device(): lax.psum_scatter(out_part.astype(low), both, scatter_dimension=0, tiled=T...  29.4 us
  transfers between devices with their start and end apart: 11, of which 2 were waited for; matrix products, arithmetic and copies ran while one was open for 30% of the time, Pallas kernels for 47%

profile of v1, /device:TPU:31, one launch (start us, length us, event | category | flops | bytes accessed | tf_op | source)
XLA Modules:
  0.0 682.3 jit_solution(17841251431978940648)
XLA Ops:
  9.0 5.4 all-to-all-start.2
  15.8 2.7 copy.180
  20.8 108.7 %gather_blocks.4 = (bf16[2048,768]{1,0:T(8,128)(2,1)}, bf16[576,2048]{1,0:T(8,128)(2,1)}, bf16[512,1024]{1,0:T(8,128)(2,1)}, bf16[512,2048]{1,0:T(8,128)(2,1)}) custom-call(bf16[256,768]{1,0:T(8,128)(2,1)} %refs_0_.1, bf16[144,256]{1,0:T(8,128)(2,1)} %dynamic-slice_bitcast_fusion.refs_1_, bf16[64,1024]{1,0:T(8,128)(2,1)} %refs_2_.1, bf16[512,256]{1,0:T(8,128)(2,1)} %refs_3_.1), custom_call_target="tpu_custom_call" | custom-call | bytes 7790592 | tf_op jit(solution)/shard_map/gather_blocks/pallas_call | solution.py:394
  130.1 3.7 fusion.68
  143.5 10.5 %sum_blocks.3 = f32[64,2048]{1,0:T(8,128)} custom-call(bf16[256,2048]{1,0:T(8,128)(2,1)} %convolution_convert_fusion.2.part), custom_call_target="tpu_custom_call" | custom-call | flops 524288 | bytes 2097152 | tf_op jit(solution)/shard_map/sum_blocks/pallas_call | solution.py:570
  156.2 41.5 %gather_blocks.5 = bf16[2048,2048]{1,0:T(8,128)(2,1)} custom-call(bf16[64,2048]{1,0:T(8,128)(2,1)} %multiply_convert_fusion.6.refs_0_), custom_call_target="tpu_custom_call" | custom-call | bytes 8126464 | tf_op jit(solution)/shard_map/gather_blocks/pallas_call | solution.py:394
  197.7 5.7 all-to-all-start.1
  203.5 18.8 %fusion.70 = f32[2048,1408]{0,1:T(8,128)} fusion(bf16[2048,2048]{1,0:T(8,128)(2,1)} %gather_blocks.5, bf16[1408,2048]{1,0:T(8,128)(2,1)} %bitcast.218), kind=kOutput, calls=%fused_computation.159 | convolution fusion | flops 11811160064 | bytes 25690112 | tf_op jit(solution)/shard_map/dot_general | solution.py:630
  223.7 5.4 all-to-all-start
  231.6 7.5 %convolution_bitcast_fusion = f32[176,2048]{1,0:T(8,128)} fusion(bf16[2048,2048]{1,0:T(8,128)(2,1)} %gather_blocks.5, bf16[176,2048]{1,0:T(8,128)(2,1)S(1)} %bitcast.191), kind=kOutput, calls=%fused_computation.28 | convolution fusion | flops 1476395008 | bytes 10551296 | tf_op jit(solution)/shard_map/dot_general | solution.py:630
  239.0 10.7 %fusion.18 = f32[792,2048]{1,0:T(8,128)S(1)} fusion(bf16[2048,2048]{1,0:T(8,128)(2,1)} %all-gather.2.cloned.1.call-done, bf16[88,2048]{1,0:T(8,128)(2,1)S(1)} %bitcast.210, bf16[704,2048]{1,0:T(8,128)(2,1)} %bitcast.219), kind=kOutput, calls=%fused_computation.34 | convolution fusion | flops 6650265600 | bytes 18120704 | tf_op jit(solution)/shard_map/dot_general | solution.py:630
  251.1 3.2 slice.176
  254.3 9.5 %multiply_convert_fusion.1 = (bf16[2,1,352,2048]{3,2,1,0:T(8,128)(2,1)}, bf16[2,1,352,2048]{3,2,1,0:T(8,128)(2,1)}, f32[2,1,352,2048]{3,2,1,0:T(8,128)S(1)}, f32[2,1,352,2048]{3,2,1,0:T(8,128)S(1)}) fusion(f32[2,1,352,2048]{3,2,1,0:T(8,128)} %bitcast.180, f32[2,2048]{1,0:T(2,128)S(1)} %bitcast.214, f32[2,2,352,2048]{3,2,1,0:T(8,128)} %bitcast.181), kind=kLoop, calls=%fused_computation.20 | loop fusion | flops 20185088 | bytes 34619392 | tf_op jit(solution)/shard_map/convert_element_type | solution.py:739
  263.9 2.6 fusion.6
  268.1 11.3 %convolution_convert_fusion = bf16[2048,2048]{1,0:T(8,128)(2,1)} fusion(bf16[88,2048]{1,0:T(8,128)(2,1)S(1)} %bitcast.211, bf16[704,2048]{1,0:T(8,128)(2,1)S(1)} %bitcast.220, bf16[88,2048]{1,0:T(8,128)(2,1)S(1)} %copy-done.25, bf16[704,2048]{1,0:T(8,128)(2,1)S(1)} %fusion.6), kind=kOutput, calls=%fused_computation.7 | convolution fusion | flops 6660947968 | bytes 14876672 | tf_op jit(solution)/shard_map/dot_general | solution.py:634
  279.4 2.3 copy.179
  282.9 6.0 fusion.15
  288.9 3.6 copy.155
  292.5 10.3 %fusion.19 = f32[792,2048]{1,0:T(8,128)S(1)} fusion(bf16[2048,2048]{1,0:T(8,128)(2,1)} %all-gather.2.cloned.1.call-done, bf16[88,2048]{1,0:T(8,128)(2,1)} %get-tuple-element.104, bf16[704,2048]{1,0:T(8,128)(2,1)} %copy-done.14), kind=kOutput, calls=%fused_computation.35 | convolution fusion | flops 6650265600 | bytes 18120704 | tf_op jit(solution)/shard_map/dot_general | solution.py:638
  302.8 2.7 copy-done.4
  306.2 5.4 all-to-all-start.6
  312.8 20.5 %fusion.10 = f32[2048,2048,1,1]{1,0,3,2:T(8,128)} fusion(bf16[2,2048,2,352]{1,3,2,0:T(8,128)(2,1)} %param.29, bf16[2,1,352,2048]{3,2,1,0:T(8,128)(2,1)} %get-tuple-element.99, bf16[2,1,352,2048]{3,2,1,0:T(8,128)(2,1)} %get-tuple-element.98), kind=kOutput, calls=%fused_computation.17 | convolution fusion | flops 11814043648 | bytes 28311552 | tf_op jit(solution)/shard_map/dot_general | solution.py:634
  333.3 11.7 %fusion.1.part = bf16[2048,2048]{1,0:T(8,128)(2,1)} fusion(f32[2048,2048,1,1]{1,0,3,2:T(8,128)} %fusion.10, bf16[176,2048]{1,0:T(8,128)(2,1)S(1)} %bitcast.193, bf16[176,2048]{1,0:T(8,128)(2,1)S(1)} %bitcast.192), kind=kOutput, calls=%fused_computation.2 | convolution fusion | flops 1484783616 | bytes 26607616 | tf_op jit(solution)/shard_map/dot_general | solution.py:634
  345.0 61.2 %sum_blocks.4 = f32[64,2048]{1,0:T(8,128)} custom-call(bf16[2048,2048]{1,0:T(8,128)(2,1)} %fusion.1.part), custom_call_target="tpu_custom_call" | custom-call | flops 4194304 | bytes 16777216 | tf_op jit(solution)/shard_map/sum_blocks/pallas_call | solution.py:570
  407.5 29.4 %reduce-scatter.4.cloned.1.call-done = bf16[64,2048]{1,0:T(8,128)(2,1)} async-done(((bf16[2048,2048]{1,0:T(8,128)(2,1)}), bf16[64,2048]{1,0:T(8,128)(2,1)}) %reduce-scatter.4.cloned.1.call-update) | async-done | bytes 262160 | tf_op jit(solution)/shard_map/reduce_scatter | solution.py:753
  436.9 2.4 fusion.64
  439.3 7.9 %gather_blocks.6 = bf16[256,2048]{1,0:T(8,128)(2,1)} custom-call(bf16[64,2048]{1,0:T(8,128)(2,1)} %get-tuple-element.94.refs_0_), custom_call_target="tpu_custom_call" | custom-call | bytes 786432 | tf_op jit(solution)/shard_map/gather_blocks/pallas_call | solution.py:394
  447.2 2.7 convolution_convert_fusion.9
  451.4 2.2 fusion.25
  455.6 7.6 %all-to-all-start.5 = ((bf16[2,88,2048]{1,0,2:T(2,128)(2,1)}), bf16[2,88,2048]{1,0,2:T(2,128)(2,1)S(1)}, u32[]{:S(2)}, u32[]{:S(2)}) async-start(bf16[2,88,2048]{1,0,2:T(2,128)(2,1)} %copy.155), calls=%async_computation.8 | async-start | bytes 2097152 | tf_op jit(solution)/shard_map/all_to_all | solution.py:762
  463.1 18.9 %fusion.12 = f32[2,2048,2,352]{1,3,2,0:T(8,128)} fusion(bf16[2048,2048]{1,0:T(8,128)(2,1)} %gather_blocks.5, bf16[2,1,352,2048]{3,2,1,0:T(8,128)(2,1)} %get-tuple-element.99, bf16[2,1,352,2048]{3,2,1,0:T(8,128)(2,1)} %get-tuple-element.98), kind=kOutput, calls=%fused_computation.22 | convolution fusion | flops 11814043648 | bytes 25690112 | tf_op jit(solution)/shard_map/dot_general | solution.py:638
  482.0 6.0 slice.184
  488.0 1.9 convert_element_type.180
  489.9 5.3 all-to-all-done.5
  495.2 5.7 all-to-all-start.4
  501.1 2.0 convert_bitcast_fusion
  503.1 2.2 copy.156
  507.0 3.2 fusion.26
  512.3 2.0 convolution_convert_fusion.1
  516.9 2.9 convolution_convert_fusion.3
  521.1 13.7 %sum_blocks.5 = f32[64,2624]{1,0:T(8,128)} custom-call(bf16[256,2624]{1,0:T(8,128)(2,1)} %pad_maximum_fusion.9.part), custom_call_target="tpu_custom_call" | custom-call | flops 671744 | bytes 2686976 | tf_op jit(solution)/shard_map/sum_blocks/pallas_call | solution.py:570
  538.0 2.5 multiply_reduce_fusion.3
  541.5 75.3 %gather_blocks.7 = (bf16[2048,768]{1,0:T(8,128)(2,1)}, bf16[2048,576]{1,0:T(8,128)(2,1)}, bf16[256,2048]{1,0:T(8,128)(2,1)}) custom-call(bf16[256,768]{1,0:T(8,128)(2,1)} %copy.153.refs_0_, bf16[64,576]{1,0:T(8,128)(2,1)} %copy-done.22, bf16[64,2048]{1,0:T(8,128)(2,1)} %add_convert_fusion.refs_2_), custom_call_target="tpu_custom_call" | custom-call | bytes 5824512 | tf_op jit(solution)/shard_map/gather_blocks/pallas_call | solution.py:394
  616.8 2.9 convert_element_type.167
  619.8 37.0 %psum.7 = f32[8,576]{1,0:T(8,128)S(1)} all-reduce(f32[8,576]{1,0:T(8,128)S(1)} %pad_maximum_fusion.21), channel_id=1, replica_groups=mesh['wide'=8,'narrow'=4] {'wide','narrow'}, use_global_device_ids=true, to_apply=%region_17.18 | all-reduce | flops 4608 | bytes 36864 | tf_op jit(solution)/shard_map/psum | solution.py:809
  656.8 5.9 all-to-all-start.3
  662.6 3.2 fusion.72
  665.8 4.1 fusion.71
  (199 shorter events, 49.4 us)
Async XLA Ops:
  7.2 12.9 %copy-start = (bf16[256,576]{0,1:T(8,128)(2,1)S(1)}, bf16[256,576]{0,1:T(8,128)(2,1)}, u32[]{:S(2)}) copy-start(bf16[256,576]{0,1:T(8,128)(2,1)} %param.22) | copy-start | bytes 884740
  7.2 11.4 %copy-start.2 = (bf16[256,2048]{1,0:T(8,128)(2,1)S(1)}, bf16[256,2048]{1,0:T(8,128)(2,1)}, u32[]{:S(2)}) copy-start(bf16[256,2048]{1,0:T(8,128)(2,1)} %param.16) | copy-start | bytes 3145732
  7.2 231.8 %all-gather.2.cloned.1.call-start = ((), (), s32[]{:S(2)}) async-start(), calls=%async_computation.11 | async-start | bytes 8650752 | tf_op jit(solution)/shard_map/all_gather | solution.py:682
  9.0 188.7 %all-to-all-start.2 = ((bf16[8,88,256]{2,1,0:T(8,128)(2,1)}), bf16[8,88,256]{2,1,0:T(8,128)(2,1)S(1)}, u32[]{:S(2)}, u32[]{:S(2)}) async-start(bf16[8,88,256]{2,1,0:T(8,128)(2,1)} %bitcast.209), calls=%async_computation.2 | async-start | bytes 720896 | tf_op jit(solution)/shard_map/all_to_all | solution.py:686
  15.8 114.0 %copy-start.38 = (f32[2048]{0:T(1024)S(1)}, f32[2048]{0:T(1024)}, u32[]{:S(2)}) copy-start(f32[2048]{0:T(1024)} %param.20) | copy-start | bytes 24580
  130.1 5.8 copy-start.11
  130.1 4.7 copy-start.15
  136.5 4.7 copy-start.23
  136.5 4.7 copy-start.24
  136.8 4.4 copy-start.30
  136.8 4.4 copy-start.32
  138.4 5.0 copy-start.34
  141.7 13.7 %copy-start.16 = (bf16[4,256,128]{1,2,0:T(8,128)(2,1)}, bf16[4,256,128]{1,2,0:T(8,128)(2,1)S(1)}, u32[]{:S(2)}) copy-start(bf16[4,256,128]{1,2,0:T(8,128)(2,1)S(1)} %convolution_convert_fusion.6) | copy-start | bytes 786436
  141.7 13.7 %copy-start.37 = (f32[2048]{0:T(1024)S(1)}, f32[2048]{0:T(1024)}, u32[]{:S(2)}) copy-start(f32[2048]{0:T(1024)} %param.26) | copy-start | bytes 24580
  197.7 26.0 %all-to-all-start.1 = ((bf16[2,704,256]{2,0,1:T(2,128)(2,1)}), bf16[2,704,256]{2,0,1:T(2,128)(2,1)}, u32[]{:S(2)}, u32[]{:S(2)}) async-start(bf16[2,704,256]{2,0,1:T(2,128)(2,1)} %bitcast.194), calls=%async_computation.1 | async-start | bytes 1441792 | tf_op jit(solution)/shard_map/all_to_all | solution.py:683
  203.5 18.9 %copy-start.44 = (f32[256,6]{0,1:T(8,128)S(1)}, f32[256,6]{0,1:T(8,128)}, u32[]{:S(2)}) copy-start(f32[256,6]{0,1:T(8,128)} %param.19) | copy-start | bytes 18436
  203.5 18.8 %copy-start.45 = (s32[256,6]{0,1:T(8,128)S(1)}, s32[256,6]{0,1:T(8,128)}, u32[]{:S(2)}) copy-start(s32[256,6]{0,1:T(8,128)} %param.18) | copy-start | bytes 18436
  223.7 30.6 %all-to-all-start = ((f32[256,8,2]{0,2,1:T(2,128)}), f32[256,8,2]{0,2,1:T(2,128)S(1)}, u32[]{:S(2)}, u32[]{:S(2)}) async-start(f32[256,8,2]{0,2,1:T(2,128)} %all_to_all.84), calls=%async_computation | async-start | bytes 32768 | tf_op jit(solution)/shard_map/all_to_all | solution.py:689
  229.2 207.7 %reduce-scatter.4.cloned.1.call-start = ((), (), s32[]{:S(2)}) async-start(), calls=%async_computation.10 | async-start | bytes 8650752 | tf_op jit(solution)/shard_map/reduce_scatter | solution.py:753
  231.6 7.5 %copy-start.26 = (bf16[8,11,8,256]{3,2,0,1:T(8,128)(2,1)S(1)}, bf16[8,11,8,256]{3,2,0,1:T(8,128)(2,1)}, u32[]{:S(2)}) copy-start(bf16[8,11,8,256]{3,2,0,1:T(8,128)(2,1)} %copy.173) | copy-start | bytes 1081348
  239.0 10.7 %copy-start.20 = (f32[176,2048]{1,0:T(8,128)S(1)}, f32[176,2048]{1,0:T(8,128)}, u32[]{:S(2)}) copy-start(f32[176,2048]{1,0:T(8,128)} %convolution_bitcast_fusion) | copy-start | bytes 4325380
  263.9 4.2 copy-start.25
  263.9 4.2 copy-start.27
  263.9 4.2 copy-start.49
  306.2 149.3 %all-to-all-start.6 = ((bf16[88,8,256]{2,0,1:T(8,128)(2,1)}), bf16[88,8,256]{2,0,1:T(8,128)(2,1)}, u32[]{:S(2)}, u32[]{:S(2)}) async-start(bf16[88,8,256]{2,0,1:T(8,128)(2,1)} %bitcast.204), calls=%async_computation.9 | async-start | bytes 720896 | tf_op jit(solution)/shard_map/all_to_all | solution.py:756
  311.7 359.5 %reduce-scatter.6.cloned.1.call-start = ((), (), s32[]{:S(2)}) async-start(), calls=%async_computation.12 | async-start | bytes 1179648 | tf_op jit(solution)/shard_map/reduce_scatter | solution.py:791
  312.7 20.5 %copy-start.13 = (bf16[22,8,8,256]{3,1,2,0:T(8,128)(2,1)S(1)}, bf16[22,8,8,256]{3,1,2,0:T(8,128)(2,1)}, u32[]{:S(2)}) copy-start(bf16[22,8,8,256]{3,1,2,0:T(8,128)(2,1)} %copy-done.12) | copy-start | bytes 2162692
  439.3 12.1 %copy-start.35 = (bf16[4,256,128]{1,2,0:T(8,128)(2,1)S(1)}, bf16[4,256,128]{1,2,0:T(8,128)(2,1)}, u32[]{:S(2)}) copy-start(bf16[4,256,128]{1,2,0:T(8,128)(2,1)} %slice.249) | copy-start | bytes 786436
  439.3 12.1 %copy-start.41 = (bf16[4,256,32]{1,2,0:T(8,128)(2,1)S(1)}, bf16[4,256,32]{1,2,0:T(8,128)(2,1)}, u32[]{:S(2)}) copy-start(bf16[4,256,32]{1,2,0:T(8,128)(2,1)} %copy-done.40) | copy-start | bytes 196612
  454.0 28.1 %copy-start.5 = (bf16[4,256,256]{1,2,0:T(8,128)(2,1)}, bf16[4,256,256]{1,2,0:T(8,128)(2,1)S(1)}, u32[]{:S(2)}) copy-start(bf16[4,256,256]{1,2,0:T(8,128)(2,1)S(1)} %pad_maximum_fusion.11) | copy-start | bytes 1572868
  455.6 39.6 %all-to-all-start.5 = ((bf16[2,88,2048]{1,0,2:T(2,128)(2,1)}), bf16[2,88,2048]{1,0,2:T(2,128)(2,1)S(1)}, u32[]{:S(2)}, u32[]{:S(2)}) async-start(bf16[2,88,2048]{1,0,2:T(2,128)(2,1)} %copy.155), calls=%async_computation.8 | async-start | bytes 2097152 | tf_op jit(solution)/shard_map/all_to_all | solution.py:762
  495.2 5.9 copy-start.7
  495.2 161.6 %all-to-all-start.4 = ((bf16[256,8,256]{2,0,1:T(8,128)(2,1)}), bf16[256,8,256]{2,0,1:T(8,128)(2,1)}, u32[]{:S(2)}, u32[]{:S(2)}) async-start(bf16[256,8,256]{2,0,1:T(8,128)(2,1)} %bitcast.186), calls=%async_computation.5 | async-start | bytes 2097152 | tf_op jit(solution)/shard_map/all_to_all | solution.py:694
  500.8 172.0 %reduce-scatter.8.cloned.1.call-start = ((), (), s32[]{:S(2)}) async-start(), calls=%async_computation.13 | async-start | bytes 2359296 | tf_op jit(solution)/shard_map/reduce_scatter | solution.py:773
  503.1 8.2 %copy-start.31 = (f32[256,32]{0,1:T(8,128)S(1)}, f32[256,32]{0,1:T(8,128)}, u32[]{:S(2)}) copy-start(f32[256,32]{0,1:T(8,128)} %copy-done.30) | copy-start | bytes 98308
  503.1 8.2 %copy-start.33 = (f32[256,32]{0,1:T(8,128)S(1)}, f32[256,32]{0,1:T(8,128)}, u32[]{:S(2)}) copy-start(f32[256,32]{0,1:T(8,128)} %copy-done.32) | copy-start | bytes 98308
  503.1 9.2 %copy-start.17 = (bf16[4,256,128]{1,2,0:T(8,128)(2,1)S(1)}, bf16[4,256,128]{1,2,0:T(8,128)(2,1)}, u32[]{:S(2)}) copy-start(bf16[4,256,128]{1,2,0:T(8,128)(2,1)} %copy-done.16) | copy-start | bytes 786436
  505.3 7.0 %copy-start.10 = (bf16[256,2048]{1,0:T(8,128)(2,1)S(1)}, bf16[256,2048]{1,0:T(8,128)(2,1)}, u32[]{:S(2)}) copy-start(bf16[256,2048]{1,0:T(8,128)(2,1)} %gather_blocks.6) | copy-start | bytes 3145732
  519.9 14.9 %copy-start.21 = (f32[256,512]{1,0:T(8,128)S(1)}, f32[256,512]{1,0:T(8,128)}, u32[]{:S(2)}) copy-start(f32[256,512]{1,0:T(8,128)} %get-tuple-element.113) | copy-start | bytes 1572868
  519.9 17.0 %copy-start.48 = (f32[64]{0:T(128)S(1)}, f32[64]{0:T(128)}, u32[]{:S(2)}) copy-start(f32[64]{0:T(128)} %get-tuple-element.92) | copy-start | bytes 772
  519.9 18.1 %copy-start.3 = (f32[256,2048]{1,0:T(8,128)S(1)}, f32[256,2048]{1,0:T(8,128)}, u32[]{:S(2)}) copy-start(f32[256,2048]{1,0:T(8,128)} %convert_element_type.141) | copy-start | bytes 6291460
  519.9 18.1 %copy-start.39 = (f32[2048]{0:T(1024)S(1)}, f32[2048]{0:T(1024)}, u32[]{:S(2)}) copy-start(f32[2048]{0:T(1024)} %param.20) | copy-start | bytes 24580
  519.9 18.1 %copy-start.46 = (f32[64]{0:T(128)S(1)}, f32[64]{0:T(128)}, u32[]{:S(2)}) copy-start(f32[64]{0:T(128)} %get-tuple-element.91) | copy-start | bytes 772
  521.1 19.5 %copy-start.19 = (f32[64,2048]{1,0:T(8,128)S(1)}, f32[64,2048]{1,0:T(8,128)}, u32[]{:S(2)}) copy-start(f32[64,2048]{1,0:T(8,128)} %get-tuple-element.95) | copy-start | bytes 1572868
  521.1 19.5 %copy-start.47 = (f32[64]{0:T(128)S(1)}, f32[64]{0:T(128)}, u32[]{:S(2)}) copy-start(f32[64]{0:T(128)} %get-tuple-element.90) | copy-start | bytes 772
  616.8 45.8 %copy-start.50 = (bf16[2048,576]{1,0:T(8,128)(2,1)S(1)}, bf16[2048,576]{1,0:T(8,128)(2,1)}, u32[]{:S(2)}) copy-start(bf16[2048,576]{1,0:T(8,128)(2,1)} %get-tuple-element.83) | copy-start | bytes 7077892
  656.8 14.4 %all-to-all-start.3 = ((bf16[64,4,512]{2,0,1:T(8,128)(2,1)}), bf16[64,4,512]{2,0,1:T(8,128)(2,1)S(1)}, u32[]{:S(2)}, u32[]{:S(2)}) async-start(bf16[64,4,512]{2,0,1:T(8,128)(2,1)} %bitcast.179), calls=%async_computation.4 | async-start | bytes 524288 | tf_op jit(solution)/shard_map/all_to_all | solution.py:766
  665.8 9.5 %copy-start.1 = (bf16[256,576]{0,1:T(8,128)(2,1)S(1)}, bf16[256,576]{0,1:T(8,128)(2,1)}, u32[]{:S(2)}) copy-start(bf16[256,576]{0,1:T(8,128)(2,1)} %param.22) | copy-start | bytes 884740
  (14 other events, 40.5 us)
Sparse Core Ops, SparseCore 0:
  11.4 106.6 all-gather.1
  279.5 157.3 reduce-scatter.3
  455.7 76.0 reduce-scatter.5
  535.1 81.5 reduce-scatter.7

commit v2 on v0

v2 whole, which is shorter than its diff:
```python
import functools

import jax
import jax.numpy as jnp
from jax import lax
from jax.experimental import pallas as pl
from jax.experimental.pallas import tpu as pltpu
from jax.sharding import PartitionSpec as P

DH = 128
DR = 64
KVR = 512


EPS = 1e-06
THETA = 50000.0
NEG_BIG = -1e30
BLOCK_ROWS = 512


def positions(seg_ids):
    row_index = jnp.arange(seg_ids.shape[0], dtype=jnp.int32)
    starts = jnp.concatenate([jnp.ones((1,), dtype=bool), seg_ids[1:] != seg_ids[:-1]])
    begins = lax.cummax(jnp.where(starts, row_index, 0), axis=0)
    return (row_index - begins).astype(jnp.float32)


def rotary_tables(pos_float):
    half_dim = DR // 2
    inv_freq = THETA ** (-(jnp.arange(half_dim, dtype=jnp.float32) * 2.0 / DR))
    angles = pos_float[:, None] * inv_freq[None, :]
    return (jnp.cos(angles), jnp.sin(angles))


def rotate(values, cos_tab, sin_tab):
    half_dim = values.shape[-1] // 2
    lower_half = values[..., :half_dim]
    upper_half = values[..., half_dim:]
    return jnp.concatenate(
        [lower_half * cos_tab - upper_half * sin_tab, upper_half * cos_tab + lower_half * sin_tab],
        -1,
    )


def unrotate(values, cos_tab, sin_tab):
    half_dim = values.shape[-1] // 2
    lower_half = values[..., :half_dim]
    upper_half = values[..., half_dim:]
    return jnp.concatenate(
        [lower_half * cos_tab + upper_half * sin_tab, upper_half * cos_tab - lower_half * sin_tab],
        -1,
    )


def rms_forward(values, gain_vec):
    inv_rms = lax.rsqrt(jnp.mean(values * values, axis=-1, keepdims=True) + EPS)
    return (values * inv_rms * gain_vec, inv_rms)


def rms_backward(values, inv_rms, gain_vec, grad_out):
    scaled = grad_out * gain_vec
    grad_in = inv_rms * scaled - values * inv_rms**3 * jnp.mean(
        values * scaled, axis=-1, keepdims=True
    )
    grad_gain = jnp.sum(grad_out * values * inv_rms, axis=0)
    return (grad_in, grad_gain)


def masked_scores(q_blk, k_heads, seg_rows, seg_cols, row_pos, col_pos):
    scale = (DH + DR) ** (-0.5)
    scores = jnp.einsum("hqc,hkc->hqk", q_blk, k_heads, preferred_element_type=jnp.float32) * scale
    allowed = (seg_rows[:, None] == seg_cols[None, :]) & (col_pos[None, :] <= row_pos[:, None])
    return jnp.where(allowed[None], scores, NEG_BIG)


def attention_forward(q_heads, k_heads, v_heads, seg_ids):
    head_count = q_heads.shape[0]
    row_total = q_heads.shape[1]
    block_rows = min(row_total, BLOCK_ROWS)
    block_count = row_total // block_rows
    col_pos = jnp.arange(row_total, dtype=jnp.int32)

    def one_block(start):
        row_pos = start + jnp.arange(block_rows, dtype=jnp.int32)
        scores = masked_scores(q_heads, k_heads, seg_ids, seg_ids, row_pos, col_pos)
        top_score = jnp.max(scores, axis=-1, keepdims=True)
        log_total = top_score + jnp.log(
            jnp.sum(jnp.exp(scores - top_score), axis=-1, keepdims=True)
        )
        prob_low = jnp.exp(scores - log_total).astype(jnp.bfloat16)
        attended = jnp.einsum("hqk,hkd->hqd", prob_low, v_heads, preferred_element_type=jnp.float32)
        return (attended.astype(jnp.bfloat16), log_total)

    starts = jnp.arange(block_count, dtype=jnp.int32) * block_rows
    attended, log_total = lax.map(one_block, starts)
    attended = attended.transpose(1, 0, 2, 3).reshape(head_count, row_total, -1)
    log_total = log_total.transpose(1, 0, 2, 3).reshape(head_count, row_total, 1)
    return (attended, log_total)


def attention_backward(q_heads, k_heads, v_heads, grad_att, log_total, seg_ids):
    scale = (DH + DR) ** (-0.5)
    head_count = q_heads.shape[0]
    row_total = q_heads.shape[1]
    block_rows = min(row_total, BLOCK_ROWS)
    block_count = row_total // block_rows
    col_pos = jnp.arange(row_total, dtype=jnp.int32)

    def one_block(carry, start):
        grad_k_acc, grad_v_acc = carry
        row_pos = start + jnp.arange(block_rows, dtype=jnp.int32)
        scores = masked_scores(q_heads, k_heads, seg_ids, seg_ids, row_pos, col_pos)
        prob_full = jnp.exp(scores - log_total)
        prob_low = prob_full.astype(jnp.bfloat16)
        grad_v_blk = jnp.einsum(
            "hqk,hqd->hkd", prob_low, grad_att, preferred_element_type=jnp.float32
        )
        grad_prob = jnp.einsum(
            "hqd,hkd->hqk", grad_att, v_heads, preferred_element_type=jnp.float32
        )
        row_dot = jnp.sum(prob_full * grad_prob, axis=-1, keepdims=True)
        grad_scores = (prob_full * (grad_prob - row_dot) * scale).astype(jnp.bfloat16)
        grad_q_blk = jnp.einsum(
            "hqk,hkc->hqc", grad_scores, k_heads, preferred_element_type=jnp.float32
        )
        grad_k_blk = jnp.einsum(
            "hqk,hqc->hkc", grad_scores, q_heads, preferred_element_type=jnp.float32
        )
        return ((grad_k_acc + grad_k_blk, grad_v_acc + grad_v_blk), grad_q_blk)

    starts = jnp.arange(block_count, dtype=jnp.int32) * block_rows
    init_acc = (jnp.zeros(k_heads.shape, jnp.float32), jnp.zeros(v_heads.shape, jnp.float32))
    (grad_k, grad_v), grad_q_blocks = lax.scan(one_block, init_acc, starts)
    grad_q = grad_q_blocks.transpose(1, 0, 2, 3).reshape(head_count, row_total, -1)
    return (grad_q, grad_k, grad_v)


MESH_IDS = pl.DeviceIdType.MESH
LOW = jnp.bfloat16
NT = (((1,), (1,)), ((), ()))
TN = (((0,), (0,)), ((), ()))


def axis_parts(mesh):
    devices = mesh.devices
    found = []
    for axis in range(devices.ndim):
        first = (0,) * devices.ndim
        line = [devices[first[:axis] + (i,) + first[axis + 1 :]] for i in range(devices.shape[axis])]
        places = [(*dev.coords, dev.core_on_chip) for dev in line]
        parts = []
        for k, name in enumerate(("x", "y", "z", "core")):
            values = [p[k] for p in places]
            if len(set(values)) > 1:
                stride = next(i for i, v in enumerate(values) if v != values[0])
                parts.append((stride, name, len(set(values))))
        found.append(tuple((name, size) for stride, name, size in sorted(parts, reverse=True)))
    return tuple(found)


def fits_kernels(mesh):
    wide, narrow = axis_parts(mesh)
    return (
        len(wide) == 2
        and wide[1][1] == 2
        and len(narrow) == 2
        and narrow[0][1] == 2
        and narrow[1] == ("core", 2)
    )


class Spot:
    def __init__(self, line):
        wide, narrow = lax.axis_index("wide"), lax.axis_index("narrow")
        self.line = line
        self.z, self.x = wide // 2, wide % 2
        self.y, self.c = narrow // 2, narrow % 2

    def wide(self, z, xf=0):
        return z * 2 + self.x + xf * (1 - 2 * self.x)

    def narrow(self, yf=0, cf=0):
        return (self.y + yf * (1 - 2 * self.y)) * 2 + self.c + cf * (1 - 2 * self.c)

    def device(self, z, xf=0, yf=0, cf=0):
        return {"wide": self.wide(z, xf), "narrow": self.narrow(yf, cf)}

    def flips(self, a, b, c):
        return a * (1 - c) + b * c, b * (1 - c) + a * c

    def index(self, z, a, b, cf=0):
        xf, yf = self.flips(a, b, self.c + cf * (1 - 2 * self.c))
        return self.wide(z, xf) * 4 + self.narrow(yf, cf)

    def routed(self, z, a, b):
        xf, yf = self.flips(a, b, self.c)
        return self.device(z, xf, yf)

    def inside(self, z):
        return (z >= 0) & (z < self.line)

    def near(self, rank):
        table = [sorted(range(self.line), key=lambda to: (abs(to - at), to))[rank] for at in range(self.line)]
        found = jnp.int32(table[0])
        for at in range(1, self.line):
            found = jnp.where(self.z == at, table[at], found)
        return found


def enter(spot, line_too, flips, wide_count=0):
    barrier = pltpu.get_barrier_semaphore()
    devices = [spot.device(spot.z, *flip) for flip in flips]
    if wide_count:
        here = spot.wide(spot.z)
        devices += [
            {"wide": lax.rem(here + step, wide_count), "narrow": spot.narrow()} for step in range(1, wide_count)
        ]
        devices = [dev for flip, dev in zip(flips, devices) if flip != (1, 0, 0)] + devices[len(flips) :]
        line_too = False
    for dev in devices:
        pl.semaphore_signal(barrier, inc=1, device_id=dev, device_id_type=MESH_IDS)
    if not line_too:
        pl.semaphore_wait(barrier, len(devices))
        return
    for step in (-1, 1):
        @pl.when(spot.inside(spot.z + step))
        def _():
            pl.semaphore_signal(barrier, inc=1, device_id=spot.device(spot.z + step), device_id_type=MESH_IDS)
    inner = spot.inside(spot.z - 1) & spot.inside(spot.z + 1)
    @pl.when(inner)
    def _():
        pl.semaphore_wait(barrier, len(devices) + 2)
    @pl.when(jnp.logical_not(inner))
    def _():
        pl.semaphore_wait(barrier, len(devices) + 1)


class Flow:
    def __init__(self, spot, kind, own, place, send, recv):
        self.spot, self.kind, self.own, self.place, self.send, self.recv = spot, kind, own, place, send, recv
        self.sent = []

    @staticmethod
    def steps(kind, line):
        ranks = (0,) if kind == "narrow" else range(line)
        firsts = (0,) if kind == "narrow" else (0, 1)
        seconds = (0,) if kind == "wide" else (0, 1)
        steps = [(r, a, b) for r in ranks for a in firsts for b in seconds]
        return sorted(steps, key=lambda s: (s[0] + s[1] + 2 * s[2], s[1], s[2]))

    @staticmethod
    def sends(kind, rank, a, b):
        moves = []
        if not a and not b and kind != "narrow":
            moves += ["up", "down"]
        if kind != "narrow" and not a and not b:
            moves.append("a")
        if kind != "wide" and not b:
            moves.append("b")
        if kind != "wide":
            moves.append("core")
        return moves

    @classmethod
    def send_count(cls, kind, line):
        return sum(len(cls.sends(kind, *step)) for step in cls.steps(kind, line))

    @staticmethod
    def blocks(kind, line):
        return {"all": line * 8, "wide": line * 2, "narrow": 4}[kind]

    def block(self, z, a, b, cf=0):
        if self.kind == "all":
            return self.spot.index(z, a, b, cf)
        return self.spot.wide(z, a) if self.kind == "wide" else self.spot.narrow(b, cf)

    def target(self, move):
        spot = self.spot
        if move in ("up", "down"):
            return spot.device(spot.z + (1 if move == "up" else -1))
        if move == "core":
            return spot.device(spot.z, 0, 0, 1)
        if self.kind == "all":
            return spot.routed(spot.z, int(move == "a"), int(move == "b"))
        return spot.device(spot.z, int(move == "a"), int(move == "b"))

    def copy(self, block, move, number, first=False):
        view = self.place(block)
        return pltpu.make_async_remote_copy(
            src_ref=self.own if first else view,
            dst_ref=view,
            send_sem=self.send.at[number],
            recv_sem=self.recv.at[block],
            device_id=self.target(move),
            device_id_type=MESH_IDS,
        )

    def arrive(self, block):
        self.copy(block, "a" if self.kind == "wide" else "core", 0).wait_recv()

    def step(self, rank, a, b):
        spot = self.spot
        z = spot.z if rank == 0 else spot.near(rank)
        block = self.block(z, a, b)
        first = rank == 0 and not a and not b
        if not first:
            self.arrive(block)
        for move in self.sends(self.kind, rank, a, b):
            copy = self.copy(block, move, len(self.sent), first)
            when = None
            if move == "up":
                when = spot.inside(spot.z + 1) & (z <= spot.z)
            elif move == "down":
                when = spot.inside(spot.z - 1) & (z >= spot.z)
            if when is None:
                copy.start()
            else:
                pl.when(when)(copy.start)
            self.sent.append((when, copy))

    def from_core(self, z, a, b):
        self.arrive(self.block(z, a, b, 1))

    def finish(self):
        for when, copy in self.sent:
            if when is None:
                copy.wait_send()
            else:
                pl.when(when)(copy.wait_send)


def move_kernel(line, items, *refs):
    count = len(items)
    srcs, dsts = refs[:count], refs[count : 2 * count]
    sends, recvs, local = refs[2 * count : 3 * count], refs[3 * count : 4 * count], refs[4 * count]
    spot = Spot(line)
    kinds = [item["kind"] for item in items]
    flips = set()
    for kind in kinds:
        flips |= {
            "all": {(1, 0, 0), (0, 1, 0), (0, 0, 1)},
            "wide": {(1, 0, 0)},
            "narrow": {(0, 1, 0), (0, 0, 1)},
            "wswap": set(),
            "nswap": {(0, 1, 0), (0, 0, 1), (0, 1, 1)},
        }[kind]
    wide_count = line * 2
    swaps = any(kind == "wswap" for kind in kinds)
    enter(spot, any(k in ("all", "wide") for k in kinds), sorted(flips), wide_count if swaps else 0)
    here_wide, here_narrow = spot.wide(spot.z), spot.narrow()

    flows, copies, own = [], [], []
    for i, item in enumerate(items):
        put = functools.partial(item["put"], dsts[i])
        if item["kind"] in ("wswap", "nswap"):
            continue
        flow = Flow(spot, item["kind"], srcs[i], put, sends[i], recvs[i])
        flows.append(flow)
        own.append(pltpu.make_async_copy(srcs[i], put(flow.block(spot.z, 0, 0)), local.at[i]))
    steps = sorted(
        ((step, flow) for flow in flows for step in Flow.steps(flow.kind, line)),
        key=lambda s: s[0][0] + s[0][1] + 2 * s[0][2],
    )
    for step, flow in steps:
        if step == (0, 0, 0):
            flow.step(*step)
    for i, item in enumerate(items):
        if item["kind"] == "wswap":
            peers = [(lax.rem(here_wide + k, wide_count), k) for k in range(1, wide_count)]
            for to, k in peers:
                copies.append((
                    pltpu.make_async_remote_copy(
                        src_ref=item["take"](srcs[i], to), dst_ref=item["put"](dsts[i], here_wide),
                        send_sem=sends[i].at[k], recv_sem=recvs[i].at[here_wide],
                        device_id={"wide": to, "narrow": here_narrow}, device_id_type=MESH_IDS,
                    ),
                    pltpu.make_async_remote_copy(
                        src_ref=item["take"](srcs[i], to), dst_ref=item["put"](dsts[i], to),
                        send_sem=sends[i].at[k], recv_sem=recvs[i].at[to],
                        device_id={"wide": to, "narrow": here_narrow}, device_id_type=MESH_IDS,
                    ),
                ))
            own.append(pltpu.make_async_copy(
                item["take"](srcs[i], here_wide), item["put"](dsts[i], here_wide), local.at[i]))
        elif item["kind"] == "nswap":
            for k, (yf, cf) in enumerate(((0, 1), (1, 0), (1, 1))):
                to = spot.narrow(yf, cf)
                dev = spot.device(spot.z, 0, yf, cf)
                copies.append((
                    pltpu.make_async_remote_copy(
                        src_ref=item["take"](srcs[i], to), dst_ref=item["put"](dsts[i], here_narrow),
                        send_sem=sends[i].at[k], recv_sem=recvs[i].at[here_narrow],
                        device_id=dev, device_id_type=MESH_IDS,
                    ),
                    pltpu.make_async_remote_copy(
                        src_ref=item["take"](srcs[i], to), dst_ref=item["put"](dsts[i], to),
                        send_sem=sends[i].at[k], recv_sem=recvs[i].at[to],
                        device_id=dev, device_id_type=MESH_IDS,
                    ),
                ))
            own.append(pltpu.make_async_copy(
                item["take"](srcs[i], here_narrow), item["put"](dsts[i], here_narrow), local.at[i]))
    for out, _ in copies:
        out.start()
    for copy in own:
        copy.start()
    for step, flow in steps:
        if step != (0, 0, 0):
            flow.step(*step)
    for flow in flows:
        if flow.kind != "wide":
            for rank, a, b in Flow.steps(flow.kind, line):
                flow.from_core(spot.z if rank == 0 else spot.near(rank), a, b)
    for _, back in copies:
        back.wait_recv()
    for flow in flows:
        flow.finish()
    for out, _ in copies:
        out.wait_send()
    for copy in own:
        copy.wait()


def move(line, items, collective_id):
    counts = {"all": line * 8, "wide": line * 2, "narrow": 4, "wswap": line * 2, "nswap": 4}
    dma = pltpu.SemaphoreType.DMA
    kinds = [item["kind"] for item in items]
    sends = [counts[kind] if kind in ("wswap", "nswap") else Flow.send_count(kind, line) for kind in kinds]
    moved = sum(item["array"].size * item["array"].dtype.itemsize * counts[item["kind"]] for item in items)
    return pl.pallas_call(
        functools.partial(move_kernel, line, items),
        out_shape=[jax.ShapeDtypeStruct(item["shape"], item["array"].dtype) for item in items],
        in_specs=[pl.BlockSpec(memory_space=pltpu.VMEM)] * len(items),
        out_specs=[pl.BlockSpec(memory_space=pl.ANY)] * len(items),
        scratch_shapes=[dma((n,)) for n in sends] + [dma((counts[kind],)) for kind in kinds] + [dma((len(items),))],
        compiler_params=pltpu.CompilerParams(collective_id=collective_id, has_side_effects=True),
        cost_estimate=pl.CostEstimate(flops=0, bytes_accessed=moved, transcendentals=0),
        name="move_blocks",
    )(*[item["array"] for item in items])


def narrow_sum_kernel(line, rows, part, out, held, summed, from_core, from_y,
                      load_sem, core_send, core_recv, y_send, y_recv):
    spot = Spot(line)
    enter(spot, False, [(0, 0, 1), (0, 1, 0)])

    def block(yf, cf):
        return part.at[pl.ds(pl.multiple_of(spot.narrow(yf, cf) * rows, rows), rows), :]

    def to_core(yf):
        return pltpu.make_async_remote_copy(
            src_ref=block(yf, 1), dst_ref=from_core.at[yf], send_sem=core_send.at[yf], recv_sem=core_recv.at[yf],
            device_id=spot.device(spot.z, 0, 0, 1), device_id_type=MESH_IDS,
        )

    def load(yf):
        return pltpu.make_async_copy(block(yf, 0), held.at[yf], load_sem.at[yf])

    over_y = pltpu.make_async_remote_copy(
        src_ref=summed, dst_ref=from_y, send_sem=y_send, recv_sem=y_recv,
        device_id=spot.device(spot.z, 0, 1, 0), device_id_type=MESH_IDS,
    )
    for yf in (1, 0):
        to_core(yf).start()
        load(yf).start()
    load(1).wait()
    to_core(1).wait_recv()
    summed[...] = (held[1].astype(jnp.float32) + from_core[1].astype(jnp.float32)).astype(summed.dtype)
    over_y.start()
    load(0).wait()
    to_core(0).wait_recv()
    total = held[0].astype(jnp.float32) + from_core[0].astype(jnp.float32)
    over_y.wait_recv()
    out[...] = total + from_y[...].astype(jnp.float32)
    over_y.wait_send()
    for yf in (1, 0):
        to_core(yf).wait_send()


def narrow_sum(line, part, collective_id):
    rows, width = part.shape[0] // 4, part.shape[1]
    dma = pltpu.SemaphoreType.DMA
    return pl.pallas_call(
        functools.partial(narrow_sum_kernel, line, rows),
        out_shape=jax.ShapeDtypeStruct((rows, width), jnp.float32),
        in_specs=[pl.BlockSpec(memory_space=pl.ANY)],
        out_specs=pl.BlockSpec(memory_space=pltpu.VMEM),
        scratch_shapes=[
            pltpu.VMEM((2, rows, width), part.dtype),
            pltpu.VMEM((rows, width), part.dtype),
            pltpu.VMEM((2, rows, width), part.dtype),
            pltpu.VMEM((rows, width), part.dtype),
            dma((2,)),
            dma((2,)),
            dma((2,)),
            dma,
            dma,
        ],
        compiler_params=pltpu.CompilerParams(collective_id=collective_id, has_side_effects=True),
        cost_estimate=pl.CostEstimate(
            flops=part.size, bytes_accessed=2 * part.size * part.dtype.itemsize, transcendentals=0
        ),
        name="narrow_sum",
    )(part)


def rows_in_kernel(line, sizes, hid_own, grad_own, gates, w_up, s_up, w_down, s_down,
                   hid_all, grad_all, act_e, act_s, dgu_e, dgu_s,
                   land_h, land_g, v_up, v_sup, v_down, v_sdown, t_act, t_sact, t_dgu, t_sdgu,
                   in_sem, h_send, h_recv, g_send, g_recv, own_sem, keep_sem, out_sem):
    rows, experts, hid, shared = sizes
    group = 4 * rows
    spot = Spot(line)
    loads = [
        pltpu.make_async_copy(src, dst, in_sem.at[i])
        for i, (src, dst) in enumerate(((w_up, v_up), (w_down, v_down), (s_up, v_sup), (s_down, v_sdown)))
    ]
    for copy in loads:
        copy.start()
    enter(spot, True, [(0, 0, 1), (0, 1, 0), (1, 0, 0)])

    def place(land, block):
        return land.at[pl.ds(pl.multiple_of(block * rows, rows), rows), :]

    flows = [
        Flow(spot, "all", hid_own, functools.partial(place, land_h), h_send, h_recv),
        Flow(spot, "all", grad_own, functools.partial(place, land_g), g_send, g_recv),
    ]
    for flow in flows:
        flow.step(0, 0, 0)
    mine = flows[0].block(spot.z, 0, 0)
    own = [
        pltpu.make_async_copy(hid_own, place(land_h, mine), own_sem.at[0]),
        pltpu.make_async_copy(grad_own, place(land_g, mine), own_sem.at[1]),
    ]
    for copy in own:
        copy.start()

    def keeps(n, at):
        span = pl.ds(pl.multiple_of(at * group, group), group)
        return (
            pltpu.make_async_copy(land_h.at[span, :], hid_all.at[span, :], keep_sem.at[0, n]),
            pltpu.make_async_copy(land_g.at[span, :], grad_all.at[span, :], keep_sem.at[1, n]),
        )

    def stores(n, at):
        cols = pl.ds(pl.multiple_of(at * group, group), group)
        slot = n % 2
        pairs = (
            (t_act.at[slot], act_e.at[:, cols], out_sem.at[0, slot]),
            (t_sact.at[slot], act_s.at[:, cols], out_sem.at[1, slot]),
            (t_dgu.at[slot], dgu_e.at[:, cols], out_sem.at[2, slot]),
            (t_sdgu.at[slot], dgu_s.at[:, cols], out_sem.at[3, slot]),
        )
        return [pltpu.make_async_copy(*pair) for pair in pairs]

    def both_ways(gate_part, up_part, grad_part, gate):
        sig = 1.0 / (1.0 + jnp.exp(-gate_part))
        silu = gate_part * sig
        if gate is not None:
            grad_part = grad_part * gate
        grad_gate = grad_part * up_part * (sig + silu * (1.0 - sig))
        act = silu * up_part
        if gate is not None:
            act = act * gate
        return act.astype(LOW), grad_gate.astype(LOW), (grad_part * silu).astype(LOW)

    done = []

    def compute(at):
        n = len(done)
        if n >= 2:
            for copy in stores(n - 2, done[n - 2]):
                copy.wait()
        slot = n % 2
        cols = pl.ds(pl.multiple_of(at * group, group), group)
        h, g = land_h[cols, :], land_g[cols, :]
        for e in range(experts):
            gu = lax.dot_general(
                v_up[2 * e * hid : 2 * (e + 1) * hid, :], h, NT, preferred_element_type=jnp.float32
            )
            da = lax.dot_general(v_down[e * hid : (e + 1) * hid, :], g, NT, preferred_element_type=jnp.float32)
            act, dg, du = both_ways(gu[:hid], gu[hid:], da, gates[e : e + 1, cols])
            t_act[slot, e * hid : (e + 1) * hid, :] = act
            t_dgu[slot, 2 * e * hid : (2 * e + 1) * hid, :] = dg
            t_dgu[slot, (2 * e + 1) * hid : 2 * (e + 1) * hid, :] = du
        gu = lax.dot_general(v_sup[...], h, NT, preferred_element_type=jnp.float32)
        da = lax.dot_general(v_sdown[...], g, NT, preferred_element_type=jnp.float32)
        act, dg, du = both_ways(gu[:shared], gu[shared:], da, None)
        t_sact[slot] = act
        t_sdgu[slot, :shared, :] = dg
        t_sdgu[slot, shared:, :] = du
        done.append(at)
        for copy in (*keeps(n, at), *stores(n, at)):
            copy.start()

    waiting = sorted(
        ((s[0] + s[1] + 2 * s[2], s) for s in Flow.steps("all", line) if s != (0, 0, 0)), key=lambda s: s[0]
    )
    loaded = False
    for _, (rank, a, b) in waiting:
        for flow in flows:
            flow.step(rank, a, b)
        if a and b:
            z = spot.z if rank == 0 else spot.near(rank)
            if not loaded:
                loaded = True
                for copy in own + loads:
                    copy.wait()
            for xf in (0, 1):
                for flow in flows:
                    for other in (0, 1):
                        ca = xf * spot.c + other * (1 - spot.c)
                        cb = other * spot.c + xf * (1 - spot.c)
                        flow.from_core(z, ca, cb)
                compute(spot.wide(z, xf))
    for flow in flows:
        flow.finish()
    count = len(done)
    for n, at in enumerate(done):
        for copy in (*keeps(n, at), *(stores(n, at) if n >= count - 2 else ())):
            copy.wait()


def rows_in(line, hid_own, grad_own, gates, w_up, s_up, w_down, s_down, experts, collective_id):
    rows, width = hid_own.shape
    tokens = rows * line * 8
    hid, shared = w_down.shape[0] // experts, s_down.shape[0]
    group = 4 * rows
    dma = pltpu.SemaphoreType.DMA
    hbm = pl.BlockSpec(memory_space=pl.ANY)
    vmem = pl.BlockSpec(memory_space=pltpu.VMEM)
    sends = Flow.send_count("all", line)
    out = [(tokens, width), (tokens, width)]
    out += [(f, tokens) for f in (w_down.shape[0], shared, w_up.shape[0], 2 * shared)]
    return pl.pallas_call(
        functools.partial(rows_in_kernel, line, (rows, experts, hid, shared)),
        out_shape=[jax.ShapeDtypeStruct(shape, LOW) for shape in out],
        in_specs=[vmem, vmem, vmem] + [hbm] * 4,
        out_specs=[hbm] * 6,
        scratch_shapes=[pltpu.VMEM((tokens, width), LOW)] * 2
        + [pltpu.VMEM(arr.shape, LOW) for arr in (w_up, s_up, w_down, s_down)]
        + [pltpu.VMEM((2, f, group), LOW) for f in (w_down.shape[0], shared, w_up.shape[0], 2 * shared)]
        + [
            dma((4,)),
            dma((sends,)),
            dma((line * 8,)),
            dma((sends,)),
            dma((line * 8,)),
            dma((2,)),
            dma((2, line * 2)),
            dma((4, 2)),
        ],
        compiler_params=pltpu.CompilerParams(
            collective_id=collective_id, has_side_effects=True, vmem_limit_bytes=60 << 20
        ),
        cost_estimate=pl.CostEstimate(
            flops=6 * (w_down.shape[0] + shared) * tokens * width,
            bytes_accessed=6 * tokens * width,
            transcendentals=(w_down.shape[0] + shared) * tokens,
        ),
        name="rows_in",
    )(hid_own, grad_own, gates, w_up, s_up, w_down, s_down)


class Sum:
    def __init__(self, spot, rows, lhs, w, loads, refs):
        self.spot, self.rows, self.lhs, self.w, self.loads = spot, rows, lhs, w, loads
        (self.stage, self.core_buf, self.b_buf, self.a_buf, self.z_buf,
         self.core_send, self.core_recv, self.b_send, self.b_recv, self.a_send, self.a_recv,
         self.z_send, self.z_recv) = refs

    def zed(self, j):
        rank = self.spot.line - 1 - j
        return self.spot.z if rank == 0 else self.spot.near(rank)

    def group(self, xf, j):
        z = self.zed(j)
        return z, self.spot.wide(z, xf)

    def place(self, at, yf, cf):
        start = pl.multiple_of(self.spot.narrow(yf, cf) * self.rows, self.rows)
        return self.stage.at[at, pl.ds(start, self.rows), :]

    def copy(self, src, dst, send, recv, number, to, device):
        return pltpu.make_async_remote_copy(
            src_ref=src, dst_ref=dst.at[to], send_sem=send.at[number], recv_sem=recv.at[to],
            device_id=device, device_id_type=MESH_IDS,
        )

    def to_core(self, z, at, xf, yf):
        s = (z * 2 + xf) * 2 + yf
        return self.copy(self.place(at, yf, 1), self.core_buf, self.core_send, self.core_recv, s, s,
                         self.spot.device(self.spot.z, 0, 0, 1))

    def to_b(self, z, at, yf, a):
        s = z * 2 + a
        return self.copy(self.place(at, yf, 0), self.b_buf, self.b_send, self.b_recv, s, s,
                         self.spot.routed(self.spot.z, 0, 1))

    def to_a(self, z, at, yf):
        return self.copy(self.place(at, yf, 0), self.a_buf, self.a_send, self.a_recv, z, z,
                         self.spot.routed(self.spot.z, 1, 0))

    def to_z(self, z, at, down):
        return self.copy(self.place(at, 0, 0), self.z_buf, self.z_send, self.z_recv, z, down * self.spot.line + z,
                         self.spot.device(self.spot.z + 1 - 2 * down))

    def only(self, core, act):
        pl.when(self.spot.c == core)(act)

    def produce(self, xf, j, chunk):
        z, at = self.group(xf, j)
        size = 4 * self.rows
        cols = pl.ds(pl.multiple_of(at * size, size), size)
        for copy in self.loads(xf, j, at):
            copy.wait()
        width = self.stage.shape[2]

        @pl.loop(0, width // chunk)
        def _(t):
            cut = pl.ds(pl.multiple_of(t * chunk, chunk), chunk)
            value = sum(
                lax.dot_general(lhs[:, cols], w[:, cut], TN, preferred_element_type=jnp.float32)
                for lhs, w in zip(self.lhs, self.w)
            )
            self.stage[at, :, cut] = value.astype(LOW)

        for yf in (1, 0):
            self.to_core(z, at, xf, yf).start()

    def joined(self, z, at, xf, yf):
        self.to_core(z, at, xf, yf).wait_recv()
        there = self.core_buf[(z * 2 + xf) * 2 + yf]
        return self.place(at, yf, 0)[...].astype(jnp.float32) + there.astype(jnp.float32)

    def send_b(self, xf, yf, a, j):
        z, at = self.group(xf, j)
        self.place(at, yf, 0)[...] = self.joined(z, at, xf, yf).astype(LOW)
        self.to_b(z, at, yf, a).start()

    def send_a(self, xf, yf, j):
        z, at = self.group(xf, j)
        value = self.joined(z, at, xf, yf)
        self.to_b(z, at, yf, 1).wait_recv()
        self.place(at, yf, 0)[...] = (value + self.b_buf[z * 2 + 1].astype(jnp.float32)).astype(LOW)
        self.to_a(z, at, yf).start()

    def send_z(self, j, out):
        spot = self.spot
        z, at = self.group(0, j)
        value = self.joined(z, at, 0, 0)
        self.to_b(z, at, 0, 0).wait_recv()
        self.to_a(z, at, 0).wait_recv()
        value += self.b_buf[z * 2].astype(jnp.float32) + self.a_buf[z].astype(jnp.float32)
        last = j == spot.line - 1
        if last:
            out[...] = value
        else:
            self.place(at, 0, 0)[...] = value.astype(LOW)
        for down in (0, 1):
            behind = spot.inside(spot.z - 1 + 2 * down)
            if last:
                @pl.when(behind)
                def _():
                    self.to_z(z, at, down).wait_recv()
                    out[...] += self.z_buf[down * spot.line + z].astype(jnp.float32)
            else:
                @pl.when((z < spot.z) if down else (z > spot.z))
                def _():
                    @pl.when(behind)
                    def _():
                        self.to_z(z, at, down).wait_recv()
                        more = self.place(at, 0, 0)[...].astype(jnp.float32)
                        more += self.z_buf[down * spot.line + z].astype(jnp.float32)
                        self.place(at, 0, 0)[...] = more.astype(LOW)
                    self.to_z(z, at, down).start()

    def early(self, j):
        self.send_b(1, 1, 1, j)
        self.only(1, lambda: self.send_b(1, 0, 0, j))

    def middle(self, j):
        self.only(0, lambda: self.send_b(0, 1, 0, j))
        self.only(0, lambda: self.send_a(1, 0, j))

    def late(self, j):
        self.only(1, lambda: self.send_a(0, 1, j))

    def finish(self):
        for j in range(self.spot.line):
            for xf in (1, 0):
                z, at = self.group(xf, j)
                for yf in (1, 0):
                    self.to_core(z, at, xf, yf).wait_send()
            z, at = self.group(1, j)
            self.to_b(z, at, 1, 1).wait_send()
            self.only(1, lambda: self.to_b(z, at, 0, 0).wait_send())
            self.only(0, lambda: self.to_a(z, at, 0).wait_send())
            z2, at2 = self.group(0, j)
            self.only(0, lambda: self.to_b(z2, at2, 1, 0).wait_send())
            self.only(1, lambda: self.to_a(z2, at2, 1).wait_send())
            if j < self.spot.line - 1:
                for down in (0, 1):
                    @pl.when((z2 < self.spot.z) if down else (z2 > self.spot.z))
                    def _():
                        self.to_z(z2, at2, down).wait_send()


def rows_out_kernel(line, rows, chunk, count, *refs):
    spot = Spot(line)
    lefts, rights = refs[: 2 * count], refs[2 * count : 4 * count]
    outs = refs[4 * count : 5 * count]
    v_lefts, v_rights = refs[5 * count : 7 * count], refs[7 * count : 9 * count]
    rest = refs[9 * count :]
    in_sem, lhs_sem = rest[:2]
    per = 13
    size = 4 * rows
    right_loads = [pltpu.make_async_copy(rights[k], v_rights[k], in_sem.at[k]) for k in range(2 * count)]

    def loader(s):
        def loads(xf, j, at):
            cols = pl.ds(pl.multiple_of(at * size, size), size)
            return [
                pltpu.make_async_copy(
                    lefts[k].at[:, cols], v_lefts[k].at[:, cols], lhs_sem.at[k, (1 - xf) * line + j]
                )
                for k in (2 * s, 2 * s + 1)
            ]

        return loads

    sums = [
        Sum(spot, rows, v_lefts[2 * s : 2 * s + 2], v_rights[2 * s : 2 * s + 2], loader(s),
            rest[2 + s * per : 2 + (s + 1) * per])
        for s in range(count)
    ]
    for s, one in enumerate(sums):
        for k in (2 * s, 2 * s + 1):
            right_loads[k].start()
        for xf in (1, 0):
            for j in range(line):
                _, at = one.group(xf, j)
                for copy in one.loads(xf, j, at):
                    copy.start()
    enter(spot, True, [(0, 0, 1), (0, 1, 0), (1, 0, 0)])
    ready = set()

    def produce(s, xf, j):
        if s not in ready:
            ready.add(s)
            for k in (2 * s, 2 * s + 1):
                right_loads[k].wait()
        sums[s].produce(xf, j, chunk)

    first = sums[0]
    for j in range(line):
        produce(0, 1, j)
        if j:
            first.early(j - 1)
    for j in range(line):
        produce(0, 0, j)
        if j == 0:
            first.early(line - 1)
        else:
            first.middle(j - 1)
    for s in range(1, count):
        later = sums[s]
        produce(s, 1, 0)
        if s == 1:
            first.middle(line - 1)
        for j in range(1, line):
            produce(s, 1, j)
            later.early(j - 1)
            if s == 1:
                first.late(j - 1)
        produce(s, 0, 0)
        later.early(line - 1)
        if s == 1:
            first.late(line - 1)
        for j in range(1, line):
            produce(s, 0, j)
            later.middle(j - 1)
            if s == 1:
                first.send_z(j - 1, outs[0])
        if s == 1:
            first.send_z(line - 1, outs[0])
        later.middle(line - 1)
        for j in range(line):
            later.late(j)
        for j in range(line):
            later.send_z(j, outs[s])
    if count == 1:
        first.middle(line - 1)
        for j in range(line):
            first.late(j)
        for j in range(line):
            first.send_z(j, outs[0])
    for one in sums:
        one.finish()


def rows_out(line, pairs, collective_id, chunk=512):
    count = len(pairs)
    lefts = [left for pair in pairs for left, _ in pair]
    rights = [right for pair in pairs for _, right in pair]
    tokens, width = lefts[0].shape[1], rights[0].shape[1]
    rows = tokens // (line * 8)
    dma = pltpu.SemaphoreType.DMA
    slots = line * 4
    scratch = [pltpu.VMEM(arr.shape, LOW) for arr in lefts + rights] + [dma((2 * count,)), dma((2 * count, line * 2))]
    for _ in range(count):
        scratch += [
            pltpu.VMEM((line * 2, 4 * rows, width), LOW),
            pltpu.VMEM((slots, rows, width), LOW),
            pltpu.VMEM((line * 2, rows, width), LOW),
            pltpu.VMEM((line, rows, width), LOW),
            pltpu.VMEM((line * 2, rows, width), LOW),
            dma((slots,)),
            dma((slots,)),
            dma((line * 2,)),
            dma((line * 2,)),
            dma((line,)),
            dma((line,)),
            dma((line,)),
            dma((line * 2,)),
        ]
    return pl.pallas_call(
        functools.partial(rows_out_kernel, line, rows, chunk, count),
        out_shape=[jax.ShapeDtypeStruct((rows, width), jnp.float32)] * count,
        in_specs=[pl.BlockSpec(memory_space=pl.ANY)] * (4 * count),
        out_specs=[pl.BlockSpec(memory_space=pltpu.VMEM)] * count,
        scratch_shapes=scratch,
        compiler_params=pltpu.CompilerParams(
            collective_id=collective_id, has_side_effects=True, vmem_limit_bytes=63 << 20
        ),
        cost_estimate=pl.CostEstimate(
            flops=2 * sum(arr.shape[0] for arr in lefts) * tokens * width,
            bytes_accessed=4 * count * tokens * width,
            transcendentals=0,
        ),
        name="rows_out",
    )(*lefts, *rights)

class Links:
    AXES = {"all": ("wide", "narrow"), "wide": "wide", "narrow": "narrow", "wswap": "wide", "nswap": "narrow"}

    def __init__(self, mesh):
        self.line = axis_parts(mesh)[0][0][1] if fits_kernels(mesh) else None
        self.shape = dict(mesh.shape)
        self.calls = 0

    def number(self):
        self.calls += 1
        return self.calls

    def item(self, array, kind, shape, put, take, plain):
        return {"array": array, "kind": kind, "shape": shape, "put": put, "take": take, "plain": plain}

    @staticmethod
    def part(axis, size):
        def view(ref, index):
            cut = pl.ds(pl.multiple_of(index * size, size), size)
            return ref.at[tuple(cut if k == axis else slice(None) for k in range(len(ref.shape)))]

        return view

    def count(self, kind):
        return self.shape["wide"] * self.shape["narrow"] if kind == "all" else self.shape[self.AXES[kind]]

    def gather(self, array, kind, axis):
        shape = list(array.shape)
        shape[axis] *= self.count(kind)
        plain = functools.partial(lax.all_gather, array, self.AXES[kind], axis=axis, tiled=True)
        return self.item(array, kind, tuple(shape), self.part(axis, array.shape[axis]), None, plain)

    def swap(self, array, kind, split, concat):
        count = self.count(kind)
        shape = list(array.shape)
        shape[split] //= count
        size = shape[split]
        put = self.part(concat, array.shape[concat])
        shape[concat] *= count
        plain = functools.partial(
            lax.all_to_all, array, self.AXES[kind], split_axis=split, concat_axis=concat, tiled=True
        )
        return self.item(array, kind, tuple(shape), put, self.part(split, size), plain)

    def grid(self, array):
        rows, cols = array.shape
        down, across = self.shape["narrow"], self.shape["wide"]

        def put(ref, index):
            at_row = pl.multiple_of((index % down) * rows, rows)
            at_col = pl.multiple_of((index // down) * cols, cols)
            return ref.at[pl.ds(at_row, rows), pl.ds(at_col, cols)]

        def plain():
            return lax.all_gather(lax.all_gather(array, "narrow", axis=0, tiled=True), "wide", axis=1, tiled=True)

        return self.item(array, "all", (rows * down, cols * across), put, None, plain)

    def weave(self, array):
        shape = (array.shape[0], self.shape["narrow"], *array.shape[1:])
        plain = functools.partial(lax.all_gather, array, "narrow", axis=1)
        return self.item(array, "narrow", shape, lambda ref, index: ref.at[:, index], None, plain)

    def move(self, *items):
        if self.line:
            return move(self.line, items, self.number())
        return [item["plain"]() for item in items]

    def narrow_sum(self, part):
        if self.line:
            return narrow_sum(self.line, part, self.number())
        return lax.psum_scatter(part, "narrow", scatter_dimension=0, tiled=True).astype(jnp.float32)

    def rows_in(self, hidden, grad, gates, w_up, s_up, w_down, s_down, experts):
        if self.line:
            return rows_in(self.line, hidden, grad, gates, w_up, s_up, w_down, s_down, experts, self.number())
        hidden, grad = (lax.all_gather(rows, self.AXES["all"], axis=0, tiled=True) for rows in (hidden, grad))

        def both_ways(up, down, gate):
            gu, grad_act = dot_nt(up, hidden), dot_nt(down, grad) * gate
            gate_part, up_part = jnp.split(gu, 2)
            sig = jax.nn.sigmoid(gate_part)
            grad_gate = grad_act * up_part * sig * (1.0 + gate_part * (1.0 - sig))
            grad_up = grad_act * gate_part * sig
            act = gate_part * sig * up_part * gate
            return act.astype(LOW), jnp.concatenate([grad_gate.astype(LOW), grad_up.astype(LOW)])

        ups, downs = jnp.split(w_up, experts), jnp.split(w_down, experts)
        pairs = [both_ways(ups[e], downs[e], gates[e : e + 1]) for e in range(experts)]
        act_s, dgu_s = both_ways(s_up, s_down, 1.0)
        acts, dgus = (jnp.concatenate(parts) for parts in zip(*pairs))
        return hidden, grad, acts, act_s, dgus, dgu_s

    def rows_out(self, *pairs):
        if self.line:
            return rows_out(self.line, pairs, self.number())
        sums = []
        for pair in pairs:
            term = sum(dot_tn(left, right) for left, right in pair).astype(LOW)
            term = lax.psum_scatter(term, self.AXES["all"], scatter_dimension=0, tiled=True)
            sums.append(term.astype(jnp.float32))
        return sums


def rows_of(array, index, count):
    return lax.dynamic_slice_in_dim(array, index * count, count, 0)


def dot_nt(lhs, rhs):
    return lax.dot_general(lhs, rhs, (((1,), (1,)), ((), ())), preferred_element_type=jnp.float32)


def dot_tn(lhs, rhs):
    return lax.dot_general(lhs, rhs, (((0,), (0,)), ((), ())), preferred_element_type=jnp.float32)


def dot_nn(lhs, rhs):
    return jnp.dot(lhs, rhs, preferred_element_type=jnp.float32)


def per_device(
    links,
    tokens_in,
    seg_ids,
    routes,
    gate_vals,
    attn_gain,
    w_query,
    w_latent,
    latent_gain,
    w_expand,
    w_output,
    ffn_gain,
    w_shared_in,
    w_shared_out,
    w_expert_in,
    w_expert_out,
    grad_output,
):
    links.calls = 0
    low = LOW
    wide_count = lax.axis_size("wide")
    narrow_count = lax.axis_size("narrow")
    wide_at = lax.axis_index("wide")
    narrow_at = lax.axis_index("narrow")
    tok_rows, width = tokens_in.shape
    own_rows = tok_rows // narrow_count
    local_experts, _, _, hidden_local = w_expert_in.shape
    num_experts = local_experts * wide_count
    head_local = w_query.shape[1] // (DH + DR)

    def mine(array):
        return rows_of(array, narrow_at, own_rows)

    x_float = tokens_in.astype(jnp.float32)
    x_normed, inv_one = rms_forward(x_float, attn_gain)
    x_low = x_normed.astype(low)
    latent_part = rows_of(w_latent.T, narrow_at, w_latent.shape[1] // narrow_count)
    chosen = routes[:, :, None] == jnp.arange(num_experts, dtype=jnp.int32)
    gate_table = jnp.sum(jnp.where(chosen, gate_vals[:, :, None], 0.0), axis=1).T
    gate_table = gate_table.reshape(wide_count, local_experts, tok_rows)
    gate_table = jnp.pad(gate_table, ((0, 0), (0, -local_experts % 8), (0, 0))).reshape(-1, tok_rows)
    wq_all, wkva_all, wkvb_all, wo_all, shared_in, shared_out, gates, x_part = links.move(
        links.gather(w_query, "wide", 0),
        links.grid(latent_part),
        links.gather(w_expand, "wide", 0),
        links.gather(w_output, "wide", 1),
        links.swap(w_shared_in.transpose(1, 2, 0), "wswap", 1, 2),
        links.swap(w_shared_out, "wswap", 0, 1),
        links.swap(gate_table, "wswap", 0, 1),
        links.swap(mine(x_low), "wswap", 1, 0),
    )

    cos_tab, sin_tab = rotary_tables(positions(seg_ids))
    queries = dot_nn(x_low, wq_all).reshape(tok_rows, head_local, DH + DR).transpose(1, 0, 2)
    q_heads = jnp.concatenate(
        [queries[..., :DH], rotate(queries[..., DH:], cos_tab, sin_tab)], -1
    ).astype(low)
    latent_all = dot_nt(x_low, wkva_all)
    latent = latent_all[:, :KVR]
    latent_normed, inv_lat = rms_forward(latent, latent_gain)
    latent_low = latent_normed.astype(low)
    key_rope = rotate(latent_all[:, KVR:], cos_tab, sin_tab).astype(low)
    expanded = dot_nn(latent_low, wkvb_all).reshape(tok_rows, head_local, 2 * DH).transpose(1, 0, 2)
    key_nope = expanded[..., :DH].astype(low)
    v_heads = expanded[..., DH:].astype(low)
    k_heads = jnp.concatenate(
        [key_nope, jnp.broadcast_to(key_rope[None], (head_local, tok_rows, DR))], -1
    )
    attended, log_total = attention_forward(q_heads, k_heads, v_heads, seg_ids)
    merged = attended.transpose(1, 0, 2).reshape(tok_rows, head_local * DH)
    mixed = links.narrow_sum(dot_nn(merged, wo_all).astype(low))

    x_rows = mine(x_float)
    inv_one_rows = mine(inv_one)
    resid = x_rows + mixed
    resid_normed, inv_two = rms_forward(resid, ffn_gain)

    expert_rows = local_experts * hidden_local
    w_up = w_expert_in.transpose(0, 2, 3, 1).reshape(2 * expert_rows, width)
    w_down = w_expert_out.reshape(expert_rows, width)
    s_up = shared_in.reshape(-1, width)
    hidden, grad_all, act_exp, act_sh, grad_gu_exp, grad_gu_sh = links.rows_in(
        resid_normed.astype(low), mine(grad_output), gates, w_up, s_up, w_down, shared_out, local_experts
    )
    grad_hidden, out_rows = links.rows_out(
        ((grad_gu_exp, w_up), (grad_gu_sh, s_up)), ((act_exp, w_down), (act_sh, shared_out))
    )
    grad_exp_out = dot_nn(act_exp, grad_all).reshape(local_experts, hidden_local, width)
    grad_shout = dot_nn(act_sh, grad_all).astype(low)
    grad_exp_in = dot_nn(grad_gu_exp, hidden).reshape(local_experts, 2, hidden_local, width)
    grad_exp_in = grad_exp_in.transpose(0, 3, 1, 2)
    grad_shin = dot_nn(grad_gu_sh, hidden).reshape(2, -1, width).astype(low)
    out_rows = (resid + out_rows).astype(low)

    grad_resid, grad_ffn = rms_backward(resid, inv_two, ffn_gain, grad_hidden)
    grad_resid = grad_resid + mine(grad_output).astype(jnp.float32)
    grad_low, x_cols = links.move(
        links.gather(grad_resid.astype(low), "narrow", 0),
        links.weave(x_part.reshape(wide_count, own_rows, -1)),
    )
    x_cols = x_cols.reshape(wide_count * tok_rows, -1)
    grad_merged = dot_nt(grad_low, wo_all)
    grad_wo = dot_tn(merged, grad_low).astype(low)
    red_wo = lax.psum_scatter(grad_wo, "wide", scatter_dimension=1, tiled=True)
    grad_att = grad_merged.reshape(tok_rows, head_local, DH).transpose(1, 0, 2).astype(low)
    grad_q, grad_k, grad_v = attention_backward(
        q_heads, k_heads, v_heads, grad_att, log_total, seg_ids
    )
    grad_q_pre = jnp.concatenate(
        [grad_q[..., :DH], unrotate(grad_q[..., DH:], cos_tab, sin_tab)], -1
    ).astype(low)
    grad_q_pre = grad_q_pre.transpose(1, 0, 2).reshape(tok_rows, head_local * (DH + DR))
    grad_rope_part = jnp.sum(grad_k[..., DH:], axis=0)
    grad_expanded = jnp.concatenate([grad_k[..., :DH], grad_v], -1).astype(low)
    grad_expanded = grad_expanded.transpose(1, 0, 2).reshape(tok_rows, head_local * 2 * DH)
    grad_wkvb = dot_tn(latent_low, grad_expanded).astype(low)
    red_wkvb = lax.psum_scatter(grad_wkvb, "wide", scatter_dimension=0, tiled=True)
    grad_latent_part = dot_nt(grad_expanded, wkvb_all)
    grad_x_part = dot_nt(grad_q_pre, wq_all)
    terms = jnp.concatenate([grad_x_part, grad_latent_part, grad_rope_part], 1)
    terms = links.narrow_sum(terms.astype(low))
    grad_x_query, latent_terms = terms[:, :width], terms[:, width:]
    grad_latent, grad_lat_gain = rms_backward(
        mine(latent), mine(inv_lat), latent_gain, latent_terms[:, :KVR]
    )
    grad_rope = unrotate(latent_terms[:, KVR:], mine(cos_tab), mine(sin_tab))
    grad_latent_all = jnp.concatenate([grad_latent, grad_rope], -1).astype(low)
    grad_x_normed = grad_x_query + dot_nn(grad_latent_all, wkva_all)
    grad_x, grad_att_gain = rms_backward(x_rows, inv_one_rows, attn_gain, grad_x_normed)
    grad_tokens = (grad_x + grad_resid).astype(low)
    gains = jnp.concatenate(
        [part.reshape(wide_count, -1) for part in (grad_att_gain, grad_ffn, grad_lat_gain)], 1
    )
    q_pre_all, latent_rows, grad_tokens, layer_out, red_shout, red_shin, gains = links.move(
        links.gather(grad_q_pre, "wide", 0),
        links.gather(grad_latent_all, "all", 0),
        links.gather(grad_tokens, "narrow", 0),
        links.swap(out_rows, "nswap", 1, 0),
        links.swap(grad_shout, "wswap", 1, 0),
        links.swap(grad_shin, "wswap", 2, 1),
        links.gather(gains, "all", 0),
    )
    red_wkva = dot_tn(x_cols, latent_rows)
    red_wq = dot_tn(x_cols, q_pre_all)
    gains = gains.reshape(-1, wide_count, gains.shape[1])
    gains = jnp.sum(lax.dynamic_index_in_dim(gains, wide_at, 1, keepdims=False), axis=0)
    part = width // wide_count
    red_att_gain, red_ffn, red_lat_gain = gains[:part], gains[part : 2 * part], gains[2 * part :]
    return (
        layer_out,
        grad_tokens.astype(jnp.float32),
        red_att_gain,
        red_wq,
        red_wkva,
        red_lat_gain,
        red_wkvb.astype(jnp.float32),
        red_wo.astype(jnp.float32),
        red_ffn,
        red_shin.astype(jnp.float32).transpose(2, 0, 1),
        red_shout.astype(jnp.float32),
        grad_exp_in,
        grad_exp_out,
    )


def solution(mesh):
    placed = (
        P("wide", None),
        P("wide"),
        P("wide", None),
        P("wide", None),
        P(),
        P("wide", "narrow"),
        P("wide", None),
        P(),
        P("wide", "narrow"),
        P("narrow", "wide"),
        P(),
        P("wide", None, "narrow"),
        P("narrow", "wide"),
        P("wide", None, None, "narrow"),
        P("wide", "narrow", None),
        P("wide", None),
    )
    return jax.shard_map(
        functools.partial(per_device, Links(mesh)),
        mesh=mesh,
        in_specs=placed,
        out_specs=(
            P("wide", "narrow"),
            P("wide", None),
            P("wide"),
            P("wide", "narrow"),
            P("wide", None),
            P("wide"),
            P("wide", "narrow"),
            P("narrow", "wide"),
            P("wide"),
            P("wide", None, "narrow"),
            P("narrow", "wide"),
            P("wide", None, None, "narrow"),
            P("wide", "narrow", None),
        ),
        check_vma=False,
    )
```

time: 2240 us -> 559 us (0.25)
  waiting for transfers between devices: 1830 us -> 0.04 us
  Pallas kernels: 0 us -> 419 us
  local copies, waits for them, and re-layouts: 123 us -> 10.4 us
  matrix products: 155 us -> 68.9 us
  starting transfers between devices: 32.7 us -> 0.29 us
  blocking collectives: 27.3 us -> 0 us
    reduce_scatter x9 -> x1, waiting for transfers between devices: 784 us -> 0.01 us  [per_device(): red_wo = lax.psum_scatter(grad_wo, 'wide', scatter_dimension=1, tiled=True)]
    all_to_all x4 -> x0, waiting for transfers between devices: 479 us -> none  [the longest x1 190 us: per_device(): lax.all_to_all(grad_send, 'wide', split_axis=0, concat_axis=0, tiled=True)]
    all_gather x7 -> x0, waiting for transfers between devices: 427 us -> none  [the longest x1 170 us: per_device(): lax.all_gather(w_shared_in, 'wide', axis=0, tiled=True)]
    pallas_call x0 -> x7, Pallas kernels: none -> 419 us  [the longest x3 219 us: move(): pl.pallas_call(functools.partial(move_kernel, line, items), out_shape=[ja...]
    dot_general x24 -> x16, matrix products: 143 us -> 60.3 us  [the longest x8 39.9 us: dot_nn(): return jnp.dot(lhs, rhs, preferred_element_type=jnp.float32)]
    reduce_scatter x1, waiting for transfers between devices: 69.6 us -> 0.01 us  [per_device(): lax.psum_scatter(grad_wkvb, 'wide', scatter_dimension=0, tiled=True)]
    psum x2 -> x0, waiting for transfers between devices: 62.4 us -> none  [the longest x1 39.1 us: per_device(): mixed_full = lax.psum(mixed_part, 'narrow')]
    gather x4 -> x0, local copies, waits for them, and re-layouts: 55.4 us -> none  [the longest x1 19.7 us: per_device(): padded[slot_tokens].reshape(wide_count, local_experts, capacity, width)]
  transfers between devices with their start and end apart: 23 -> 2, of which waited for: 20 -> 0; matrix products, arithmetic and copies ran while one was open for 10% -> 13% of each run, Pallas kernels for 0% -> 21%
where the time goes in v2:
time: 559 us; the launch traced here: 550 us
  Pallas kernels  419 us (75%)
  matrix products  68.9 us (12%)
  other arithmetic  35.9 us (6%)
  between operations  15.4 us (3%)
  local copies, waits for them, and re-layouts  10.4 us (2%)
    pallas_call x3, Pallas kernels, move(): pl.pallas_call(functools.partial(move_kernel, line, items), out_shape=[ja...  219 us
    pallas_call x1, Pallas kernels, rows_out(): pl.pallas_call(functools.partial(rows_out_kernel, line, rows, chunk, coun...  95.5 us
    pallas_call x1, Pallas kernels, rows_in(): pl.pallas_call(functools.partial(rows_in_kernel, line, (rows, experts, hi...  81.1 us
    dot_general x8, matrix products, dot_nn(): return jnp.dot(lhs, rhs, preferred_element_type=jnp.float32)  39.9 us
    pallas_call x2, Pallas kernels, narrow_sum(): pl.pallas_call(functools.partial(narrow_sum_kernel, line, rows), out_shap...  23.2 us
  transfers between devices with their start and end apart: 2, of which 0 were waited for; matrix products, arithmetic and copies ran while one was open for 13% of the time, Pallas kernels for 21%

profile of v2, /device:TPU:31, one launch (start us, length us, event | category | flops | bytes accessed | tf_op | source)
XLA Modules:
  0.0 549.8 jit_solution(7244473556346666470)
XLA Ops:
  8.2 1.5 fusion.19
  9.6 1.5 multiply_reduce_fusion
  11.2 2.8 convert_element_type.102
  15.6 1.8 constant_dynamic-slice_fusion
  17.4 99.8 %move_blocks.3 = (bf16[2048,768]{1,0:T(8,128)(2,1)}, bf16[576,2048]{1,0:T(8,128)(2,1)}, bf16[512,1024]{1,0:T(8,128)(2,1)}, bf16[512,2048]{1,0:T(8,128)(2,1)}, bf...) custom-call(bf16[256,768]{1,0:T(8,128)(2,1)} %refs_0_.1, ...), custom_call_target="tpu_custom_call" | custom-call | bytes 19922944 | tf_op jit(solution)/shard_map/move_blocks/pallas_call | solution.py:430
  117.2 2.8 fusion.43
  120.0 0.9 fusion.39
  123.2 3.3 fusion.42
  128.9 1.7 convolution_convert_fusion.1.part
  130.6 10.5 %narrow_sum.2 = f32[64,2048]{1,0:T(8,128)} custom-call(bf16[256,2048]{1,0:T(8,128)(2,1)} %convolution_convert_fusion.1.part), custom_call_target="tpu_custom_call" | custom-call | flops 524288 | bytes 2097152 | tf_op jit(solution)/shard_map/narrow_sum/pallas_call | solution.py:483
  141.1 1.4 multiply_reduce_fusion.6
  143.8 81.1 %rows_in.1 = (bf16[2048,2048]{1,0:T(8,128)(2,1)}, bf16[2048,2048]{1,0:T(8,128)(2,1)}, bf16[704,2048]{1,0:T(8,128)(2,1)}, bf16[88,2048]{1,0:T(8,128)(2,1)}, bf16[...) custom-call(bf16[64,2048]{1,0:T(8,128)(2,1)} %multiply_convert_fusion.1.hid_own, ...), custom_call_target="tpu_custom_call" | custom-call | flops 19931332608 | bytes 25165824 | tf_op jit(solution)/shard_map/rows_in/pallas_call | solution.py:636
  224.9 95.5 %rows_out.1 = (f32[64,2048]{1,0:T(8,128)}, f32[64,2048]{1,0:T(8,128)}) custom-call(bf16[1408,2048]{1,0:T(8,128)(2,1)} %get-tuple-element.102.refs_0_, bf16[176,2048]{1,0:T(8,128)(2,1)} %get-tuple-element.103.refs_1_, bf16[704,2048]{1,0:T(8,128)(2,1)} %get-tuple-element.104.refs_2_, bf16[88,2048]{1,0:T(8,128)(2,1)} %get-tuple-element.105.refs_3_, ...), custom_call_target="tpu_custom_call" | custom-call | flops 19931332608 | bytes 33554432 | tf_op jit(solution)/shard_map/rows_out/pallas_call | solution.py:928
  320.5 2.7 multiply_reduce_fusion.2
  323.2 2.1 fusion.38
  325.3 17.1 %move_blocks.4 = (bf16[256,2048]{1,0:T(8,128)(2,1)}, bf16[8,4,64,256]{3,2,1,0:T(8,128)(2,1)}) custom-call(bf16[64,2048]{1,0:T(8,128)(2,1)} %get-tuple-element.130.refs_0_, bf16[8,64,256]{2,1,0:T(8,128)(2,1)} %bitcast.104), custom_call_target="tpu_custom_call" | custom-call | bytes 2097152 | tf_op jit(solution)/shard_map/move_blocks/pallas_call | solution.py:430
  342.4 2.7 convolution_convert_fusion.10
  345.3 1.3 fusion.20
  347.0 3.1 fusion.6
  350.1 1.1 slice.170
  351.3 1.6 convolution_convert_fusion.5
  353.2 3.2 convolution_convert_fusion
  356.5 3.1 fusion.7
  359.6 1.0 add_convert_fusion.2
  360.6 1.1 slice.171
  361.7 1.0 slice_reduce_fusion
  363.2 0.9 copy.118.refs_0_
  364.2 3.9 convolution_convert_fusion.2
  368.4 2.6 pad_maximum_fusion.part
  370.9 12.7 %narrow_sum.3 = f32[64,2624]{1,0:T(8,128)} custom-call(bf16[256,2624]{1,0:T(8,128)(2,1)} %pad_maximum_fusion.part), custom_call_target="tpu_custom_call" | custom-call | flops 671744 | bytes 2686976 | tf_op jit(solution)/shard_map/narrow_sum/pallas_call | solution.py:483
  383.6 0.9 add_convert_fusion.5
  384.6 1.1 multiply_reduce_fusion.8
  385.7 1.0 subtract_convert_fusion
  386.8 2.6 multiply_reduce_fusion.3
  389.5 5.8 %convolution_convert_fusion.4.refs_4_ = bf16[88,2048]{1,0:T(8,128)(2,1)} fusion(bf16[88,2048]{1,0:T(8,128)(2,1)S(1)} %copy-done.17, bf16[2048,2048]{1,0:T(8,128)(2,1)} %get-tuple-element.110), kind=kOutput, calls=%fused_computation.5 | convolution fusion | flops 738377728 | bytes 9109504 | tf_op jit(solution)/shard_map/dot_general | solution.py:1062
  395.3 2.6 convolution_convert_fusion.3
  398.6 0.9 add_convert_fusion.1.refs_2_
  399.5 102.2 %move_blocks.5 = (bf16[2048,768]{1,0:T(8,128)(2,1)}, bf16[2048,576]{1,0:T(8,128)(2,1)}, bf16[256,2048]{1,0:T(8,128)(2,1)}, bf16[256,512]{1,0:T(8,128)(2,1)}, bf1...) custom-call(bf16[256,768]{1,0:T(8,128)(2,1)} %copy.118.refs_0_, ...), custom_call_target="tpu_custom_call" | custom-call | bytes 16842752 | tf_op jit(solution)/shard_map/move_blocks/pallas_call | solution.py:430
  501.8 1.4 dynamic-slice_reduce_fusion
  504.2 2.9 convert_element_type.122
  507.1 1.9 fusion.44
  509.0 3.8 fusion.45
  512.9 1.2 convert_bitcast_fusion
  514.1 0.9 convert_element_type.127
  515.0 8.2 %fusion.47 = f32[704,2048]{1,0:T(8,128)} fusion(bf16[704,2048]{1,0:T(8,128)(2,1)S(1)} %copy-done.53, bf16[2048,2048]{1,0:T(8,128)(2,1)S(1)} %bitcast.88), kind=kOutput, calls=%fused_computation.120 | convolution fusion | flops 5905580032 | bytes 17039360 | tf_op jit(solution)/shard_map/dot_general | solution.py:1062
  523.3 15.1 %fusion.46 = f32[1408,2048]{1,0:T(8,128)} fusion(bf16[1408,2048]{1,0:T(8,128)(2,1)S(1)} %bitcast.122, bf16[2048,2048]{1,0:T(8,128)(2,1)S(1)} %bitcast.120), kind=kOutput, calls=%fused_computation.119 | convolution fusion | flops 11811160064 | bytes 25690112 | tf_op jit(solution)/shard_map/dot_general | solution.py:1062
  538.4 1.6 convert_element_type.124
  540.0 1.8 convert_element_type.126
  (185 shorter events, 12.7 us)
Async XLA Ops:
  7.2 7.8 %copy-start = (bf16[256,576]{0,1:T(8,128)(2,1)S(1)}, bf16[256,576]{0,1:T(8,128)(2,1)}, u32[]{:S(2)}) copy-start(bf16[256,576]{0,1:T(8,128)(2,1)} %param.22) | copy-start | bytes 884740
  7.2 7.5 %copy-start.2 = (bf16[256,2048]{1,0:T(8,128)(2,1)S(1)}, bf16[256,2048]{1,0:T(8,128)(2,1)}, u32[]{:S(2)}) copy-start(bf16[256,2048]{1,0:T(8,128)(2,1)} %param.16) | copy-start | bytes 3145732
  7.2 6.8 %copy-start.45 = (f32[256,6]{0,1:T(8,128)S(1)}, f32[256,6]{0,1:T(8,128)}, u32[]{:S(2)}) copy-start(f32[256,6]{0,1:T(8,128)} %param.19) | copy-start | bytes 18436
  7.2 6.7 %copy-start.46 = (s32[256,6]{0,1:T(8,128)S(1)}, s32[256,6]{0,1:T(8,128)}, u32[]{:S(2)}) copy-start(s32[256,6]{0,1:T(8,128)} %param.18) | copy-start | bytes 18436
  7.2 7.4 %copy-start.31 = (f32[2048]{0:T(1024)S(1)}, f32[2048]{0:T(1024)}, u32[]{:S(2)}) copy-start(f32[2048]{0:T(1024)} %param.20) | copy-start | bytes 24580
  7.2 531.2 %reduce-scatter.3.cloned.1.call-start = ((), (), s32[]{:S(2)}) async-start(), calls=%async_computation.2 | async-start | bytes 1179648 | tf_op jit(solution)/shard_map/reduce_scatter | solution.py:1182
  14.0 103.2 %copy-start.47 = (f32[256]{0:T(256)}, f32[256]{0:T(256)S(1)}, u32[]{:S(2)}) copy-start(f32[256]{0:T(256)S(1)} %add_rsqrt_fusion.1) | copy-start | bytes 3076
  117.2 3.7 copy-start.8
  117.2 3.7 copy-start.41
  121.6 5.8 %copy-start.10 = (bf16[256,1024]{0,1:T(8,128)(2,1)}, bf16[256,1024]{0,1:T(8,128)(2,1)S(1)}, u32[]{:S(2)}) copy-start(bf16[256,1024]{0,1:T(8,128)(2,1)S(1)} %copy.127) | copy-start | bytes 1572868
  122.9 3.6 copy-start.21
  123.1 3.7 copy-start.23
  123.2 3.7 copy-start.37
  128.2 12.9 %copy-start.38 = (f32[4,256]{1,0:T(4,128)}, f32[4,256]{1,0:T(4,128)S(1)}, u32[]{:S(2)}) copy-start(f32[4,256]{1,0:T(4,128)S(1)} %log_add_fusion) | copy-start | bytes 12292
  128.6 13.9 %copy-start.12 = (bf16[4,256,128]{1,2,0:T(8,128)(2,1)}, bf16[4,256,128]{1,2,0:T(8,128)(2,1)S(1)}, u32[]{:S(2)}) copy-start(bf16[4,256,128]{1,2,0:T(8,128)(2,1)S(1)} %convolution_convert_fusion.7) | copy-start | bytes 786436
  128.9 14.1 %copy-start.30 = (f32[2048]{0:T(1024)S(1)}, f32[2048]{0:T(1024)}, u32[]{:S(2)}) copy-start(f32[2048]{0:T(1024)} %param.26) | copy-start | bytes 24580
  143.0 81.9 %copy-start.49 = (f32[64]{0:T(128)}, f32[64]{0:T(128)S(1)}, u32[]{:S(2)}) copy-start(f32[64]{0:T(128)S(1)} %get-tuple-element.152) | copy-start | bytes 772
  224.9 98.2 %copy-start.18 = (bf16[64,2048]{1,0:T(8,128)(2,1)S(1)}, bf16[64,2048]{1,0:T(8,128)(2,1)}, u32[]{:S(2)}) copy-start(bf16[64,2048]{1,0:T(8,128)(2,1)} %get-tuple-element.156.grad_own) | copy-start | bytes 786436
  325.3 20.0 %copy-start.11 = (bf16[256,1024]{0,1:T(8,128)(2,1)S(1)}, bf16[256,1024]{0,1:T(8,128)(2,1)}, u32[]{:S(2)}) copy-start(bf16[256,1024]{0,1:T(8,128)(2,1)} %copy-done.10) | copy-start | bytes 1572868
  342.3 4.3 copy-start.4
  342.3 4.3 copy-start.39
  346.6 4.7 copy-start.7
  346.6 4.7 copy-start.42
  346.6 4.7 copy-start.44
  352.9 187.1 %reduce-scatter.5.cloned.1.call-start = ((), (), s32[]{:S(2)}) async-start(), calls=%async_computation.3 | async-start | bytes 2359296 | tf_op jit(solution)/shard_map/reduce_scatter | solution.py:1169
  356.4 6.2 %copy-start.9 = (bf16[512,1024]{1,0:T(8,128)(2,1)S(1)}, bf16[512,1024]{1,0:T(8,128)(2,1)}, u32[]{:S(2)}) copy-start(bf16[512,1024]{1,0:T(8,128)(2,1)} %get-tuple-element.97) | copy-start | bytes 3145732
  363.2 4.9 copy-start.48
  368.1 16.5 %copy-start.16 = (f32[256,512]{1,0:T(8,128)S(1)}, f32[256,512]{1,0:T(8,128)}, u32[]{:S(2)}) copy-start(f32[256,512]{1,0:T(8,128)} %get-tuple-element.142) | copy-start | bytes 1572868
  368.3 18.5 %copy-start.5 = (f32[256,2048]{1,0:T(8,128)S(1)}, f32[256,2048]{1,0:T(8,128)}, u32[]{:S(2)}) copy-start(f32[256,2048]{1,0:T(8,128)} %convert_element_type.102) | copy-start | bytes 6291460
  368.4 18.4 %copy-start.32 = (f32[2048]{0:T(1024)S(1)}, f32[2048]{0:T(1024)}, u32[]{:S(2)}) copy-start(f32[2048]{0:T(1024)} %param.20) | copy-start | bytes 24580
  383.6 5.8 %copy-start.17 = (bf16[88,2048]{1,0:T(8,128)(2,1)S(1)}, bf16[88,2048]{1,0:T(8,128)(2,1)}, u32[]{:S(2)}) copy-start(bf16[88,2048]{1,0:T(8,128)(2,1)} %get-tuple-element.105.refs_3_) | copy-start | bytes 1081348
  386.8 8.5 %copy-start.19 = (bf16[64,576]{1,0:T(8,128)(2,1)}, bf16[64,576]{1,0:T(8,128)(2,1)S(1)}, u32[]{:S(2)}) copy-start(bf16[64,576]{1,0:T(8,128)(2,1)S(1)} %pad_maximum_fusion.9.refs_1_) | copy-start | bytes 221188
  386.8 8.5 %slice-start.2 = ((s8[8388608]{0:T(1024)(128)(4,1)}), s8[4194304]{0:T(1024)(128)(4,1)S(1)}, s32[]{:S(2)}) async-start(s8[8388608]{0:T(1024)(128)(4,1)} %bitcast.117), calls=%async_computation.6 | async-start | bytes 8388608
  389.5 5.8 %slice-start.3 = ((s8[8388608]{0:T(1024)(128)(4,1)}), s8[4194304]{0:T(1024)(128)(4,1)S(1)}, s32[]{:S(2)}) async-start(s8[8388608]{0:T(1024)(128)(4,1)} %bitcast.117), calls=%async_computation.7 | async-start | bytes 8388608
  389.5 5.8 %copy-start.52 = (bf16[176,2048]{1,0:T(8,128)(2,1)S(1)}, bf16[176,2048]{1,0:T(8,128)(2,1)}, u32[]{:S(2)}) copy-start(bf16[176,2048]{1,0:T(8,128)(2,1)} %get-tuple-element.103.refs_1_) | copy-start | bytes 2162692
  399.5 107.6 %copy-start.51 = (bf16[8,4,64,256]{3,2,1,0:T(8,128)(2,1)S(1)}, bf16[8,4,64,256]{3,2,1,0:T(8,128)(2,1)}, u32[]{:S(2)}) copy-start(bf16[8,4,64,256]{3,2,1,0:T(8,128)(2,1)} %get-tuple-element.115) | copy-start | bytes 3145732
  501.7 5.4 copy-start.50
  504.2 10.8 %slice-start = ((s8[8388608]{0:T(1024)(128)(4,1)}), s8[4194304]{0:T(1024)(128)(4,1)S(1)}, s32[]{:S(2)}) async-start(s8[8388608]{0:T(1024)(128)(4,1)} %bitcast.87), calls=%async_computation.4 | async-start | bytes 8388608
  507.1 7.8 %slice-start.1 = ((s8[8388608]{0:T(1024)(128)(4,1)}), s8[4194304]{0:T(1024)(128)(4,1)S(1)}, s32[]{:S(2)}) async-start(s8[8388608]{0:T(1024)(128)(4,1)} %bitcast.87), calls=%async_computation.5 | async-start | bytes 8388608
  509.0 3.8 copy-start.20
  509.0 5.0 copy-start.22
  509.0 5.9 %copy-start.53 = (bf16[704,2048]{1,0:T(8,128)(2,1)S(1)}, bf16[704,2048]{1,0:T(8,128)(2,1)}, u32[]{:S(2)}) copy-start(bf16[704,2048]{1,0:T(8,128)(2,1)} %get-tuple-element.104.refs_2_) | copy-start | bytes 8650756
  512.8 10.4 %slice-start.4 = ((s8[8388608]{0:T(1024)(128)(4,1)}), s8[4194304]{0:T(1024)(128)(4,1)S(1)}, s32[]{:S(2)}) async-start(s8[8388608]{0:T(1024)(128)(4,1)} %bitcast.119), calls=%async_computation.8 | async-start | bytes 8388608
  512.9 10.4 %slice-start.6 = ((s8[5767168]{0:T(1024)(128)(4,1)}), s8[4194304]{0:T(1024)(128)(4,1)S(1)}, s32[]{:S(2)}) async-start(s8[5767168]{0:T(1024)(128)(4,1)} %bitcast.121), calls=%async_computation.10 | async-start | bytes 8388608
  515.0 8.2 %slice-start.5 = ((s8[8388608]{0:T(1024)(128)(4,1)}), s8[4194304]{0:T(1024)(128)(4,1)S(1)}, s32[]{:S(2)}) async-start(s8[8388608]{0:T(1024)(128)(4,1)} %bitcast.119), calls=%async_computation.9 | async-start | bytes 8388608
  515.0 8.2 %slice-start.7 = ((s8[5767168]{0:T(1024)(128)(4,1)}), s8[1572864]{0:T(1024)(128)(4,1)S(1)}, s32[]{:S(2)}) async-start(s8[5767168]{0:T(1024)(128)(4,1)} %bitcast.121), calls=%async_computation.11 | async-start | bytes 3145728
  523.2 18.6 %copy-start.27 = (bf16[256,512]{1,0:T(8,128)(2,1)S(1)}, bf16[256,512]{1,0:T(8,128)(2,1)}, u32[]{:S(2)}) copy-start(bf16[256,512]{1,0:T(8,128)(2,1)} %get-tuple-element.171) | copy-start | bytes 786436
  523.3 19.3 %copy-start.1 = (bf16[256,576]{0,1:T(8,128)(2,1)S(1)}, bf16[256,576]{0,1:T(8,128)(2,1)}, u32[]{:S(2)}) copy-start(bf16[256,576]{0,1:T(8,128)(2,1)} %param.22) | copy-start | bytes 884740
  (16 other events, 35.2 us)
Sparse Core Ops, SparseCore 0:
  353.0 62.7 reduce-scatter.2
  419.4 82.1 reduce-scatter.4

commit v3 on v2

--- a/solution.py
+++ b/solution.py
@@ -244,20 +244,20 @@
     def steps(kind, line):
         ranks = (0,) if kind == "narrow" else range(line)
         firsts = (0,) if kind == "narrow" else (0, 1)
-        seconds = (0,) if kind == "wide" else (0, 1)
+        seconds = (0,) if kind in ("wide", "wide2") else (0, 1)
         steps = [(r, a, b) for r in ranks for a in firsts for b in seconds]
         return sorted(steps, key=lambda s: (s[0] + s[1] + 2 * s[2], s[1], s[2]))
 
     @staticmethod
     def sends(kind, rank, a, b):
-        moves = []
-        if not a and not b and kind != "narrow":
-            moves += ["up", "down"]
-        if kind != "narrow" and not a and not b:
+        along = kind != "narrow" and (kind in ("all2", "wide2") or not (a or b))
+        moves = ["up", "down"] if along else []
+        fresh = not rank or kind in ("all", "wide", "narrow")
+        if kind != "narrow" and fresh and not a and not b:
             moves.append("a")
-        if kind != "wide" and not b:
+        if kind not in ("wide", "wide2") and fresh and not b:
             moves.append("b")
-        if kind != "wide":
+        if kind not in ("wide", "wide2"):
             moves.append("core")
         return moves
 
@@ -267,12 +267,12 @@
 
     @staticmethod
     def blocks(kind, line):
-        return {"all": line * 8, "wide": line * 2, "narrow": 4}[kind]
+        return {"all": line * 8, "all2": line * 8, "wide": line * 2, "wide2": line * 2, "narrow": 4}[kind]
 
     def block(self, z, a, b, cf=0):
-        if self.kind == "all":
+        if self.kind in ("all", "all2"):
             return self.spot.index(z, a, b, cf)
-        return self.spot.wide(z, a) if self.kind == "wide" else self.spot.narrow(b, cf)
+        return self.spot.narrow(b, cf) if self.kind == "narrow" else self.spot.wide(z, a)
 
     def target(self, move):
         spot = self.spot
@@ -280,7 +280,7 @@
             return spot.device(spot.z + (1 if move == "up" else -1))
         if move == "core":
             return spot.device(spot.z, 0, 0, 1)
-        if self.kind == "all":
+        if self.kind in ("all", "all2"):
             return spot.routed(spot.z, int(move == "a"), int(move == "b"))
         return spot.device(spot.z, int(move == "a"), int(move == "b"))
 
@@ -296,7 +296,7 @@
         )
 
     def arrive(self, block):
-        self.copy(block, "a" if self.kind == "wide" else "core", 0).wait_recv()
+        self.copy(block, "a" if self.kind in ("wide", "wide2") else "core", 0).wait_recv()
 
     def step(self, rank, a, b):
         spot = self.spot
@@ -329,11 +329,210 @@
                 pl.when(when)(copy.wait_send)
 
 
-def move_kernel(line, items, *refs):
+class NarrowSum:
+    def __init__(self, spot, rows, part, refs):
+        self.spot, self.rows, self.part = spot, rows, part
+        (self.held, self.summed, self.core_buf, self.y_buf, self.load_sem, self.core_send, self.core_recv,
+         self.y_send, self.y_recv) = refs
+
+    @staticmethod
+    def scratch(rows, width, dtype):
+        dma = pltpu.SemaphoreType.DMA
+        return [
+            *(pltpu.VMEM(shape, dtype) for shape in ((2, rows, width), (rows, width), (2, rows, width), (rows, width))),
+            *(dma((2,)) for _ in range(3)),
+            dma,
+            dma,
+        ]
+
+    def block(self, yf, cf):
+        start = pl.multiple_of(self.spot.narrow(yf, cf) * self.rows, self.rows)
+        return self.part.at[pl.ds(start, self.rows), :]
+
+    def to_core(self, yf):
+        return pltpu.make_async_remote_copy(
+            src_ref=self.block(yf, 1), dst_ref=self.core_buf.at[yf], send_sem=self.core_send.at[yf],
+            recv_sem=self.core_recv.at[yf], device_id=self.spot.device(self.spot.z, 0, 0, 1), device_id_type=MESH_IDS,
+        )
+
+    def load(self, yf):
+        return pltpu.make_async_copy(self.block(yf, 0), self.held.at[yf], self.load_sem.at[yf])
+
+    def over_y(self):
+        return pltpu.make_async_remote_copy(
+            src_ref=self.summed, dst_ref=self.y_buf, send_sem=self.y_send, recv_sem=self.y_recv,
+            device_id=self.spot.device(self.spot.z, 0, 1, 0), device_id_type=MESH_IDS,
+        )
+
+    def start(self):
+        for yf in (1, 0):
+            self.to_core(yf).start()
+            self.load(yf).start()
+
+    def joined(self, yf):
+        self.load(yf).wait()
+        self.to_core(yf).wait_recv()
+        return self.held[yf].astype(jnp.float32) + self.core_buf[yf].astype(jnp.float32)
+
+    def send(self):
+        self.summed[...] = self.joined(1).astype(self.summed.dtype)
+        self.over_y().start()
+
+    def total(self):
+        value = self.joined(0)
+        self.over_y().wait_recv()
+        return value + self.y_buf[...].astype(jnp.float32)
+
+    def finish(self):
+        self.over_y().wait_send()
+        for yf in (1, 0):
+            self.to_core(yf).wait_send()
+
+
+def latent_back(value, lat, cos_sin, lat_gain, w_lat, w_rope, tokens, gain, grad_resid):
+    width, lat_width = tokens.shape[1], lat.shape[1]
+    at = width + lat_width
+    grad_x, grad_lat = value[:, :width], value[:, width:at]
+    rope = value[:, at : at + 128] * cos_sin[0] + value[:, at + 128 :] * cos_sin[1]
+    inv = lax.rsqrt(jnp.mean(lat * lat, axis=-1, keepdims=True) + EPS)
+    scaled = grad_lat * lat_gain
+    down = inv * scaled - lat * inv**3 * jnp.mean(lat * scaled, axis=-1, keepdims=True)
+    lat_terms = jnp.sum(grad_lat * lat * inv, axis=0, keepdims=True)
+    lat_low, rope_low = down.astype(LOW), rope.astype(LOW)
+    grad_x += jnp.dot(lat_low, w_lat, preferred_element_type=jnp.float32)
+    grad_x += jnp.dot(rope_low[:, :DR], w_rope, preferred_element_type=jnp.float32)
+    x = tokens.astype(jnp.float32)
+    inv = lax.rsqrt(jnp.mean(x * x, axis=-1, keepdims=True) + EPS)
+    scaled = grad_x * gain
+    back = inv * scaled - x * inv**3 * jnp.mean(x * scaled, axis=-1, keepdims=True)
+    gain_terms = jnp.sum(grad_x * x * inv, axis=0, keepdims=True)
+    return (back + grad_resid).astype(LOW), lat_low, rope_low, gain_terms, lat_terms
+
+
+class WideSum:
+    def __init__(self, spot, take, src, dst, refs):
+        self.spot, self.take, self.src, self.dst = spot, take, src, dst
+        (self.stage, self.x_buf, self.z_buf, self.total, self.x_send, self.x_recv, self.z_send, self.z_recv,
+         self.out_sem) = refs
+
+    @staticmethod
+    def scratch(line, block, dtype):
+        dma = pltpu.SemaphoreType.DMA
+        return [
+            pltpu.VMEM((line, *block), dtype),
+            pltpu.VMEM((line, *block), dtype),
+            pltpu.VMEM((line * 2, *block), dtype),
+            pltpu.VMEM(block, jnp.float32),
+            *(dma((n,)) for n in (line, line, line, line * 2)),
+            dma,
+        ]
+
+    def zed(self, j):
+        rank = self.spot.line - 1 - j
+        return self.spot.z if rank == 0 else self.spot.near(rank)
+
+    def to_x(self, z):
+        return pltpu.make_async_remote_copy(
+            src_ref=self.take(self.src, self.spot.wide(z, 1)), dst_ref=self.x_buf.at[z],
+            send_sem=self.x_send.at[z], recv_sem=self.x_recv.at[z],
+            device_id=self.spot.device(self.spot.z, 1), device_id_type=MESH_IDS,
+        )
+
+    def to_z(self, z, down):
+        return pltpu.make_async_remote_copy(
+            src_ref=self.stage.at[z], dst_ref=self.z_buf.at[down * self.spot.line + z],
+            send_sem=self.z_send.at[z], recv_sem=self.z_recv.at[down * self.spot.line + z],
+            device_id=self.spot.device(self.spot.z + 1 - 2 * down), device_id_type=MESH_IDS,
+        )
+
+    def start(self):
+        for j in range(self.spot.line):
+            self.to_x(self.zed(j)).start()
+
+    def step(self, j):
+        spot = self.spot
+        z = self.zed(j)
+        last = j == spot.line - 1
+        self.to_x(z).wait_recv()
+        value = self.take(self.src, spot.wide(z))[...].astype(jnp.float32) + self.x_buf[z].astype(jnp.float32)
+        if last:
+            self.total[...] = value
+        else:
+            self.stage[z] = value.astype(self.stage.dtype)
+        for down in (0, 1):
+            behind = spot.inside(spot.z - 1 + 2 * down)
+            if last:
+                @pl.when(behind)
+                def _():
+                    self.to_z(z, down).wait_recv()
+                    self.total[...] += self.z_buf[down * spot.line + z].astype(jnp.float32)
+            else:
+                @pl.when((z < spot.z) if down else (z > spot.z))
+                def _():
+                    @pl.when(behind)
+                    def _():
+                        self.to_z(z, down).wait_recv()
+                        more = self.stage[z].astype(jnp.float32) + self.z_buf[down * spot.line + z].astype(jnp.float32)
+                        self.stage[z] = more.astype(self.stage.dtype)
+                    self.to_z(z, down).start()
+        if last:
+            pltpu.make_async_copy(self.total, self.dst, self.out_sem).start()
+
+    def finish(self):
+        spot = self.spot
+        for j in range(spot.line):
+            z = self.zed(j)
+            self.to_x(z).wait_send()
+            if j < spot.line - 1:
+                for down in (0, 1):
+                    @pl.when((z < spot.z) if down else (z > spot.z))
+                    def _():
+                        self.to_z(z, down).wait_send()
+        pltpu.make_async_copy(self.total, self.dst, self.out_sem).wait()
+
+
+def cut_of(ref, axis, start, size):
+    return ref.at[tuple(pl.ds(start, size) if k == axis else slice(None) for k in range(len(ref.shape)))]
+
+
+def routes(item):
+    kind, split = item["kind"], item["split"]
+    if split is None:
+        return [(kind, None)]
+    axis, first = split
+    return [(kind, (axis, 0, first)), (kind + "2", (axis, first, item["array"].shape[axis] - first))]
+
+
+def swap_sends(item, line):
+    return {"wswap": line * 2, "nswap": 4}[item["kind"]]
+
+
+def item_scratch(item, line):
+    dma = pltpu.SemaphoreType.DMA
+    if item["kind"] == "wsum":
+        return WideSum.scratch(line, item["shape"], item["array"].dtype)
+    if item["kind"] in ("wswap", "nswap"):
+        return [dma((swap_sends(item, line),)), dma((swap_sends(item, line),))]
+    return [
+        sem
+        for kind, _ in routes(item)
+        for sem in (dma((Flow.send_count(kind, line),)), dma((Flow.blocks(kind, line),)))
+    ]
+
+
+def move_kernel(line, items, front_count, *refs):
     count = len(items)
-    srcs, dsts = refs[:count], refs[count : 2 * count]
-    sends, recvs, local = refs[2 * count : 3 * count], refs[3 * count : 4 * count], refs[4 * count]
+    given = [i for i, item in enumerate(items) if not item.get("late")]
+    srcs = dict(zip(given, refs))
+    front, refs = refs[len(given) : len(given) + front_count], refs[len(given) + front_count :]
+    dsts, local, rest = refs[:count], refs[count], list(refs[count + 1 :])
+    late = [i for i in range(count) if i not in given]
+    for i in late:
+        srcs[i] = rest.pop(0)
     spot = Spot(line)
+    if front_count:
+        terms, lat, cos_sin, lat_gain, w_lat, w_rope, tokens, gain, grad_resid, ffn_terms = front
+        narrow = NarrowSum(spot, terms.shape[0] // 4, terms, [rest.pop(0) for _ in range(9)])
     kinds = [item["kind"] for item in items]
     flips = set()
     for kind in kinds:
@@ -343,100 +542,133 @@
             "narrow": {(0, 1, 0), (0, 0, 1)},
             "wswap": set(),
             "nswap": {(0, 1, 0), (0, 0, 1), (0, 1, 1)},
+            "wsum": {(1, 0, 0)},
         }[kind]
     wide_count = line * 2
     swaps = any(kind == "wswap" for kind in kinds)
-    enter(spot, any(k in ("all", "wide") for k in kinds), sorted(flips), wide_count if swaps else 0)
+    enter(spot, any(k in ("all", "wide", "wsum") for k in kinds), sorted(flips), wide_count if swaps else 0)
     here_wide, here_narrow = spot.wide(spot.z), spot.narrow()
 
-    flows, copies, own = [], [], []
+    flows, sums, copies, own, own_late, held_back = [], [], [], [], [], []
+    if front_count:
+        narrow.start()
     for i, item in enumerate(items):
-        put = functools.partial(item["put"], dsts[i])
-        if item["kind"] in ("wswap", "nswap"):
+        refs_of = [rest.pop(0) for _ in item_scratch(item, line)]
+        put, take = item["put"], item["take"]
+        if item["kind"] == "wsum":
+            sums.append(WideSum(spot, take, srcs[i], dsts[i], refs_of))
             continue
-        flow = Flow(spot, item["kind"], srcs[i], put, sends[i], recvs[i])
-        flows.append(flow)
-        own.append(pltpu.make_async_copy(srcs[i], put(flow.block(spot.z, 0, 0)), local.at[i]))
+        if item["kind"] not in ("wswap", "nswap"):
+            for n, (kind, cut) in enumerate(routes(item)):
+
+                def place(block, i=i, put=put, cut=cut):
+                    view = put(dsts[i], block)
+                    return view if cut is None else cut_of(view, *cut)
+
+                part = srcs[i] if cut is None else cut_of(srcs[i], *cut)
+                flows.append(Flow(spot, kind, part, place, *refs_of[2 * n : 2 * n + 2]))
+                if i in late:
+                    held_back.append(flows[-1])
+            (own_late if i in late else own).append(
+                pltpu.make_async_copy(srcs[i], put(dsts[i], flows[-1].block(spot.z, 0, 0)), local.at[i])
+            )
+            continue
+        send, recv = refs_of
+        if item["kind"] == "wswap":
+            here = here_wide
+            peers = [lax.rem(here + k, wide_count) for k in range(1, wide_count)]
+            devices = [{"wide": to, "narrow": here_narrow} for to in peers]
+        else:
+            here = here_narrow
+            ways = ((0, 1), (1, 0), (1, 1))
+            peers = [spot.narrow(*way) for way in ways]
+            devices = [spot.device(spot.z, 0, *way) for way in ways]
+        for k, (to, dev) in enumerate(zip(peers, devices)):
+            src = take(srcs[i], to)
+            copies.append(tuple(
+                pltpu.make_async_remote_copy(
+                    src_ref=src, dst_ref=put(dsts[i], at), send_sem=send.at[k], recv_sem=recv.at[at],
+                    device_id=dev, device_id_type=MESH_IDS,
+                )
+                for at in (here, to)
+            ))
+        own.append(pltpu.make_async_copy(take(srcs[i], here), put(dsts[i], here), local.at[i]))
     steps = sorted(
         ((step, flow) for flow in flows for step in Flow.steps(flow.kind, line)),
         key=lambda s: s[0][0] + s[0][1] + 2 * s[0][2],
     )
     for step, flow in steps:
-        if step == (0, 0, 0):
+        if step == (0, 0, 0) and flow not in held_back:
             flow.step(*step)
-    for i, item in enumerate(items):
-        if item["kind"] == "wswap":
-            peers = [(lax.rem(here_wide + k, wide_count), k) for k in range(1, wide_count)]
-            for to, k in peers:
-                copies.append((
-                    pltpu.make_async_remote_copy(
-                        src_ref=item["take"](srcs[i], to), dst_ref=item["put"](dsts[i], here_wide),
-                        send_sem=sends[i].at[k], recv_sem=recvs[i].at[here_wide],
-                        device_id={"wide": to, "narrow": here_narrow}, device_id_type=MESH_IDS,
-                    ),
-                    pltpu.make_async_remote_copy(
-                        src_ref=item["take"](srcs[i], to), dst_ref=item["put"](dsts[i], to),
-                        send_sem=sends[i].at[k], recv_sem=recvs[i].at[to],
-                        device_id={"wide": to, "narrow": here_narrow}, device_id_type=MESH_IDS,
-                    ),
-                ))
-            own.append(pltpu.make_async_copy(
-                item["take"](srcs[i], here_wide), item["put"](dsts[i], here_wide), local.at[i]))
-        elif item["kind"] == "nswap":
-            for k, (yf, cf) in enumerate(((0, 1), (1, 0), (1, 1))):
-                to = spot.narrow(yf, cf)
-                dev = spot.device(spot.z, 0, yf, cf)
-                copies.append((
-                    pltpu.make_async_remote_copy(
-                        src_ref=item["take"](srcs[i], to), dst_ref=item["put"](dsts[i], here_narrow),
-                        send_sem=sends[i].at[k], recv_sem=recvs[i].at[here_narrow],
-                        device_id=dev, device_id_type=MESH_IDS,
-                    ),
-                    pltpu.make_async_remote_copy(
-                        src_ref=item["take"](srcs[i], to), dst_ref=item["put"](dsts[i], to),
-                        send_sem=sends[i].at[k], recv_sem=recvs[i].at[to],
-                        device_id=dev, device_id_type=MESH_IDS,
-                    ),
-                ))
-            own.append(pltpu.make_async_copy(
-                item["take"](srcs[i], here_narrow), item["put"](dsts[i], here_narrow), local.at[i]))
-    for out, _ in copies:
-        out.start()
+    for one in sums:
+        one.start()
     for copy in own:
         copy.start()
+    if front_count:
+        narrow.send()
+        values = latent_back(
+            narrow.total(), lat[...], cos_sin[...], lat_gain[...], w_lat[...], w_rope[...], tokens[...], gain[...],
+            grad_resid[...],
+        )
+        rows_to, lat_to, rope_to, gains_to = (srcs[i] for i in late)
+        rows_to[...], lat_to[...], rope_to[...] = values[:3]
+        width = gain.shape[1]
+        gains_to[:, :width] = values[3]
+        gains_to[:, width : 2 * width] = ffn_terms[...]
+        gains_to[:, 2 * width :] = values[4]
+        for flow in held_back:
+            flow.step(0, 0, 0)
+        for copy in own_late:
+            copy.start()
+    level = 0
     for step, flow in steps:
+        if sum(step) > level:
+            if level == 1:
+                for out, _ in copies:
+                    out.start()
+            if level and level <= line:
+                for one in sums:
+                    one.step(level - 1)
+            level += 1
         if step != (0, 0, 0):
             flow.step(*step)
+    for late in range(max(level, 1), line + 1):
+        for one in sums:
+            one.step(late - 1)
     for flow in flows:
-        if flow.kind != "wide":
+        if flow.kind not in ("wide", "wide2"):
             for rank, a, b in Flow.steps(flow.kind, line):
                 flow.from_core(spot.z if rank == 0 else spot.near(rank), a, b)
     for _, back in copies:
         back.wait_recv()
-    for flow in flows:
+    for flow in (*flows, *sums, *([narrow] if front_count else [])):
         flow.finish()
     for out, _ in copies:
         out.wait_send()
-    for copy in own:
+    for copy in (*own, *own_late):
         copy.wait()
 
 
-def move(line, items, collective_id):
-    counts = {"all": line * 8, "wide": line * 2, "narrow": 4, "wswap": line * 2, "nswap": 4}
-    dma = pltpu.SemaphoreType.DMA
-    kinds = [item["kind"] for item in items]
-    sends = [counts[kind] if kind in ("wswap", "nswap") else Flow.send_count(kind, line) for kind in kinds]
-    moved = sum(item["array"].size * item["array"].dtype.itemsize * counts[item["kind"]] for item in items)
+def move(line, items, collective_id, front=()):
+    moved = sum(item["array"].size * item["array"].dtype.itemsize for item in items) * line * 2
+    given = [i for i, item in enumerate(items) if not item.get("late")]
+    hbm, vmem = pl.BlockSpec(memory_space=pl.ANY), pl.BlockSpec(memory_space=pltpu.VMEM)
     return pl.pallas_call(
-        functools.partial(move_kernel, line, items),
-        out_shape=[jax.ShapeDtypeStruct(item["shape"], item["array"].dtype) for item in items],
-        in_specs=[pl.BlockSpec(memory_space=pltpu.VMEM)] * len(items),
-        out_specs=[pl.BlockSpec(memory_space=pl.ANY)] * len(items),
-        scratch_shapes=[dma((n,)) for n in sends] + [dma((counts[kind],)) for kind in kinds] + [dma((len(items),))],
+        functools.partial(move_kernel, line, items, len(front)),
+        out_shape=[
+            jax.ShapeDtypeStruct(item["shape"], jnp.float32 if item["kind"] == "wsum" else item["array"].dtype)
+            for item in items
+        ],
+        in_specs=[vmem] * len(given) + ([hbm] + [vmem] * (len(front) - 1) if front else []),
+        out_specs=[hbm] * len(items),
+        scratch_shapes=[pltpu.SemaphoreType.DMA((len(items),))]
+        + [pltpu.VMEM(item["array"].shape, item["array"].dtype) for item in items if item.get("late")]
+        + (NarrowSum.scratch(front[0].shape[0] // 4, front[0].shape[1], front[0].dtype) if front else [])
+        + [ref for item in items for ref in item_scratch(item, line)],
         compiler_params=pltpu.CompilerParams(collective_id=collective_id, has_side_effects=True),
         cost_estimate=pl.CostEstimate(flops=0, bytes_accessed=moved, transcendentals=0),
         name="move_blocks",
-    )(*[item["array"] for item in items])
+    )(*[items[i]["array"] for i in given], *front)
 
 
 def narrow_sum_kernel(line, rows, part, out, held, summed, from_core, from_y,
@@ -507,8 +739,9 @@
 def rows_in_kernel(line, sizes, hid_own, grad_own, gates, w_up, s_up, w_down, s_down,
                    hid_all, grad_all, act_e, act_s, dgu_e, dgu_s,
                    land_h, land_g, v_up, v_sup, v_down, v_sdown, t_act, t_sact, t_dgu, t_sdgu,
-                   in_sem, h_send, h_recv, g_send, g_recv, own_sem, keep_sem, out_sem):
-    rows, experts, hid, shared = sizes
+                   in_sem, own_sem, keep_sem, out_sem, *sems):
+    rows, experts, hid, shared, first = sizes
+    h_sems, g_sems = sems[:4], sems[4:]
     group = 4 * rows
     spot = Spot(line)
     loads = [
@@ -519,19 +752,22 @@
         copy.start()
     enter(spot, True, [(0, 0, 1), (0, 1, 0), (1, 0, 0)])
 
-    def place(land, block):
-        return land.at[pl.ds(pl.multiple_of(block * rows, rows), rows), :]
-
+    def place(land, cut, block):
+        return land.at[pl.ds(pl.multiple_of(block * rows, rows), rows), cut]
+
+    width = hid_own.shape[1]
+    cuts = (("all", pl.ds(0, first)), ("all2", pl.ds(first, width - first)))
     flows = [
-        Flow(spot, "all", hid_own, functools.partial(place, land_h), h_send, h_recv),
-        Flow(spot, "all", grad_own, functools.partial(place, land_g), g_send, g_recv),
+        Flow(spot, kind, src.at[:, cut], functools.partial(place, land, cut), send, recv)
+        for src, land, sems in ((hid_own, land_h, h_sems), (grad_own, land_g, g_sems))
+        for (kind, cut), (send, recv) in zip(cuts, (sems[:2], sems[2:]))
     ]
     for flow in flows:
         flow.step(0, 0, 0)
     mine = flows[0].block(spot.z, 0, 0)
     own = [
-        pltpu.make_async_copy(hid_own, place(land_h, mine), own_sem.at[0]),
-        pltpu.make_async_copy(grad_own, place(land_g, mine), own_sem.at[1]),
+        pltpu.make_async_copy(hid_own, place(land_h, slice(None), mine), own_sem.at[0]),
+        pltpu.make_async_copy(grad_own, place(land_g, slice(None), mine), own_sem.at[1]),
     ]
     for copy in own:
         copy.start()
@@ -630,11 +866,12 @@
     dma = pltpu.SemaphoreType.DMA
     hbm = pl.BlockSpec(memory_space=pl.ANY)
     vmem = pl.BlockSpec(memory_space=pltpu.VMEM)
-    sends = Flow.send_count("all", line)
+    first = width * 13 // 16 // 128 * 128
+    flow_sems = [dma((n,)) for kind in ("all", "all2") for n in (Flow.send_count(kind, line), line * 8)]
     out = [(tokens, width), (tokens, width)]
     out += [(f, tokens) for f in (w_down.shape[0], shared, w_up.shape[0], 2 * shared)]
     return pl.pallas_call(
-        functools.partial(rows_in_kernel, line, (rows, experts, hid, shared)),
+        functools.partial(rows_in_kernel, line, (rows, experts, hid, shared, first)),
         out_shape=[jax.ShapeDtypeStruct(shape, LOW) for shape in out],
         in_specs=[vmem, vmem, vmem] + [hbm] * 4,
         out_specs=[hbm] * 6,
@@ -643,13 +880,11 @@
         + [pltpu.VMEM((2, f, group), LOW) for f in (w_down.shape[0], shared, w_up.shape[0], 2 * shared)]
         + [
             dma((4,)),
-            dma((sends,)),
-            dma((line * 8,)),
-            dma((sends,)),
-            dma((line * 8,)),
             dma((2,)),
             dma((2, line * 2)),
             dma((4, 2)),
+            *flow_sems,
+            *flow_sems,
         ],
         compiler_params=pltpu.CompilerParams(
             collective_id=collective_id, has_side_effects=True, vmem_limit_bytes=60 << 20
@@ -810,10 +1045,32 @@
 def rows_out_kernel(line, rows, chunk, count, *refs):
     spot = Spot(line)
     lefts, rights = refs[: 2 * count], refs[2 * count : 4 * count]
-    outs = refs[4 * count : 5 * count]
-    v_lefts, v_rights = refs[5 * count : 7 * count], refs[7 * count : 9 * count]
-    rest = refs[9 * count :]
-    in_sem, lhs_sem = rest[:2]
+    resid, gain, grad_rows = refs[4 * count : 4 * count + 3]
+    refs = refs[4 * count + 3 :]
+    out, grad_resid, grad_gain, grad_all = refs[:4]
+    total, low_rows = refs[4:6]
+    refs = refs[6:]
+    v_lefts, v_rights = refs[: 2 * count], refs[2 * count : 4 * count]
+    rest = refs[4 * count :]
+    in_sem, lhs_sem, send, recv, own_sem = rest[:5]
+    rest = rest[3:]
+    flow = Flow(
+        spot, "narrow", low_rows, lambda block: grad_all.at[pl.ds(pl.multiple_of(block * rows, rows), rows), :], send, recv
+    )
+    own = pltpu.make_async_copy(low_rows, flow.place(spot.narrow()), own_sem)
+
+    def norm_back():
+        h, grad = resid[...], total[...]
+        inv = lax.rsqrt(jnp.mean(h * h, axis=-1, keepdims=True) + EPS)
+        scaled = grad * gain[...]
+        value = grad_rows[...].astype(jnp.float32) + inv * scaled
+        value -= h * inv**3 * jnp.mean(h * scaled, axis=-1, keepdims=True)
+        grad_resid[...] = value
+        low_rows[...] = value.astype(LOW)
+        grad_gain[...] = jnp.sum(grad * h * inv, axis=0, keepdims=True)
+        flow.step(0, 0, 0)
+        own.start()
+
     per = 13
     size = 4 * rows
     right_loads = [pltpu.make_async_copy(rights[k], v_rights[k], in_sem.at[k]) for k in range(2 * count)]
@@ -853,7 +1110,7 @@
                 right_loads[k].wait()
         sums[s].produce(xf, j, chunk)
 
-    first = sums[0]
+    first, later = sums
     for j in range(line):
         produce(0, 1, j)
         if j:
@@ -864,43 +1121,38 @@
             first.early(line - 1)
         else:
             first.middle(j - 1)
-    for s in range(1, count):
-        later = sums[s]
-        produce(s, 1, 0)
-        if s == 1:
+    for j in range(line):
+        produce(1, 1, j)
+        if j == 0:
             first.middle(line - 1)
-        for j in range(1, line):
-            produce(s, 1, j)
+        else:
             later.early(j - 1)
-            if s == 1:
-                first.late(j - 1)
-        produce(s, 0, 0)
-        later.early(line - 1)
-        if s == 1:
+            first.late(j - 1)
+    for j in range(line):
+        produce(1, 0, j)
+        if j == 0:
+            later.early(line - 1)
             first.late(line - 1)
-        for j in range(1, line):
-            produce(s, 0, j)
+        else:
             later.middle(j - 1)
-            if s == 1:
-                first.send_z(j - 1, outs[0])
-        if s == 1:
-            first.send_z(line - 1, outs[0])
-        later.middle(line - 1)
-        for j in range(line):
-            later.late(j)
-        for j in range(line):
-            later.send_z(j, outs[s])
-    if count == 1:
-        first.middle(line - 1)
-        for j in range(line):
-            first.late(j)
-        for j in range(line):
-            first.send_z(j, outs[0])
-    for one in sums:
+    later.middle(line - 1)
+    for j in range(line - 1):
+        first.send_z(j, total)
+        later.late(j)
+    first.send_z(line - 1, total)
+    norm_back()
+    later.late(line - 1)
+    flow.step(0, 0, 1)
+    for j in range(line):
+        later.send_z(j, out)
+    for b in (0, 1):
+        flow.from_core(spot.z, 0, b)
+    for one in (*sums, flow):
         one.finish()
-
-
-def rows_out(line, pairs, collective_id, chunk=512):
+    own.wait()
+
+
+def rows_out(line, pairs, resid, gain, grad_rows, collective_id, chunk=512):
     count = len(pairs)
     lefts = [left for pair in pairs for left, _ in pair]
     rights = [right for pair in pairs for _, right in pair]
@@ -908,7 +1160,9 @@
     rows = tokens // (line * 8)
     dma = pltpu.SemaphoreType.DMA
     slots = line * 4
-    scratch = [pltpu.VMEM(arr.shape, LOW) for arr in lefts + rights] + [dma((2 * count,)), dma((2 * count, line * 2))]
+    scratch = [pltpu.VMEM((rows, width), jnp.float32), pltpu.VMEM((rows, width), LOW)]
+    scratch += [pltpu.VMEM(arr.shape, LOW) for arr in lefts + rights] + [dma((2 * count,)), dma((2 * count, line * 2))]
+    scratch += [dma((Flow.send_count("narrow", line),)), dma((4,)), dma]
     for _ in range(count):
         scratch += [
             pltpu.VMEM((line * 2, 4 * rows, width), LOW),
@@ -927,9 +1181,14 @@
         ]
     return pl.pallas_call(
         functools.partial(rows_out_kernel, line, rows, chunk, count),
-        out_shape=[jax.ShapeDtypeStruct((rows, width), jnp.float32)] * count,
-        in_specs=[pl.BlockSpec(memory_space=pl.ANY)] * (4 * count),
-        out_specs=[pl.BlockSpec(memory_space=pltpu.VMEM)] * count,
+        out_shape=[
+            jax.ShapeDtypeStruct((rows, width), jnp.float32),
+            jax.ShapeDtypeStruct((rows, width), jnp.float32),
+            jax.ShapeDtypeStruct((1, width), jnp.float32),
+            jax.ShapeDtypeStruct((4 * rows, width), LOW),
+        ],
+        in_specs=[pl.BlockSpec(memory_space=pl.ANY)] * (4 * count) + [pl.BlockSpec(memory_space=pltpu.VMEM)] * 3,
+        out_specs=[pl.BlockSpec(memory_space=pltpu.VMEM)] * 3 + [pl.BlockSpec(memory_space=pl.ANY)],
         scratch_shapes=scratch,
         compiler_params=pltpu.CompilerParams(
             collective_id=collective_id, has_side_effects=True, vmem_limit_bytes=63 << 20
@@ -940,7 +1199,7 @@
             transcendentals=0,
         ),
         name="rows_out",
-    )(*lefts, *rights)
+    )(*lefts, *rights, resid, gain, grad_rows)
 
 class Links:
     AXES = {"all": ("wide", "narrow"), "wide": "wide", "narrow": "narrow", "wswap": "wide", "nswap": "narrow"}
@@ -954,8 +1213,10 @@
         self.calls += 1
         return self.calls
 
-    def item(self, array, kind, shape, put, take, plain):
-        return {"array": array, "kind": kind, "shape": shape, "put": put, "take": take, "plain": plain}
+    def item(self, array, kind, shape, put, take, plain, split=None):
+        return {
+            "array": array, "kind": kind, "shape": shape, "put": put, "take": take, "plain": plain, "split": split
+        }
 
     @staticmethod
     def part(axis, size):
@@ -968,11 +1229,20 @@
     def count(self, kind):
         return self.shape["wide"] * self.shape["narrow"] if kind == "all" else self.shape[self.AXES[kind]]
 
-    def gather(self, array, kind, axis):
+    def gather(self, array, kind, axis, split=None):
         shape = list(array.shape)
         shape[axis] *= self.count(kind)
         plain = functools.partial(lax.all_gather, array, self.AXES[kind], axis=axis, tiled=True)
-        return self.item(array, kind, tuple(shape), self.part(axis, array.shape[axis]), None, plain)
+        return self.item(array, kind, tuple(shape), self.part(axis, array.shape[axis]), None, plain, split)
+
+    def wide_sum(self, array, axis):
+        shape = list(array.shape)
+        shape[axis] //= self.shape["wide"]
+
+        def plain():
+            return lax.psum_scatter(array, "wide", scatter_dimension=axis, tiled=True).astype(jnp.float32)
+
+        return self.item(array, "wsum", tuple(shape), None, self.part(axis, shape[axis]), plain)
 
     def swap(self, array, kind, split, concat):
         count = self.count(kind)
@@ -1005,6 +1275,33 @@
         plain = functools.partial(lax.all_gather, array, "narrow", axis=1)
         return self.item(array, "narrow", shape, lambda ref, index: ref.at[:, index], None, plain)
 
+    def move_back(self, items, front):
+        rows, width = front[8].shape
+        lat_width = front[1].shape[1]
+        low, full = functools.partial(jax.ShapeDtypeStruct, dtype=LOW), jax.ShapeDtypeStruct
+        total = self.count("all")
+        if self.line:
+            late = [
+                self.gather(low((rows, width)), "narrow", 0),
+                self.gather(low((rows, lat_width)), "all", 0),
+                self.gather(low((rows, 128)), "all", 0),
+                self.item(
+                    full((1, 2 * width + lat_width), jnp.float32), "all", (total, 1, 2 * width + lat_width),
+                    lambda ref, index: ref.at[index], None, None,
+                ),
+            ]
+            late = [{**item, "late": True} for item in late]
+            return move(self.line, (*items, *late), self.number(), front)
+        summed = lax.psum_scatter(front[0], "narrow", scatter_dimension=0, tiled=True).astype(jnp.float32)
+        tokens, lat, rope, gain_terms, lat_terms = latent_back(summed, *front[1:9])
+        gains = jnp.concatenate([gain_terms, front[9], lat_terms], 1)
+        late = [
+            lax.all_gather(tokens, "narrow", axis=0, tiled=True),
+            *(lax.all_gather(part, self.AXES["all"], axis=0, tiled=True) for part in (lat, rope)),
+            lax.all_gather(gains, self.AXES["all"], axis=0),
+        ]
+        return [item["plain"]() for item in items] + late
+
     def move(self, *items):
         if self.line:
             return move(self.line, items, self.number())
@@ -1035,15 +1332,19 @@
         acts, dgus = (jnp.concatenate(parts) for parts in zip(*pairs))
         return hidden, grad, acts, act_s, dgus, dgu_s
 
-    def rows_out(self, *pairs):
+    def rows_out(self, pairs, resid, gain, grad_rows):
         if self.line:
-            return rows_out(self.line, pairs, self.number())
+            return rows_out(self.line, pairs, resid, gain.reshape(1, -1), grad_rows, self.number())
         sums = []
         for pair in pairs:
             term = sum(dot_tn(left, right) for left, right in pair).astype(LOW)
             term = lax.psum_scatter(term, self.AXES["all"], scatter_dimension=0, tiled=True)
             sums.append(term.astype(jnp.float32))
-        return sums
+        inv = lax.rsqrt(jnp.mean(resid * resid, axis=-1, keepdims=True) + EPS)
+        grad_resid, grad_gain = rms_backward(resid, inv, gain, sums[0])
+        grad_resid = grad_resid + grad_rows.astype(jnp.float32)
+        grad_all = lax.all_gather(grad_resid.astype(LOW), "narrow", axis=0, tiled=True)
+        return sums[1], grad_resid, grad_gain, grad_all
 
 
 def rows_of(array, index, count):
@@ -1097,7 +1398,7 @@
         return rows_of(array, narrow_at, own_rows)
 
     x_float = tokens_in.astype(jnp.float32)
-    x_normed, inv_one = rms_forward(x_float, attn_gain)
+    x_normed, _ = rms_forward(x_float, attn_gain)
     x_low = x_normed.astype(low)
     latent_part = rows_of(w_latent.T, narrow_at, w_latent.shape[1] // narrow_count)
     chosen = routes[:, :, None] == jnp.arange(num_experts, dtype=jnp.int32)
@@ -1105,10 +1406,10 @@
     gate_table = gate_table.reshape(wide_count, local_experts, tok_rows)
     gate_table = jnp.pad(gate_table, ((0, 0), (0, -local_experts % 8), (0, 0))).reshape(-1, tok_rows)
     wq_all, wkva_all, wkvb_all, wo_all, shared_in, shared_out, gates, x_part = links.move(
-        links.gather(w_query, "wide", 0),
+        links.gather(w_query, "wide", 0, (1, 5 * w_query.shape[1] // 6)),
         links.grid(latent_part),
-        links.gather(w_expand, "wide", 0),
-        links.gather(w_output, "wide", 1),
+        links.gather(w_expand, "wide", 0, (1, 7 * w_expand.shape[1] // 8)),
+        links.gather(w_output, "wide", 1, (0, 7 * w_output.shape[0] // 8)),
         links.swap(w_shared_in.transpose(1, 2, 0), "wswap", 1, 2),
         links.swap(w_shared_out, "wswap", 0, 1),
         links.swap(gate_table, "wswap", 0, 1),
@@ -1122,7 +1423,7 @@
     ).astype(low)
     latent_all = dot_nt(x_low, wkva_all)
     latent = latent_all[:, :KVR]
-    latent_normed, inv_lat = rms_forward(latent, latent_gain)
+    latent_normed, _ = rms_forward(latent, latent_gain)
     latent_low = latent_normed.astype(low)
     key_rope = rotate(latent_all[:, KVR:], cos_tab, sin_tab).astype(low)
     expanded = dot_nn(latent_low, wkvb_all).reshape(tok_rows, head_local, 2 * DH).transpose(1, 0, 2)
@@ -1136,9 +1437,8 @@
     mixed = links.narrow_sum(dot_nn(merged, wo_all).astype(low))
 
     x_rows = mine(x_float)
-    inv_one_rows = mine(inv_one)
     resid = x_rows + mixed
-    resid_normed, inv_two = rms_forward(resid, ffn_gain)
+    resid_normed, _ = rms_forward(resid, ffn_gain)
 
     expert_rows = local_experts * hidden_local
     w_up = w_expert_in.transpose(0, 2, 3, 1).reshape(2 * expert_rows, width)
@@ -1147,8 +1447,11 @@
     hidden, grad_all, act_exp, act_sh, grad_gu_exp, grad_gu_sh = links.rows_in(
         resid_normed.astype(low), mine(grad_output), gates, w_up, s_up, w_down, shared_out, local_experts
     )
-    grad_hidden, out_rows = links.rows_out(
-        ((grad_gu_exp, w_up), (grad_gu_sh, s_up)), ((act_exp, w_down), (act_sh, shared_out))
+    out_rows, grad_resid, grad_ffn, grad_low = links.rows_out(
+        (((grad_gu_exp, w_up), (grad_gu_sh, s_up)), ((act_exp, w_down), (act_sh, shared_out))),
+        resid,
+        ffn_gain,
+        mine(grad_output),
     )
     grad_exp_out = dot_nn(act_exp, grad_all).reshape(local_experts, hidden_local, width)
     grad_shout = dot_nn(act_sh, grad_all).astype(low)
@@ -1157,13 +1460,6 @@
     grad_shin = dot_nn(grad_gu_sh, hidden).reshape(2, -1, width).astype(low)
     out_rows = (resid + out_rows).astype(low)
 
-    grad_resid, grad_ffn = rms_backward(resid, inv_two, ffn_gain, grad_hidden)
-    grad_resid = grad_resid + mine(grad_output).astype(jnp.float32)
-    grad_low, x_cols = links.move(
-        links.gather(grad_resid.astype(low), "narrow", 0),
-        links.weave(x_part.reshape(wide_count, own_rows, -1)),
-    )
-    x_cols = x_cols.reshape(wide_count * tok_rows, -1)
     grad_merged = dot_nt(grad_low, wo_all)
     grad_wo = dot_tn(merged, grad_low).astype(low)
     red_wo = lax.psum_scatter(grad_wo, "wide", scatter_dimension=1, tiled=True)
@@ -1179,38 +1475,52 @@
     grad_expanded = jnp.concatenate([grad_k[..., :DH], grad_v], -1).astype(low)
     grad_expanded = grad_expanded.transpose(1, 0, 2).reshape(tok_rows, head_local * 2 * DH)
     grad_wkvb = dot_tn(latent_low, grad_expanded).astype(low)
-    red_wkvb = lax.psum_scatter(grad_wkvb, "wide", scatter_dimension=0, tiled=True)
     grad_latent_part = dot_nt(grad_expanded, wkvb_all)
     grad_x_part = dot_nt(grad_q_pre, wq_all)
-    terms = jnp.concatenate([grad_x_part, grad_latent_part, grad_rope_part], 1)
-    terms = links.narrow_sum(terms.astype(low))
-    grad_x_query, latent_terms = terms[:, :width], terms[:, width:]
-    grad_latent, grad_lat_gain = rms_backward(
-        mine(latent), mine(inv_lat), latent_gain, latent_terms[:, :KVR]
-    )
-    grad_rope = unrotate(latent_terms[:, KVR:], mine(cos_tab), mine(sin_tab))
-    grad_latent_all = jnp.concatenate([grad_latent, grad_rope], -1).astype(low)
-    grad_x_normed = grad_x_query + dot_nn(grad_latent_all, wkva_all)
-    grad_x, grad_att_gain = rms_backward(x_rows, inv_one_rows, attn_gain, grad_x_normed)
-    grad_tokens = (grad_x + grad_resid).astype(low)
-    gains = jnp.concatenate(
-        [part.reshape(wide_count, -1) for part in (grad_att_gain, grad_ffn, grad_lat_gain)], 1
-    )
-    q_pre_all, latent_rows, grad_tokens, layer_out, red_shout, red_shin, gains = links.move(
-        links.gather(grad_q_pre, "wide", 0),
-        links.gather(grad_latent_all, "all", 0),
-        links.gather(grad_tokens, "narrow", 0),
-        links.swap(out_rows, "nswap", 1, 0),
-        links.swap(grad_shout, "wswap", 1, 0),
-        links.swap(grad_shin, "wswap", 2, 1),
-        links.gather(gains, "all", 0),
-    )
-    red_wkva = dot_tn(x_cols, latent_rows)
+    half = DR // 2
+    rope_pad = jnp.zeros((tok_rows, 128 - DR), jnp.float32)
+    changed = (grad_rope_part[:, half:], grad_rope_part[:, :half])
+    terms = jnp.concatenate(
+        [grad_x_part, grad_latent_part, grad_rope_part, rope_pad, *changed, rope_pad], 1
+    ).astype(low)
+    cos_rows, sin_rows = mine(cos_tab), mine(sin_tab)
+    lane_pad = jnp.zeros((own_rows, 128 - DR), jnp.float32)
+    cos_sin = jnp.stack([
+        jnp.concatenate([cos_rows, cos_rows, lane_pad], 1),
+        jnp.concatenate([sin_rows, -sin_rows, lane_pad], 1),
+    ])
+    (q_pre_all, red_wkvb, x_cols, layer_out, red_shout, red_shin, grad_tokens, latent_rows, rope_rows,
+     gains) = links.move_back(
+        (
+            links.gather(grad_q_pre, "wide", 0, (1, 5 * grad_q_pre.shape[1] // 6)),
+            links.wide_sum(grad_wkvb, 0),
+            links.weave(x_part.reshape(wide_count, own_rows, -1)),
+            links.swap(out_rows, "nswap", 1, 0),
+            links.swap(grad_shout, "wswap", 1, 0),
+            links.swap(grad_shin, "wswap", 2, 1),
+        ),
+        (
+            terms,
+            mine(latent),
+            cos_sin,
+            latent_gain.reshape(1, -1),
+            wkva_all[:KVR],
+            wkva_all[KVR:],
+            mine(tokens_in),
+            attn_gain.reshape(1, -1),
+            grad_resid,
+            grad_ffn.reshape(1, -1),
+        ),
+    )
+    x_cols = x_cols.reshape(wide_count * tok_rows, -1)
+    red_wkva = dot_tn(x_cols, jnp.concatenate([latent_rows, rope_rows[:, :DR]], 1))
     red_wq = dot_tn(x_cols, q_pre_all)
-    gains = gains.reshape(-1, wide_count, gains.shape[1])
-    gains = jnp.sum(lax.dynamic_index_in_dim(gains, wide_at, 1, keepdims=False), axis=0)
+    gains = jnp.sum(gains, axis=(0, 1))
     part = width // wide_count
-    red_att_gain, red_ffn, red_lat_gain = gains[:part], gains[part : 2 * part], gains[2 * part :]
+    lat_part = KVR // wide_count
+    red_att_gain = rows_of(gains[:width], wide_at, part)
+    red_ffn = rows_of(gains[width : 2 * width], wide_at, part)
+    red_lat_gain = rows_of(gains[2 * width :], wide_at, lat_part)
     return (
         layer_out,
         grad_tokens.astype(jnp.float32),
@@ -1218,7 +1528,7 @@
         red_wq,
         red_wkva,
         red_lat_gain,
-        red_wkvb.astype(jnp.float32),
+        red_wkvb,
         red_wo.astype(jnp.float32),
         red_ffn,
         red_shin.astype(jnp.float32).transpose(2, 0, 1),

time: 559 us -> 537 us (0.961)
  Pallas kernels: 419 us -> 400 us
  other arithmetic: 35.9 us -> 23.1 us
  local copies, waits for them, and re-layouts: 10.4 us -> 22.1 us
    pallas_call x2 -> x1, Pallas kernels: 23.2 us -> 10.4 us  [narrow_sum(): pl.pallas_call(functools.partial(narrow_sum_kernel, line, rows), out_shap...]
    pallas_call x3 -> x2, Pallas kernels: 219 us -> 212 us  [move(): pl.pallas_call(functools.partial(move_kernel, line, items, len(front)), o...]
    dot_general x8 -> x7, matrix products: 39.9 us -> 41.2 us  [dot_nn(): return jnp.dot(lhs, rhs, preferred_element_type=jnp.float32)]
  transfers between devices with their start and end apart: 2 -> 1, of which waited for: 0 -> 0; matrix products, arithmetic and copies ran while one was open for 13% -> 14% of each run, Pallas kernels for 21% -> 21%
where the time goes in v3:
time: 537 us; the launch traced here: 529 us
  Pallas kernels  400 us (74%)
  matrix products  68.2 us (13%)
  other arithmetic  23.1 us (4%)
  local copies, waits for them, and re-layouts  22.1 us (4%)
  between operations  15.2 us (3%)
    pallas_call x2, Pallas kernels, move(): pl.pallas_call(functools.partial(move_kernel, line, items, len(front)), o...  212 us
    pallas_call x1, Pallas kernels, rows_out(): pl.pallas_call(functools.partial(rows_out_kernel, line, rows, chunk, coun...  101 us
    pallas_call x1, Pallas kernels, rows_in(): pl.pallas_call(functools.partial(rows_in_kernel, line, (rows, experts, hi...  77.2 us
    dot_general x7, matrix products, dot_nn(): return jnp.dot(lhs, rhs, preferred_element_type=jnp.float32)  41.2 us
  transfers between devices with their start and end apart: 1, of which 0 were waited for; matrix products, arithmetic and copies ran while one was open for 14% of the time, Pallas kernels for 21%

profile of v3, /device:TPU:31, one launch (start us, length us, event | category | flops | bytes accessed | tf_op | source)
XLA Modules:
  0.0 528.8 jit_solution(8077467801332947284)
XLA Ops:
  7.3 0.9 slice_compare_fusion
  8.2 1.5 fusion.23
  9.6 1.5 multiply_reduce_fusion
  11.2 2.8 convert_element_type.89
  15.6 0.8 constant_dynamic-slice_fusion.5.refs_7_
  16.7 98.3 %move_blocks.2 = (bf16[2048,768]{1,0:T(8,128)(2,1)}, bf16[576,2048]{1,0:T(8,128)(2,1)}, bf16[512,1024]{1,0:T(8,128)(2,1)}, bf16[512,2048]{1,0:T(8,128)(2,1)}, bf...) custom-call(bf16[256,768]{1,0:T(8,128)(2,1)} %refs_0_.1, ...), custom_call_target="tpu_custom_call" | custom-call | bytes 18153472 | tf_op jit(solution)/shard_map/move_blocks/pallas_call | solution.py:656
  115.0 3.1 fusion.47
  118.1 0.8 fusion.42
  118.9 1.3 convolution_convert_fusion.6
  120.2 1.2 copy.127
  123.7 3.5 fusion.46
  127.6 1.6 fusion.45
  130.5 1.7 convolution_convert_fusion.1.part
  132.2 10.4 %narrow_sum.1 = f32[64,2048]{1,0:T(8,128)} custom-call(bf16[256,2048]{1,0:T(8,128)(2,1)} %convolution_convert_fusion.1.part), custom_call_target="tpu_custom_call" | custom-call | flops 524288 | bytes 2097152 | tf_op jit(solution)/shard_map/narrow_sum/pallas_call | solution.py:715
  142.6 1.4 multiply_reduce_fusion.2
  144.0 2.0 constant_dynamic-slice_fusion
  146.0 0.8 multiply_convert_fusion.1.hid_own
  146.8 77.2 %rows_in.1 = (bf16[2048,2048]{1,0:T(8,128)(2,1)}, bf16[2048,2048]{1,0:T(8,128)(2,1)}, bf16[704,2048]{1,0:T(8,128)(2,1)}, bf16[88,2048]{1,0:T(8,128)(2,1)}, bf16[...) custom-call(bf16[64,2048]{1,0:T(8,128)(2,1)} %multiply_convert_fusion.1.hid_own, ...), custom_call_target="tpu_custom_call" | custom-call | flops 19931332608 | bytes 25165824 | tf_op jit(solution)/shard_map/rows_in/pallas_call | solution.py:873
  224.0 100.9 %rows_out.1 = (f32[64,2048]{1,0:T(8,128)}, f32[64,2048]{1,0:T(8,128)}, f32[1,2048]{1,0:T(1,128)}, bf16[256,2048]{1,0:T(8,128)(2,1)}) custom-call(bf16[1408,2048]{1,0:T(8,128)(2,1)} %get-tuple-element.105.refs_0_, bf16[176,2048]{1,0:T(8,128)(2,1)} %get-tuple-element.106.refs_1_, bf16[704,2048]{1,0:T(8,128)(2,1)} %get-tuple-element.107.refs_2_, ...), custom_call_target="tpu_custom_call" | custom-call | flops 19931332608 | bytes 33554432 | tf_op jit(solution)/shard_map/rows_out/pallas_call | solution.py:1182
  324.9 3.3 convolution_convert_fusion
  328.2 2.8 convolution_convert_fusion.10
  331.2 1.3 fusion.24
  332.5 2.3 fusion.11
  334.8 0.9 copy-done.21
  335.7 1.1 slice.168
  337.2 3.1 fusion.10
  340.3 0.9 copy.118.refs_0_
  341.3 3.1 convolution_convert_fusion.2
  344.4 1.2 slice.167
  345.7 1.6 convolution_convert_fusion.5.refs_1_
  347.7 1.1 slice_reduce_fusion
  348.8 0.8 fusion.41
  349.6 1.5 slice.111.refs_10_
  352.6 2.2 convolution_convert_fusion.4.refs_4_
  354.8 0.9 slice-done.4
  355.8 2.6 convolution_convert_fusion.3
  358.6 1.6 constant_dynamic-slice_fusion.3.refs_7_
  361.0 1.9 concatenate.48.refs_6_
  362.9 113.3 %move_blocks.3 = (bf16[2048,768]{1,0:T(8,128)(2,1)}, f32[64,1024]{1,0:T(8,128)}, bf16[8,4,64,256]{3,2,1,0:T(8,128)(2,1)}, bf16[256,512]{1,0:T(8,128)(2,1)}, bf16...) custom-call(bf16[256,768]{1,0:T(8,128)(2,1)} %copy.118.refs_0_, ...), custom_call_target="tpu_custom_call" | custom-call | bytes 27279360 | tf_op jit(solution)/shard_map/move_blocks/pallas_call | solution.py:656
  476.2 1.5 reduce_sum.81
  477.8 2.9 convert_element_type.107
  481.9 1.2 convert_bitcast_fusion
  483.1 0.9 convert_element_type.110
  484.1 1.9 fusion.48
  486.0 2.0 fusion.1
  488.5 11.0 %fusion.50 = f32[704,2048]{1,0:T(8,128)} fusion(bf16[704,2048]{1,0:T(8,128)(2,1)} %get-tuple-element.107.refs_2_, bf16[2048,2048]{1,0:T(8,128)(2,1)} %get-tuple-element.112), kind=kOutput, calls=%fused_computation.108 | convolution fusion | flops 5905580032 | bytes 17039360 | tf_op jit(solution)/shard_map/dot_general | solution.py:1363
  499.5 18.8 %fusion.49 = f32[1408,2048]{1,0:T(8,128)} fusion(bf16[1408,2048]{1,0:T(8,128)(2,1)} %get-tuple-element.105.refs_0_, bf16[2048,2048]{1,0:T(8,128)(2,1)} %get-tuple-element.113), kind=kOutput, calls=%fused_computation.107 | convolution fusion | flops 11811160064 | bytes 25690112 | tf_op jit(solution)/shard_map/dot_general | solution.py:1363
  518.3 1.8 convert_element_type.109
  (157 shorter events, 12.7 us)
Async XLA Ops:
  7.2 7.5 %copy-start = (bf16[256,576]{0,1:T(8,128)(2,1)S(1)}, bf16[256,576]{0,1:T(8,128)(2,1)}, u32[]{:S(2)}) copy-start(bf16[256,576]{0,1:T(8,128)(2,1)} %param.22) | copy-start | bytes 884740
  7.2 8.1 %copy-start.2 = (bf16[256,2048]{1,0:T(8,128)(2,1)S(1)}, bf16[256,2048]{1,0:T(8,128)(2,1)}, u32[]{:S(2)}) copy-start(bf16[256,2048]{1,0:T(8,128)(2,1)} %param.16) | copy-start | bytes 3145732
  7.2 6.7 %copy-start.41 = (f32[256,6]{0,1:T(8,128)S(1)}, f32[256,6]{0,1:T(8,128)}, u32[]{:S(2)}) copy-start(f32[256,6]{0,1:T(8,128)} %param.19) | copy-start | bytes 18436
  7.2 6.7 %copy-start.42 = (s32[256,6]{0,1:T(8,128)S(1)}, s32[256,6]{0,1:T(8,128)}, u32[]{:S(2)}) copy-start(s32[256,6]{0,1:T(8,128)} %param.18) | copy-start | bytes 18436
  7.2 8.1 %copy-start.35 = (f32[2048]{0:T(1024)S(1)}, f32[2048]{0:T(1024)}, u32[]{:S(2)}) copy-start(f32[2048]{0:T(1024)} %param.20) | copy-start | bytes 24580
  7.2 511.1 %reduce-scatter.2.cloned.1.call-start = ((), (), s32[]{:S(2)}) async-start(), calls=%async_computation.1 | async-start | bytes 2359296 | tf_op jit(solution)/shard_map/reduce_scatter | solution.py:1465
  115.0 4.0 copy-start.7
  115.0 3.9 copy-start.36
  118.9 3.2 copy-start.38
  121.5 5.8 %copy-start.9 = (bf16[256,1024]{0,1:T(8,128)(2,1)}, bf16[256,1024]{0,1:T(8,128)(2,1)S(1)}, u32[]{:S(2)}) copy-start(bf16[256,1024]{0,1:T(8,128)(2,1)S(1)} %copy.127) | copy-start | bytes 1572868
  122.8 4.5 copy-start.18
  122.8 4.6 copy-start.17
  127.4 2.7 copy-start.10
  127.5 3.0 copy-start.29
  127.5 3.0 copy-start.31
  127.5 3.0 copy-start.13
  127.6 4.7 copy-start.26
  130.1 12.5 %copy-start.33 = (f32[4,256]{1,0:T(4,128)}, f32[4,256]{1,0:T(4,128)S(1)}, u32[]{:S(2)}) copy-start(f32[4,256]{1,0:T(4,128)S(1)} %log_add_fusion) | copy-start | bytes 12292
  132.2 13.8 %copy-start.40 = (f32[2048]{0:T(1024)S(1)}, f32[2048]{0:T(1024)}, u32[]{:S(2)}) copy-start(f32[2048]{0:T(1024)} %param.26) | copy-start | bytes 24580
  144.0 80.0 %copy-start.5 = (f32[64,2048]{1,0:T(8,128)}, f32[64,2048]{1,0:T(8,128)S(1)}, u32[]{:S(2)}) copy-start(f32[64,2048]{1,0:T(8,128)S(1)} %get-tuple-element.129.refs_8_) | copy-start | bytes 1572868
  328.2 3.0 copy-start.11
  328.2 4.3 copy-start.4
  328.2 4.3 copy-start.27
  328.2 4.3 copy-start.34
  332.5 4.7 copy-start.25
  332.5 4.7 copy-start.30
  332.5 4.7 copy-start.32
  341.2 4.4 copy-start.37
  341.2 4.4 copy-start.39
  341.2 11.3 %slice-start = ((s8[8388608]{0:T(1024)(128)(4,1)}), s8[4194304]{0:T(1024)(128)(4,1)S(1)}, s32[]{:S(2)}) async-start(s8[8388608]{0:T(1024)(128)(4,1)} %bitcast.83), calls=%async_computation.2 | async-start | bytes 8388608
  344.3 2.9 copy-start.8
  344.3 5.2 copy-start.12
  345.6 6.9 %slice-start.1 = ((s8[8388608]{0:T(1024)(128)(4,1)}), s8[4194304]{0:T(1024)(128)(4,1)S(1)}, s32[]{:S(2)}) async-start(s8[8388608]{0:T(1024)(128)(4,1)} %bitcast.83), calls=%async_computation.3 | async-start | bytes 8388608
  347.7 4.1 copy-start.6
  347.7 4.1 copy-start.19
  349.6 3.0 copy-start.15
  351.8 3.0 slice-start.3
  352.5 3.2 slice-start.4
  352.6 3.3 copy-start.47
  476.2 5.7 %copy-start.16 = (bf16[2,704,256]{2,1,0:T(8,128)(2,1)S(1)}, bf16[2,704,256]{2,1,0:T(8,128)(2,1)}, u32[]{:S(2)}) copy-start(bf16[2,704,256]{2,1,0:T(8,128)(2,1)} %get-tuple-element.124) | copy-start | bytes 2162692
  476.2 6.9 %copy-start.20 = (bf16[704,256]{1,0:T(8,128)(2,1)S(1)}, bf16[704,256]{1,0:T(8,128)(2,1)}, u32[]{:S(2)}) copy-start(bf16[704,256]{1,0:T(8,128)(2,1)} %get-tuple-element.125) | copy-start | bytes 1081348
  477.7 6.3 %copy-start.28 = (f32[4608]{0:T(1024)}, f32[4608]{0:T(1024)S(1)}, u32[]{:S(2)}) copy-start(f32[4608]{0:T(1024)S(1)} %reduce_sum.81) | copy-start | bytes 55300
  477.8 6.3 %copy-start.45 = (bf16[8,4,64,256]{3,2,1,0:T(8,128)(2,1)S(1)}, bf16[8,4,64,256]{3,2,1,0:T(8,128)(2,1)}, u32[]{:S(2)}) copy-start(bf16[8,4,64,256]{3,2,1,0:T(8,128)(2,1)} %get-tuple-element.119) | copy-start | bytes 3145732
  480.7 3.4 copy-start.43
  486.0 2.0 slice-start.2
  499.5 20.6 %copy-start.23 = (bf16[256,512]{1,0:T(8,128)(2,1)S(1)}, bf16[256,512]{1,0:T(8,128)(2,1)}, u32[]{:S(2)}) copy-start(bf16[256,512]{1,0:T(8,128)(2,1)} %get-tuple-element.166) | copy-start | bytes 786436
  499.5 21.3 %copy-start.22 = (f32[64,1024]{1,0:T(8,128)S(1)}, f32[64,1024]{1,0:T(8,128)}, u32[]{:S(2)}) copy-start(f32[64,1024]{1,0:T(8,128)} %get-tuple-element.172) | copy-start | bytes 786436
  499.5 22.0 %copy-start.1 = (bf16[256,576]{0,1:T(8,128)(2,1)S(1)}, bf16[256,576]{0,1:T(8,128)(2,1)}, u32[]{:S(2)}) copy-start(bf16[256,576]{0,1:T(8,128)(2,1)} %param.22) | copy-start | bytes 884740
  (6 other events, 8.6 us)
Sparse Core Ops, SparseCore 0:
  328.3 83.9 reduce-scatter.1
